TPU v7x, 32 devices: a whole 2x2x4 slice. The times are simulated.
32 devices in a mesh: cuts: 8 (over y, x, core), tr: 4 (over z).
Axes of the slice: x: 2, y: 2, z: 4, core: 2. Of those that a mesh axis runs over, the one named last changes fastest.
Arguments:
- cells: int32 [2, 8, 2, 1024], P(None, 'cuts'), may hold values from 1 to 509
- offsets: float32 [2, 8, 2, 1024], P(None, 'cuts'), may hold values from 0 to 1
- charges: float32 [2, 8, 1024], P(None, 'cuts'), may hold values from 0.5 to 2
- momenta: float32 [2, 8, 2, 1024], P(None, 'cuts', None, 'tr'), may hold values from -6 to 6
- green: float32 [1024, 1024], replicated, may hold values from -0.1875 to 0.1875
Outputs:
- momenta_out: float32 [2, 8, 2, 1024], P(None, 'cuts', None, 'tr')
Inputs may be any that keep to these rules, and one draw needn't show every extreme that they name: `cells`: every cell index lies in 1 .. 509.
All inputs are finite; a program needn't handle non-finite values.
Results may differ from a plain program's by a relative error of at most 0.017.
Values may be sent and summed in bfloat16 or wider, within the bound.
No kernel may reach another device: no remote copies, remote signals or barrier semaphores. Data moves between devices by JAX's collectives and lax.ppermute only.
A program may use at most 64 MiB of HBM per device.

v0:
```python
import math

import jax
import jax.numpy as jnp
from jax import lax
from jax.sharding import PartitionSpec as P

SECTIONS = 4


drift_step = 0.5


def padded(cells, sides, width):
    for axis, dim in sides:
        count = lax.axis_size(axis)
        ends = count - 1
        head = lax.slice_in_dim(cells, 0, width, axis=dim)
        tail = lax.slice_in_dim(cells, cells.shape[dim] - width, cells.shape[dim], axis=dim)
        cells = jnp.concatenate(
            [
                lax.ppermute(tail, axis, [(i, (i + 1) % count) for i in range(ends)]),
                cells,
                lax.ppermute(head, axis, [((i + 1) % count, i) for i in range(ends)]),
            ],
            axis=dim,
        )
    return cells


def shifted(value, axis, steps):
    count = lax.axis_size(axis)
    pairs = [(source, (source + steps) % count) for source in range(count)]
    return lax.ppermute(value, axis, pairs)


def phase_angles(frequency, position, period):
    return 2.0 * math.pi / period * (frequency * position % period).astype(jnp.float32)


def column_table(inputs, with_imag, begin_col, col_count, piece_width, period):
    columns = begin_col + lax.iota(jnp.int32, col_count)
    halves = columns // piece_width % 2
    frequency = columns // (2 * piece_width) * piece_width + columns % piece_width
    position = lax.iota(jnp.int32, inputs)[:, None]
    theta = phase_angles(frequency[None, :], position, period)
    cosine = jnp.cos(theta)
    sine = jnp.sin(theta)
    table = jnp.where(halves[None, :] == 0, cosine, -sine)
    if with_imag:
        lower = jnp.where(halves[None, :] == 0, sine, cosine)
        table = jnp.concatenate([table, lower], axis=0)
    return table.astype(jnp.bfloat16)


def row_table(inputs, period):
    theta = phase_angles(
        lax.iota(jnp.int32, period)[:, None], lax.iota(jnp.int32, inputs)[None, :], period
    )
    return jnp.concatenate([jnp.cos(theta), jnp.sin(theta)], axis=0).astype(jnp.bfloat16)


def forward_rows(table, spectrum, piece_width):
    both_parts = jnp.dot(table, spectrum, preferred_element_type=jnp.float32)
    period = table.shape[0] // 2
    cosine_part = both_parts[:period]
    sine_part = both_parts[period:]
    real_part = cosine_part[:, :piece_width] + sine_part[:, piece_width:]
    imag_part = cosine_part[:, piece_width:] - sine_part[:, :piece_width]
    return (real_part, imag_part)


def hat_weights(cells_along, fraction, first_node, node_count):
    nodes = first_node + lax.iota(jnp.int32, node_count)[None, :]
    lower = jnp.where(cells_along[:, None] == nodes, 1.0 - fraction[:, None], 0.0)
    upper = jnp.where(cells_along[:, None] + 1 == nodes, fraction[:, None], 0.0)
    return lower + upper


def deposit(cells, offsets, charges, first_node, node_rows, node_cols):
    particles = cells.shape[1]
    block_size = math.gcd(particles, 512)
    grid_sum = jnp.zeros((node_rows, node_cols), jnp.float32)
    for number in range(particles // block_size):
        begin_at = number * block_size
        finish_at = begin_at + block_size
        weight_rows = hat_weights(
            cells[0, begin_at:finish_at], offsets[0, begin_at:finish_at], first_node, node_rows
        )
        weight_cols = hat_weights(
            cells[1, begin_at:finish_at], offsets[1, begin_at:finish_at], 0, node_cols
        )
        weight_cols = charges[begin_at:finish_at][:, None] * weight_cols
        grid_sum = grid_sum + lax.dot_general(
            weight_rows.astype(jnp.bfloat16),
            weight_cols.astype(jnp.bfloat16),
            (((0,), (0,)), ((), ())),
            preferred_element_type=jnp.float32,
        )
    return grid_sum.astype(jnp.bfloat16)


def drift(cells, offsets, moment, extent):
    place = cells.astype(jnp.float32) + offsets + drift_step * moment
    place = jnp.clip(place, 1.0, extent - 2.0 - 1.0 / 64.0)
    whole = jnp.floor(place)
    return (whole.astype(jnp.int32), place - whole)


def potentials(pair_grid, pair_columns, pair_rows, kernel_re, kernel_im, piece_width):
    spectrum = jnp.dot(pair_grid, pair_columns, preferred_element_type=jnp.float32).astype(
        jnp.bfloat16
    )
    spectrum = lax.all_to_all(spectrum, "tr", split_axis=1, concat_axis=0, tiled=True)
    forward_re, forward_im = forward_rows(pair_rows, spectrum, piece_width)
    scaled = jnp.concatenate(
        [
            forward_re * kernel_re - forward_im * kernel_im,
            forward_re * kernel_im + forward_im * kernel_re,
        ],
        axis=1,
    ).astype(jnp.bfloat16)
    period = pair_rows.shape[0] // 2
    extent = pair_rows.shape[1]
    halves = lax.dot_general(
        pair_rows.reshape(2, period, extent),
        scaled,
        (((1,), (0,)), ((), ())),
        preferred_element_type=jnp.float32,
    )
    cosine_part = halves[0]
    sine_part = halves[1]
    inverse = jnp.concatenate(
        [
            cosine_part[:, :piece_width] - sine_part[:, piece_width:],
            cosine_part[:, piece_width:] + sine_part[:, :piece_width],
        ],
        axis=1,
    ).astype(jnp.bfloat16)
    inverse = lax.all_to_all(inverse, "tr", split_axis=0, concat_axis=1, tiled=True)
    potential = lax.dot_general(
        inverse, pair_columns, (((1,), (1,)), ((), ())), preferred_element_type=jnp.float32
    ) * (1.0 / (period * period))
    return potential.reshape(potential.shape[0], 2, extent)


def field_grids(potential):
    widened = padded(potential.astype(jnp.bfloat16), (("tr", 0),), 1).astype(potential.dtype)
    along_rows = (widened[:-2] - widened[2:]) * 0.5
    sideways = jnp.pad(potential, ((0, 0), (0, 0), (1, 1)))
    along_cols = (sideways[:, :, :-2] - sideways[:, :, 2:]) * 0.5
    stacked = jnp.stack([along_rows, along_cols], axis=0)
    node_rows = potential.shape[0]
    return (
        jnp.transpose(stacked, (2, 0, 1, 3))
        .reshape(2, 2 * node_rows, potential.shape[2])
        .astype(jnp.bfloat16)
    )


def kick_terms(cells, offsets, fields, first_node, node_rows, row_count):
    node_cols = fields.shape[2]
    block_size = math.gcd(row_count, 256)

    def one_block(number):
        begin_at = number * block_size
        columns = []
        for beam_index in range(2):
            row_cells = lax.dynamic_slice_in_dim(cells[beam_index, 0], begin_at, block_size)
            col_cells = lax.dynamic_slice_in_dim(cells[beam_index, 1], begin_at, block_size)
            row_frac = lax.dynamic_slice_in_dim(offsets[beam_index, 0], begin_at, block_size)
            col_frac = lax.dynamic_slice_in_dim(offsets[beam_index, 1], begin_at, block_size)
            weight_rows = hat_weights(row_cells, row_frac, first_node, node_rows).astype(
                jnp.bfloat16
            )
            weight_cols = hat_weights(col_cells, col_frac, 0, node_cols).astype(jnp.bfloat16)
            projected = lax.dot_general(
                weight_cols,
                fields[1 - beam_index],
                (((1,), (1,)), ((), ())),
                preferred_element_type=jnp.float32,
            )
            projected = projected.reshape(block_size, 2, node_rows)
            columns.append(jnp.sum(projected * weight_rows.astype(jnp.float32)[:, None, :], axis=2))
        return jnp.concatenate(columns, axis=1)

    blocks = lax.map(one_block, jnp.arange(row_count // block_size, dtype=jnp.int32))
    return blocks.reshape(row_count, 4)


def per_device(cells, offsets, charges, momenta, green):
    shards = lax.axis_size("tr")
    shard_index = lax.axis_index("tr")
    period = green.shape[0]
    extent = period // 2
    node_rows = extent // shards
    piece_width = period // shards
    first_node = shard_index * node_rows
    kernel_columns = column_table(
        period, False, shard_index * 2 * piece_width, 2 * piece_width, piece_width, period
    )
    kernel_cols = jnp.dot(
        green.astype(jnp.bfloat16), kernel_columns, preferred_element_type=jnp.float32
    ).astype(jnp.bfloat16)
    kernel_re, kernel_im = forward_rows(row_table(period, period), kernel_cols, piece_width)
    pair_columns = column_table(extent, True, 0, 2 * period, piece_width, period)
    pair_rows = row_table(extent, period)
    local_cells = cells[:, 0]
    local_offsets = offsets[:, 0]
    local_charges = charges[:, 0]
    moment = momenta
    particle_rows = momenta.shape[-1]
    for section_index in range(SECTIONS):
        charge_grids = [
            deposit(
                local_cells[beam_index],
                local_offsets[beam_index],
                local_charges[beam_index],
                first_node,
                node_rows,
                extent,
            )
            for beam_index in range(2)
        ]
        if section_index > 0:
            charge_grids = [
                shifted(charge_grids[0], "cuts", 2 * section_index),
                shifted(charge_grids[1], "cuts", -2 * section_index),
            ]
        pair_grid = jnp.concatenate(charge_grids, axis=1)
        potential = potentials(
            pair_grid, pair_columns, pair_rows, kernel_re, kernel_im, piece_width
        )
        fields = field_grids(potential)
        kick_sums = lax.psum_scatter(
            kick_terms(
                local_cells,
                local_offsets,
                fields,
                first_node,
                node_rows,
                particle_rows * lax.axis_size("tr"),
            ),
            "tr",
            scatter_dimension=0,
            tiled=True,
        )
        moment = moment + jnp.transpose(kick_sums).reshape(moment.shape)
        if section_index + 1 < SECTIONS:
            whole_moment = lax.all_gather(moment, "tr", axis=3, tiled=True)
            local_cells, local_offsets = drift(
                local_cells, local_offsets, whole_moment[:, 0], extent
            )
    return moment


def solution(mesh):
    return jax.shard_map(
        per_device,
        mesh=mesh,
        in_specs=(
            P(None, "cuts", None, None),
            P(None, "cuts", None, None),
            P(None, "cuts", None),
            P(None, "cuts", None, "tr"),
            P(),
        ),
        out_specs=P(None, "cuts", None, "tr"),
        check_vma=False,
    )
```

profile of v0, /device:TPU:0, one launch (start us, length us, event | category | flops | bytes accessed | tf_op | source)
XLA Modules:
  0.0 464.8 jit_solution(5562730413649528818)
XLA Ops:
  8.9 17.6 %select_convert_fusion.1 = (bf16[512,2048]{1,0:T(8,128)(2,1)S(1)}, bf16[512,2048]{1,0:T(8,128)(2,1)S(1)}) fusion(s32[2048]{0:T(1024)S(1)} %fusion.410, pred[2048]{0:T(1024)(128)(4,1)S(1)} %fusion.407), kind=kLoop, calls=%fused_computation.211 | loop fusion | flops 19922944 | bytes 4204544 | tf_op jit(solution)/shard_map/convert.42
  31.8 6.3 %all-to-all-start = ((bf16[128,4,512]{2,0,1:T(8,128)(2,1)}), bf16[128,4,512]{2,0,1:T(8,128)(2,1)S(1)}, u32[]{:S(2)}, u32[]{:S(2)}) async-start(bf16[128,4,512]{2,0,1:T(8,128)(2,1)} %bitcast.355), calls=%async_computation | async-start | bytes 1048576 | tf_op jit(solution)/shard_map/all_to_all | solution.py:114
  38.5 16.9 %sine_convert_fusion = (bf16[1024,1024]{1,0:T(8,128)(2,1)S(1)}, bf16[1024,1024]{1,0:T(8,128)(2,1)S(1)}) fusion(), kind=kLoop, calls=%fused_computation.206 | loop fusion | flops 16777216 | bytes 4194304 | tf_op jit(solution)/shard_map/convert.41
  55.4 9.6 %fusion.116.clone.5 = bf16[512,1024]{1,0:T(8,128)(2,1)S(1)} fusion(f32[1024,1024]{1,0:T(8,128)S(1)} %copy-done.28, s32[512]{0:T(512)S(1)} %fusion.417, pred[512]{0:T(512)(128)(4,1)S(1)} %fusion.414), kind=kOutput, calls=%fused_computation.243.clone.clone.clone.2 | convolution fusion | flops 1084227584 | bytes 5245440 | tf_op jit(solution)/shard_map/dot_general | solution.py:202
  65.0 8.7 %fusion.144 = (bf16[1024,512]{1,0:T(8,128)(2,1)S(1)}, bf16[1024,512]{1,0:T(8,128)(2,1)S(1)}) fusion(), kind=kLoop, calls=%fused_computation.359 | loop fusion | flops 8388608 | bytes 2097152 | tf_op jit(solution)/shard_map/sin | solution.py:60
  75.3 4.4 fusion.90
  86.6 19.0 %all_to_all.140 = bf16[4,128,512]{1,2,0:T(8,128)(2,1)S(1)} all-to-all(bf16[4,128,512]{1,2,0:T(8,128)(2,1)S(1)} %pad_maximum_fusion.1), channel_id=1, replica_groups=mesh['cuts'=8,'tr'=4] {'tr'}, dimensions={0} | all-to-all | bytes 1048576 | tf_op jit(solution)/shard_map/all_to_all | solution.py:140
  105.6 3.1 convolution_multiply_fusion.11
  113.9 4.1 collective-permute-done.1
  119.5 11.0 %while.40 = (s32[]{:T(128)}, f32[4,256,4]{1,2,0:T(4,128)S(1)}, s32[2,2,1024]{2,1,0:T(2,128)S(1)}, s32[4]{0:T(128)S(1)}, f32[2,2,1024]{2,1,0:T(2,128)S(1)}, /*ind...) while((s32[]{:T(128)}, f32[4,256,4]{1,2,0:T(4,128)S(1)}, ...), condition=%wide.region_3.4_spmd, body=%wide.region_0.3_spmd.sunk | while | flops 136513664 | bytes 2225343 | solution.py:187
  131.6 21.3 %reduce-scatter.13.cloned.1.call-done = f32[256,4]{1,0:T(8,128)} async-done(((f32[1024,4]{1,0:T(8,128)}), f32[256,4]{1,0:T(8,128)}) %reduce-scatter.13.cloned.1.call-update) | async-done | bytes 4112
  154.0 11.9 %all_gather.9 = f32[2,1,2,1024]{3,2,0,1:T(2,128)S(1)} all-gather(f32[2,1,2,256]{3,2,0,1:T(2,128)S(1)} %bitcast_add_fusion.5), channel_id=1, replica_groups=mesh['cuts'=8,'tr'=4] {'tr'}, dimensions={3}, use_global_device_ids=true | all-gather | bytes 20480 | tf_op jit(solution)/shard_map/all_gather | solution.py:250
  177.2 12.8 %all_to_all.141 = bf16[128,4,512]{2,0,1:T(8,128)(2,1)S(1)} all-to-all(bf16[128,4,512]{2,0,1:T(8,128)(2,1)S(1)} %bitcast.500), channel_id=1, replica_groups=mesh['cuts'=8,'tr'=4] {'tr'}, dimensions={1} | all-to-all | bytes 1048576 | tf_op jit(solution)/shard_map/all_to_all | solution.py:114
  195.0 13.0 %all_to_all.142 = bf16[4,128,512]{1,2,0:T(8,128)(2,1)S(1)} all-to-all(bf16[4,128,512]{1,2,0:T(8,128)(2,1)S(1)} %pad_maximum_fusion.2), channel_id=1, replica_groups=mesh['cuts'=8,'tr'=4] {'tr'}, dimensions={0} | all-to-all | bytes 1048576 | tf_op jit(solution)/shard_map/all_to_all | solution.py:140
  216.3 4.2 collective-permute-done.5
  221.9 10.5 %while.41 = (s32[]{:T(128)}, f32[4,256,4]{1,2,0:T(4,128)S(1)}, s32[2,2,1024]{2,1,0:T(2,128)S(1)}, s32[4]{0:T(128)S(1)}, f32[2,2,1024]{2,1,0:T(2,128)S(1)}, /*ind...) while((s32[]{:T(128)}, f32[4,256,4]{1,2,0:T(4,128)S(1)}, ...), condition=%wide.region_8.9_spmd, body=%wide.region_5.8_spmd.sunk | while | flops 136513664 | bytes 2225343 | solution.py:187
  233.5 21.2 %reduce-scatter.15.cloned.1.call-done = f32[256,4]{1,0:T(8,128)} async-done(((f32[1024,4]{1,0:T(8,128)}), f32[256,4]{1,0:T(8,128)}) %reduce-scatter.15.cloned.1.call-update) | async-done | bytes 4112
  255.7 11.9 %all_gather.10 = f32[2,1,2,1024]{3,2,0,1:T(2,128)S(1)} all-gather(f32[2,1,2,256]{3,2,0,1:T(2,128)S(1)} %add.991), channel_id=1, replica_groups=mesh['cuts'=8,'tr'=4] {'tr'}, dimensions={3}, use_global_device_ids=true | all-gather | bytes 20480 | tf_op jit(solution)/shard_map/all_gather | solution.py:250
  274.6 3.4 collective-permute-done.7
  278.9 13.0 %all_to_all.143 = bf16[128,4,512]{2,0,1:T(8,128)(2,1)S(1)} all-to-all(bf16[128,4,512]{2,0,1:T(8,128)(2,1)S(1)} %bitcast.501), channel_id=1, replica_groups=mesh['cuts'=8,'tr'=4] {'tr'}, dimensions={1} | all-to-all | bytes 1048576 | tf_op jit(solution)/shard_map/all_to_all | solution.py:114
  297.0 12.8 %all_to_all.144 = bf16[4,128,512]{1,2,0:T(8,128)(2,1)S(1)} all-to-all(bf16[4,128,512]{1,2,0:T(8,128)(2,1)S(1)} %pad_maximum_fusion.3), channel_id=1, replica_groups=mesh['cuts'=8,'tr'=4] {'tr'}, dimensions={0} | all-to-all | bytes 1048576 | tf_op jit(solution)/shard_map/all_to_all | solution.py:140
  318.1 4.2 collective-permute-done.9
  323.7 10.5 %while.42 = (s32[]{:T(128)}, f32[4,256,4]{1,2,0:T(4,128)S(1)}, s32[2,2,1024]{2,1,0:T(2,128)S(1)}, s32[4]{0:T(128)S(1)}, f32[2,2,1024]{2,1,0:T(2,128)S(1)}, /*ind...) while((s32[]{:T(128)}, f32[4,256,4]{1,2,0:T(4,128)S(1)}, ...), condition=%wide.region_13.14_spmd, body=%wide.region_10.13_spmd.sunk | while | flops 136513664 | bytes 2225343 | solution.py:187
  335.3 20.2 %reduce-scatter.17.cloned.1.call-done = f32[256,4]{1,0:T(8,128)} async-done(((f32[1024,4]{1,0:T(8,128)}), f32[256,4]{1,0:T(8,128)}) %reduce-scatter.17.cloned.1.call-update) | async-done | bytes 4112
  356.6 11.9 %all_gather.11 = f32[2,1,2,1024]{3,2,1,0:T(2,128)S(1)} all-gather(f32[2,1,2,256]{3,2,1,0:T(2,128)S(1)} %bitcast_add_fusion.4), channel_id=1, replica_groups=mesh['cuts'=8,'tr'=4] {'tr'}, dimensions={3}, use_global_device_ids=true | all-gather | bytes 20480 | tf_op jit(solution)/shard_map/all_gather | solution.py:250
  375.9 5.1 %collective-permute-done.11 = bf16[128,512]{1,0:T(8,128)(2,1)S(1)} collective-permute-done((bf16[128,512]{1,0:T(8,128)(2,1)S(1)}, bf16[128,512]{1,0:T(8,128)(2,1)S(1)}, u32[]{:S(2)}, u32[]{:S(2)}) %collective-permute-start.11) | collective-permute-done | bytes 131104 | tf_op jit(solution)/shard_map/ppermute | solution.py:34
  381.8 12.8 %all_to_all.145 = bf16[128,4,512]{2,0,1:T(8,128)(2,1)S(1)} all-to-all(bf16[128,4,512]{2,0,1:T(8,128)(2,1)S(1)} %bitcast.502), channel_id=1, replica_groups=mesh['cuts'=8,'tr'=4] {'tr'}, dimensions={1} | all-to-all | bytes 1048576 | tf_op jit(solution)/shard_map/all_to_all | solution.py:114
  399.6 12.8 %all_to_all.146 = bf16[4,128,512]{1,2,0:T(8,128)(2,1)S(1)} all-to-all(bf16[4,128,512]{1,2,0:T(8,128)(2,1)S(1)} %pad_maximum_fusion.4), channel_id=1, replica_groups=mesh['cuts'=8,'tr'=4] {'tr'}, dimensions={0} | all-to-all | bytes 1048576 | tf_op jit(solution)/shard_map/all_to_all | solution.py:140
  412.4 3.1 convolution_multiply_fusion.8
  420.7 4.2 collective-permute-done.13
  426.3 9.5 %while.43 = (s32[]{:T(128)}, f32[4,256,4]{1,2,0:T(4,128)S(1)}, s32[2,2,1024]{2,1,0:T(2,128)S(1)}, s32[4]{0:T(128)S(1)}, f32[2,2,1024]{2,1,0:T(2,128)S(1)}, /*ind...) while((s32[]{:T(128)}, f32[4,256,4]{1,2,0:T(4,128)S(1)}, ...), condition=%wide.region_18.19_spmd, body=%wide.region_15.18_spmd.sunk | while | flops 136513664 | bytes 2225343 | solution.py:187
  436.9 19.4 %reduce-scatter.19.cloned.1.call-done = f32[256,4]{1,0:T(8,128)} async-done(((f32[1024,4]{1,0:T(8,128)}), f32[256,4]{1,0:T(8,128)}) %reduce-scatter.19.cloned.1.call-update) | async-done | bytes 4112
  (635 shorter events, 127.0 us)
Async XLA Ops:
  31.8 47.8 %all-to-all-start = ((bf16[128,4,512]{2,0,1:T(8,128)(2,1)}), bf16[128,4,512]{2,0,1:T(8,128)(2,1)S(1)}, u32[]{:S(2)}, u32[]{:S(2)}) async-start(bf16[128,4,512]{2,0,1:T(8,128)(2,1)} %bitcast.355), calls=%async_computation | async-start | bytes 1048576 | tf_op jit(solution)/shard_map/all_to_all | solution.py:114
  38.2 114.7 %reduce-scatter.13.cloned.1.call-start = ((), (), s32[]{:S(2)}) async-start(), calls=%async_computation.12 | async-start | bytes 655360
  38.4 16.9 %copy-start.28 = (f32[1024,1024]{1,0:T(8,128)S(1)}, f32[1024,1024]{1,0:T(8,128)}, u32[]{:S(2)}) copy-start(f32[1024,1024]{1,0:T(8,128)} %param.17) | copy-start | bytes 12582916
  86.5 19.0 %copy-start.14 = (bf16[512,2048]{1,0:T(8,128)(2,1)S(1)}, bf16[512,2048]{1,0:T(8,128)(2,1)}, u32[]{:S(2)}) copy-start(bf16[512,2048]{1,0:T(8,128)(2,1)} %copy-done.13) | copy-start | bytes 6291460
  110.4 3.5 collective-permute-start
  112.5 5.5 %collective-permute-start.1 = (bf16[1,2,512]{2,1,0:T(2,128)(2,1)S(1)}, bf16[1,2,512]{2,1,0:T(2,128)(2,1)S(1)}, u32[]{:S(2)}, u32[]{:S(2)}) collective-permute-start(bf16[1,2,512]{2,1,0:T(2,128)(2,1)S(1)} %get-tuple-element.339), channel_id=1, source_target_pairs={{1,0},{2,1},{3,2},{5,4},{6,5},{7,6},{9,8},{10,9},{11,10},{13,12},{... | collective-permute-start | bytes 6152 | tf_op jit(solution)/shard_map/ppermute | solution.py:24
  119.5 34.5 %copy-start.27 = (f32[2,1,2,256]{3,2,1,0:T(2,128)S(1)}, f32[2,1,2,256]{3,2,1,0:T(2,128)}, u32[]{:S(2)}) copy-start(f32[2,1,2,256]{3,2,1,0:T(2,128)} %param.16) | copy-start | bytes 12292
  131.5 123.1 %reduce-scatter.15.cloned.1.call-start = ((), (), s32[]{:S(2)}) async-start(), calls=%async_computation.13 | async-start | bytes 655360
  167.8 5.9 %collective-permute-start.2 = (bf16[128,512]{1,0:T(8,128)(2,1)S(1)}, bf16[128,512]{1,0:T(8,128)(2,1)S(1)}, u32[]{:S(2)}, u32[]{:S(2)}) collective-permute-start(bf16[128,512]{1,0:T(8,128)(2,1)S(1)} %fusion.121), channel_id=1, source_target_pairs={{0,8},{4,12},{8,16},{12,20},{16,24},{20,28},{24,0},{28,4},{1,9},{5... | collective-permute-start | bytes 393224 | tf_op jit(solution)/shard_map/ppermute | solution.py:34
  171.3 5.0 %collective-permute-start.3 = (bf16[128,512]{1,0:T(8,128)(2,1)S(1)}, bf16[128,512]{1,0:T(8,128)(2,1)S(1)}, u32[]{:S(2)}, u32[]{:S(2)}) collective-permute-start(bf16[128,512]{1,0:T(8,128)(2,1)S(1)} %fusion.122), channel_id=1, source_target_pairs={{0,24},{4,28},{8,0},{12,4},{16,8},{20,12},{24,16},{28,20},{1,25},{... | collective-permute-start | bytes 393224 | tf_op jit(solution)/shard_map/ppermute | solution.py:34
  177.1 12.9 %copy-start.2 = (bf16[1024,512]{1,0:T(8,128)(2,1)S(1)}, bf16[1024,512]{1,0:T(8,128)(2,1)}, u32[]{:S(2)}) copy-start(bf16[1024,512]{1,0:T(8,128)(2,1)} %copy-done.1) | copy-start | bytes 3145732
  177.1 12.9 %copy-start.6 = (bf16[1024,512]{1,0:T(8,128)(2,1)S(1)}, bf16[1024,512]{1,0:T(8,128)(2,1)}, u32[]{:S(2)}) copy-start(bf16[1024,512]{1,0:T(8,128)(2,1)} %copy-done.5) | copy-start | bytes 3145732
  194.9 13.0 %copy-start.16 = (bf16[512,2048]{1,0:T(8,128)(2,1)S(1)}, bf16[512,2048]{1,0:T(8,128)(2,1)}, u32[]{:S(2)}) copy-start(bf16[512,2048]{1,0:T(8,128)(2,1)} %copy-done.13) | copy-start | bytes 6291460
  212.8 3.4 collective-permute-start.4
  215.0 5.5 %collective-permute-start.5 = (bf16[1,2,512]{2,1,0:T(2,128)(2,1)S(1)}, bf16[1,2,512]{2,1,0:T(2,128)(2,1)S(1)}, u32[]{:S(2)}, u32[]{:S(2)}) collective-permute-start(bf16[1,2,512]{2,1,0:T(2,128)(2,1)S(1)} %get-tuple-element.337), channel_id=1, source_target_pairs={{1,0},{2,1},{3,2},{5,4},{6,5},{7,6},{9,8},{10,9},{11,10},{13,12},{... | collective-permute-start | bytes 6152 | tf_op jit(solution)/shard_map/ppermute | solution.py:24
  233.5 122.1 %reduce-scatter.17.cloned.1.call-start = ((), (), s32[]{:S(2)}) async-start(), calls=%async_computation.14 | async-start | bytes 655360
  269.6 5.0 %collective-permute-start.6 = (bf16[128,512]{1,0:T(8,128)(2,1)S(1)}, bf16[128,512]{1,0:T(8,128)(2,1)S(1)}, u32[]{:S(2)}, u32[]{:S(2)}) collective-permute-start(bf16[128,512]{1,0:T(8,128)(2,1)S(1)} %fusion.123), channel_id=1, source_target_pairs={{0,16},{4,20},{8,24},{12,28},{16,0},{20,4},{24,8},{28,12},{1,17},{... | collective-permute-start | bytes 393224 | tf_op jit(solution)/shard_map/ppermute | solution.py:34
  273.0 5.0 %collective-permute-start.7 = (bf16[128,512]{1,0:T(8,128)(2,1)S(1)}, bf16[128,512]{1,0:T(8,128)(2,1)S(1)}, u32[]{:S(2)}, u32[]{:S(2)}) collective-permute-start(bf16[128,512]{1,0:T(8,128)(2,1)S(1)} %fusion.124), channel_id=1, source_target_pairs={{0,16},{4,20},{8,24},{12,28},{16,0},{20,4},{24,8},{28,12},{1,17},{... | collective-permute-start | bytes 393224 | tf_op jit(solution)/shard_map/ppermute | solution.py:34
  278.9 13.1 %copy-start.3 = (bf16[1024,512]{1,0:T(8,128)(2,1)S(1)}, bf16[1024,512]{1,0:T(8,128)(2,1)}, u32[]{:S(2)}) copy-start(bf16[1024,512]{1,0:T(8,128)(2,1)} %copy-done.1) | copy-start | bytes 3145732
  278.9 13.1 %copy-start.7 = (bf16[1024,512]{1,0:T(8,128)(2,1)S(1)}, bf16[1024,512]{1,0:T(8,128)(2,1)}, u32[]{:S(2)}) copy-start(bf16[1024,512]{1,0:T(8,128)(2,1)} %copy-done.5) | copy-start | bytes 3145732
  296.9 12.9 %copy-start.18 = (bf16[512,2048]{1,0:T(8,128)(2,1)S(1)}, bf16[512,2048]{1,0:T(8,128)(2,1)}, u32[]{:S(2)}) copy-start(bf16[512,2048]{1,0:T(8,128)(2,1)} %copy-done.13) | copy-start | bytes 6291460
  314.7 3.4 collective-permute-start.8
  316.8 5.5 %collective-permute-start.9 = (bf16[1,2,512]{2,1,0:T(2,128)(2,1)S(1)}, bf16[1,2,512]{2,1,0:T(2,128)(2,1)S(1)}, u32[]{:S(2)}, u32[]{:S(2)}) collective-permute-start(bf16[1,2,512]{2,1,0:T(2,128)(2,1)S(1)} %get-tuple-element.335), channel_id=1, source_target_pairs={{1,0},{2,1},{3,2},{5,4},{6,5},{7,6},{9,8},{10,9},{11,10},{13,12},{... | collective-permute-start | bytes 6152 | tf_op jit(solution)/shard_map/ppermute | solution.py:24
  335.3 121.0 %reduce-scatter.19.cloned.1.call-start = ((), (), s32[]{:S(2)}) async-start(), calls=%async_computation.15 | async-start | bytes 655360
  370.5 5.4 %collective-permute-start.10 = (bf16[128,512]{1,0:T(8,128)(2,1)S(1)}, bf16[128,512]{1,0:T(8,128)(2,1)S(1)}, u32[]{:S(2)}, u32[]{:S(2)}) collective-permute-start(bf16[128,512]{1,0:T(8,128)(2,1)S(1)} %fusion.125), channel_id=1, source_target_pairs={{0,24},{4,28},{8,0},{12,4},{16,8},{20,12},{24,16},{28,20},{1,25},{... | collective-permute-start | bytes 393224 | tf_op jit(solution)/shard_map/ppermute | solution.py:34
  373.2 7.8 %copy-start.19 = (bf16[512,2048]{1,0:T(8,128)(2,1)S(1)}, bf16[512,2048]{1,0:T(8,128)(2,1)}, u32[]{:S(2)}) copy-start(bf16[512,2048]{1,0:T(8,128)(2,1)} %copy-done.13) | copy-start | bytes 6291460
  375.0 5.9 %collective-permute-start.11 = (bf16[128,512]{1,0:T(8,128)(2,1)S(1)}, bf16[128,512]{1,0:T(8,128)(2,1)S(1)}, u32[]{:S(2)}, u32[]{:S(2)}) collective-permute-start(bf16[128,512]{1,0:T(8,128)(2,1)S(1)} %fusion.126), channel_id=1, source_target_pairs={{0,8},{4,12},{8,16},{12,20},{16,24},{20,28},{24,0},{28,4},{1,9},{5... | collective-permute-start | bytes 393224 | tf_op jit(solution)/shard_map/ppermute | solution.py:34
  381.7 12.9 %copy-start.4 = (bf16[1024,512]{1,0:T(8,128)(2,1)S(1)}, bf16[1024,512]{1,0:T(8,128)(2,1)}, u32[]{:S(2)}) copy-start(bf16[1024,512]{1,0:T(8,128)(2,1)} %copy-done.1) | copy-start | bytes 3145732
  381.7 12.9 %copy-start.8 = (bf16[1024,512]{1,0:T(8,128)(2,1)S(1)}, bf16[1024,512]{1,0:T(8,128)(2,1)}, u32[]{:S(2)}) copy-start(bf16[1024,512]{1,0:T(8,128)(2,1)} %copy-done.5) | copy-start | bytes 3145732
  399.2 13.2 %copy-start.20 = (bf16[512,2048]{1,0:T(8,128)(2,1)S(1)}, bf16[512,2048]{1,0:T(8,128)(2,1)}, u32[]{:S(2)}) copy-start(bf16[512,2048]{1,0:T(8,128)(2,1)} %copy-done.13) | copy-start | bytes 6291460
  417.3 3.4 collective-permute-start.12
  419.4 5.5 %collective-permute-start.13 = (bf16[1,2,512]{2,1,0:T(2,128)(2,1)S(1)}, bf16[1,2,512]{2,1,0:T(2,128)(2,1)S(1)}, u32[]{:S(2)}, u32[]{:S(2)}) collective-permute-start(bf16[1,2,512]{2,1,0:T(2,128)(2,1)S(1)} %get-tuple-element.333), channel_id=1, source_target_pairs={{1,0},{2,1},{3,2},{5,4},{6,5},{7,6},{9,8},{10,9},{11,10},{13,12},{... | collective-permute-start | bytes 6152 | tf_op jit(solution)/shard_map/ppermute | solution.py:24
  (16 other events, 74.2 us)
Sparse Core Ops, SparseCore 0:
  131.7 21.2 reduce-scatter.12
  233.6 21.0 reduce-scatter.14
  335.4 20.1 reduce-scatter.16
  437.0 19.2 reduce-scatter.18
where the time goes:
time: 470 us; the launch traced here: 465 us
  blocking collectives  132 us (28%)
  waiting for transfers between devices  113 us (24%)
  matrix products  67.8 us (14%)
  other arithmetic  63.9 us (14%)
  local copies, waits for them, and re-layouts  31.6 us (7%)
  starting transfers between devices  28.2 us (6%)
  between operations  15.3 us (3%)
  loops' own time  13.5 us (3%)
    unnamed x8, waiting for transfers between devices  82.2 us
    all_to_all x4, blocking collectives, potentials(): lax.all_to_all(inverse, 'tr', split_axis=0, concat_axis=1, tiled=True)  57.6 us
    another operation x11, other arithmetic  39.5 us
    all_to_all x3, blocking collectives, potentials(): lax.all_to_all(spectrum, 'tr', split_axis=1, concat_axis=0, tiled=True)  38.7 us
    all_gather x3, blocking collectives, per_device(): whole_moment = lax.all_gather(moment, 'tr', axis=3, tiled=True)  35.7 us
    ppermute x4, waiting for transfers between devices, padded(): lax.ppermute(head, axis, [((i + 1) % count, i) for i in range(ends)])  16.6 us
    dot_general x16, matrix products, deposit(): lax.dot_general(weight_rows.astype(jnp.bfloat16), weight_cols.astype(jnp....  14.4 us
    ppermute x6, waiting for transfers between devices, shifted(): return lax.ppermute(value, axis, pairs)  13.7 us
  transfers between devices with their start and end apart: 19, of which 14 were waited for; matrix products, arithmetic and copies ran while one was open for 10% of the time, Pallas kernels for 0%

commit v1 on v0

v1 whole, which is shorter than its diff:
```python
import functools
import math

import jax
import jax.numpy as jnp
import numpy as np
from jax import lax
from jax.experimental import pallas as pl
from jax.experimental.pallas import tpu as pltpu
from jax.sharding import PartitionSpec as P

SECTIONS = 4
DRIFT_STEP = 0.5
GROUP = 16
VMEM_LIMIT = 40 * 1024 * 1024

VMEM = pl.BlockSpec(memory_space=pltpu.VMEM)
ANY = pl.BlockSpec(memory_space=pl.ANY)


def dot_nn(left, right):
    return jnp.dot(left, right, preferred_element_type=jnp.float32)


def dot_nt(left, right):
    return lax.dot_general(
        left, right, (((1,), (1,)), ((), ())), preferred_element_type=jnp.float32
    )


def phases(products, period):
    theta = 2.0 * np.pi / period * (products % period)
    return np.cos(theta).astype(np.float32), np.sin(theta).astype(np.float32)


def factors(extent, period):
    half = extent // 2
    span = np.arange(extent, dtype=np.int64)
    odd = 2 * span + 1
    fine = np.arange(GROUP, dtype=np.int64)
    coarse = np.arange(extent // GROUP, dtype=np.int64)
    col_coarse = phases(2 * GROUP * coarse[:, None] * span[None, :], 2 * period)
    col_fine = phases((2 * fine + 1)[:, None] * span[None, :], 2 * period)
    inv_coarse = phases(GROUP * coarse[:, None] * odd[None, :], 2 * period)
    inv_fine = phases(fine[:, None] * odd[None, :], 2 * period)
    rows = np.arange(half, dtype=np.int64)
    row_coarse = phases(4 * GROUP * np.arange(half // GROUP)[:, None] * rows[None, :], period)
    starts = (4 * fine[None, :] + np.arange(4)[:, None]).reshape(-1)
    row_fine = phases(starts[:, None] * rows[None, :], period)
    return col_coarse + col_fine + inv_coarse + inv_fine + row_coarse + row_fine


def quarter_sums(lower, upper):
    (low_re, low_im), (high_re, high_im) = lower, upper
    return (
        (low_re + high_re, low_im + high_im),
        (low_re + high_im, low_im - high_re),
        (low_re - high_re, low_im - high_im),
        (low_re - high_im, low_im + high_re),
    )


def joined(pair):
    return jnp.concatenate([pair[0].astype(jnp.bfloat16), pair[1].astype(jnp.bfloat16)], axis=1)


def setup_kernel(
    green_ref,
    cc_cos, cc_sin, cf_cos, cf_sin,
    ic_cos, ic_sin, if_cos, if_sin,
    rc_cos, rc_sin, rf_cos, rf_sin,
    col_ref, inv_ref, row_ref, spec_ref,
    green_vm, sem,
):
    extent = cc_cos.shape[1]
    half = extent // 2
    period = green_ref.shape[0]
    copies = [
        pltpu.make_async_copy(
            green_ref.at[pl.ds(q * half, half)], green_vm.at[pl.ds(q * half, half)], sem.at[q]
        )
        for q in range(4)
    ]
    for copy in copies:
        copy.start()

    for i in range(extent // GROUP):
        rows = slice(i * GROUP, (i + 1) * GROUP)
        lower = slice(extent + i * GROUP, extent + (i + 1) * GROUP)
        ca, sa = cc_cos[i : i + 1, :], cc_sin[i : i + 1, :]
        cb, sb = cf_cos[...], cf_sin[...]
        col_ref[rows, :] = (ca * cb - sa * sb).astype(jnp.bfloat16)
        col_ref[lower, :] = (-(sa * cb + ca * sb)).astype(jnp.bfloat16)
        ca, sa = ic_cos[i : i + 1, :], ic_sin[i : i + 1, :]
        cb, sb = if_cos[...], if_sin[...]
        inv_ref[rows, :extent] = (ca * cb - sa * sb).astype(jnp.bfloat16)
        inv_ref[rows, extent:] = (-(sa * cb + ca * sb)).astype(jnp.bfloat16)
    for j in range(4):
        cb, sb = rf_cos[j * GROUP : (j + 1) * GROUP, :], rf_sin[j * GROUP : (j + 1) * GROUP, :]
        for i in range(half // GROUP):
            upper = slice(i * GROUP, (i + 1) * GROUP)
            lower = slice(half + i * GROUP, half + (i + 1) * GROUP)
            ca, sa = rc_cos[i : i + 1, :], rc_sin[i : i + 1, :]
            cosine = (ca * cb - sa * sb).astype(jnp.bfloat16)
            sine = sa * cb + ca * sb
            minus = (-sine).astype(jnp.bfloat16)
            sine = sine.astype(jnp.bfloat16)
            row_ref[j, upper, :half] = cosine
            row_ref[j, upper, half:] = sine
            row_ref[j, lower, :half] = minus
            row_ref[j, lower, half:] = cosine

    for copy in copies:
        copy.wait()
    scale = 1.0 / (period * period)
    chunk = math.gcd(extent, 256)
    for begin in range(0, extent, chunk):
        parity = lax.broadcasted_iota(jnp.int32, (chunk, half), 0) + begin
        sign = jnp.where(parity % 2 == 0, 1.0, -1.0)
        table = jnp.concatenate(
            [col_ref[begin : begin + chunk, :], col_ref[extent + begin : extent + begin + chunk, :]],
            axis=0,
        )
        parts = []
        for q in range(4):
            block = green_vm[q * half : (q + 1) * half, :].astype(jnp.bfloat16)
            near = dot_nt(table, block[:, :extent])
            far = dot_nt(table, block[:, extent:])
            parts.append(
                (near[:chunk] - sign * far[chunk:], near[chunk:] + sign * far[:chunk])
            )
        (a, b, c, d) = parts
        even = (a[0] + c[0], a[1] + c[1])
        even_less = (a[0] - c[0], a[1] - c[1])
        odd = (b[0] + d[0], b[1] + d[1])
        odd_less = (b[0] - d[0], b[1] - d[1])
        sums = (
            (even[0] + odd[0], even[1] + odd[1]),
            (even_less[0] + odd_less[1], even_less[1] - odd_less[0]),
            (even[0] - odd[0], even[1] - odd[1]),
            (even_less[0] - odd_less[1], even_less[1] + odd_less[0]),
        )
        for j in range(4):
            spec_ref[j, begin : begin + chunk, :] = dot_nt(joined(sums[j]), row_ref[j]) * scale


def hat_rows(position, count):
    nodes = lax.broadcasted_iota(jnp.int32, (count, position.shape[1]), 0).astype(jnp.float32)
    return jnp.maximum(1.0 - jnp.abs(nodes - position), 0.0)


def kicks(guest_rows, guest_cols, guest_charge, rows, cols, col_ref, inv_ref, row_ref, spec_ref, back_ref):
    extent = col_ref.shape[1]
    half = extent // 2
    weight_rows = hat_rows(guest_rows, extent).astype(jnp.bfloat16)
    weight_cols = (guest_charge * hat_rows(guest_cols, extent)).astype(jnp.bfloat16)
    grid = dot_nt(weight_cols, weight_rows).astype(jnp.bfloat16)
    chunk = math.gcd(extent, 256)
    for begin in range(0, extent, chunk):
        here = slice(begin, begin + chunk)
        there = slice(extent + begin, extent + begin + chunk)
        real = dot_nn(col_ref[here, :], grid)
        imag = dot_nn(col_ref[there, :], grid)
        sums = quarter_sums(
            (real[:, :half], imag[:, :half]), (real[:, half:], imag[:, half:])
        )
        backs = []
        for j in range(4):
            forward = dot_nt(joined(sums[j]), row_ref[j])
            kernel_re = spec_ref[j, here, :half]
            kernel_im = spec_ref[j, here, half:]
            forward_re, forward_im = forward[:, :half], forward[:, half:]
            scaled = joined(
                (
                    forward_re * kernel_re - forward_im * kernel_im,
                    forward_re * kernel_im + forward_im * kernel_re,
                )
            )
            back = dot_nn(scaled, row_ref[j])
            backs.append((back[:, :half], back[:, half:]))
        (a, b, c, d) = backs
        even = (a[0] + c[0], a[1] + c[1])
        even_less = (a[0] - c[0], a[1] - c[1])
        odd = (b[0] + d[0], b[1] + d[1])
        odd_less = (b[0] - d[0], b[1] - d[1])
        back_ref[here, :] = joined((even[0] + odd[0], even_less[0] - odd_less[1]))
        back_ref[there, :] = joined((even[1] + odd[1], even_less[1] + odd_less[0]))
    potential = dot_nn(inv_ref[...], back_ref[...])
    zero_lane = jnp.zeros((extent, 1), jnp.float32)
    zero_row = jnp.zeros((1, extent), jnp.float32)
    before = jnp.concatenate([zero_lane, potential[:, :-1]], axis=1)
    after = jnp.concatenate([potential[:, 1:], zero_lane], axis=1)
    along_rows = (before - after).astype(jnp.bfloat16)
    before = jnp.concatenate([zero_row, potential[:-1, :]], axis=0)
    after = jnp.concatenate([potential[1:, :], zero_row], axis=0)
    along_cols = (before - after).astype(jnp.bfloat16)
    weight_rows = hat_rows(rows, extent).astype(jnp.bfloat16)
    weight_cols = hat_rows(cols, extent).astype(jnp.bfloat16).astype(jnp.float32)
    kick_rows = jnp.sum(dot_nn(along_rows, weight_rows) * weight_cols, axis=0, keepdims=True)
    kick_cols = jnp.sum(dot_nn(along_cols, weight_rows) * weight_cols, axis=0, keepdims=True)
    return kick_rows, kick_cols


def advance(position, moment, extent):
    return jnp.clip(position + DRIFT_STEP * moment, 1.0, extent - 2.0 - 1.0 / 64.0)


def section_kernel(last, guest_ref, own_ref, moment_ref, col_ref, inv_ref, row_ref, spec_ref, *rest):
    extent = col_ref.shape[1]
    back_ref = rest[-1]
    rows, cols = own_ref[0:1, :], own_ref[1:2, :]
    kick_rows, kick_cols = kicks(
        guest_ref[0:1, :], guest_ref[1:2, :], guest_ref[2:3, :], rows, cols,
        col_ref, inv_ref, row_ref, spec_ref, back_ref,
    )
    moment_rows = moment_ref[0:1, :] + kick_rows
    moment_cols = moment_ref[1:2, :] + kick_cols
    out_moment_ref = rest[0]
    out_moment_ref[0:1, :] = moment_rows
    out_moment_ref[1:2, :] = moment_cols
    if not last:
        out_ref = rest[1]
        out_ref[0:1, :] = advance(rows, moment_rows, extent)
        out_ref[1:2, :] = advance(cols, moment_cols, extent)
        out_ref[2:4, :] = own_ref[2:4, :]


def per_device(cells, offsets, charges, momenta, green):
    shards = lax.axis_size("tr")
    slices = lax.axis_size("cuts")
    shard = lax.axis_index("tr")
    period = green.shape[0]
    extent = period // 2
    half = extent // 2
    particles = cells.shape[-1]
    own_count = momenta.shape[-1]
    role = shard % 2

    def slot(cut, part):
        return (cut % slices) * shards + part

    def exchange(value, steps):
        pairs = []
        for cut in range(slices):
            for part in range(shards):
                turn = steps if part % 2 == 1 else -steps
                pairs.append((slot(cut, part), slot(cut + turn, part ^ 1)))
        return lax.ppermute(value, ("cuts", "tr"), pairs)

    pieces = [lax.dynamic_index_in_dim(momenta[:, 0], 1 - role, 0, keepdims=False)]
    for step in range(1, shards):
        wanted = 1 - (shard + step) % 2
        sent = lax.dynamic_index_in_dim(momenta[:, 0], wanted, 0, keepdims=False)
        pieces.append(
            lax.ppermute(sent, "tr", [(i, (i + step) % shards) for i in range(shards)])
        )
    moment = jnp.concatenate(pieces[::-1], axis=1)
    moment = jnp.roll(moment, (shard + 1) * own_count, axis=1)

    position = cells[:, 0].astype(jnp.float32) + offsets[:, 0]
    packets = jnp.concatenate(
        [position, charges[:, 0][:, None], jnp.zeros((2, 1, particles), jnp.float32)], axis=1
    )
    own = lax.dynamic_index_in_dim(packets, 1 - role, 0, keepdims=False)
    guest = lax.dynamic_index_in_dim(packets, role, 0, keepdims=False)

    tables = pl.pallas_call(
        setup_kernel,
        out_shape=(
            jax.ShapeDtypeStruct((2 * extent, extent), jnp.bfloat16),
            jax.ShapeDtypeStruct((extent, 2 * extent), jnp.bfloat16),
            jax.ShapeDtypeStruct((4, extent, extent), jnp.bfloat16),
            jax.ShapeDtypeStruct((4, extent, extent), jnp.float32),
        ),
        in_specs=[ANY] + [VMEM] * 12,
        out_specs=(VMEM,) * 4,
        scratch_shapes=[
            pltpu.VMEM((period, period), jnp.float32),
            pltpu.SemaphoreType.DMA((4,)),
        ],
        compiler_params=pltpu.CompilerParams(vmem_limit_bytes=VMEM_LIMIT),
        cost_estimate=pl.CostEstimate(
            flops=3 * period**3, bytes_accessed=8 * period**2, transcendentals=0
        ),
        name="setup",
    )(green, *[jnp.asarray(value) for value in factors(extent, period)])

    for section in range(SECTIONS):
        last = section + 1 == SECTIONS
        if section > 0:
            guest = exchange(own, 2 * section)
        shapes = [jax.ShapeDtypeStruct((2, particles), jnp.float32)]
        if not last:
            shapes.append(jax.ShapeDtypeStruct((4, particles), jnp.float32))
        results = pl.pallas_call(
            functools.partial(section_kernel, last),
            out_shape=tuple(shapes),
            in_specs=[VMEM] * 7,
            out_specs=(VMEM,) * len(shapes),
            scratch_shapes=[pltpu.VMEM((2 * extent, extent), jnp.bfloat16)],
            compiler_params=pltpu.CompilerParams(vmem_limit_bytes=VMEM_LIMIT),
            cost_estimate=pl.CostEstimate(
                flops=5 * period**3, bytes_accessed=8 * period**2, transcendentals=0
            ),
            name="section",
        )(guest, own, moment, *tables)
        moment = results[0]
        if not last:
            own = results[1]

    mine = lax.dynamic_slice_in_dim(moment, shard * own_count, own_count, axis=1)
    partner = shard + 1 - 2 * role
    theirs = lax.dynamic_slice_in_dim(moment, partner * own_count, own_count, axis=1)
    received = exchange(theirs, 0)
    first = jnp.where(role == 1, mine, received)
    second = jnp.where(role == 1, received, mine)
    return jnp.stack([first, second])[:, None]


def solution(mesh):
    return jax.shard_map(
        per_device,
        mesh=mesh,
        in_specs=(
            P(None, "cuts", None, None),
            P(None, "cuts", None, None),
            P(None, "cuts", None),
            P(None, "cuts", None, "tr"),
            P(),
        ),
        out_specs=P(None, "cuts", None, "tr"),
        check_vma=False,
    )
```

time: 470 us -> 83 us (0.18)
  blocking collectives: 132 us -> 0 us
  waiting for transfers between devices: 113 us -> 12.6 us
  matrix products: 67.8 us -> 0 us
  other arithmetic: 63.9 us -> 2.12 us
  Pallas kernels: 0 us -> 31.6 us
  starting transfers between devices: 28.2 us -> 13 us
  between operations: 15.3 us -> 0.14 us
  loops' own time: 13.5 us -> 0 us
  local copies, waits for them, and re-layouts: 31.6 us -> 22.4 us
    all_to_all x7 -> x0, blocking collectives: 96.2 us -> none  [the longest x4 57.6 us: potentials(): lax.all_to_all(inverse, 'tr', split_axis=0, concat_axis=1, tiled=True)]
    unnamed x8 -> x0, waiting for transfers between devices: 82.2 us -> none
    dot_general x66 -> x0, matrix products: 67.8 us -> none  [the longest x16 14.4 us: deposit(): lax.dot_general(weight_rows.astype(jnp.bfloat16), weight_cols.astype(jnp....]
    another operation x15 -> x1, other arithmetic: 40.5 us -> 0.01 us  [per_device(): return jnp.stack([first, second])[:, None]]
    all_gather x3 -> x0, blocking collectives: 35.7 us -> none  [per_device(): whole_moment = lax.all_gather(moment, 'tr', axis=3, tiled=True)]
    pallas_call x0 -> x5, Pallas kernels: none -> 31.6 us  [the longest x4 26.6 us: per_device(): pl.pallas_call(functools.partial(section_kernel, last), out_shape=tuple(s...]
    ppermute x14 -> x7, waiting for transfers between devices: 30.4 us -> 12.6 us  [the longest x4 12.6 us: exchange(): return lax.ppermute(value, ('cuts', 'tr'), pairs)]
    another operation x4 -> x0, loops' own time: 13.5 us -> none  [kick_terms(): lax.map(one_block, jnp.arange(row_count // block_size, dtype=jnp.int32))]
  transfers between devices with their start and end apart: 19 -> 7, of which waited for: 14 -> 4; matrix products, arithmetic and copies ran while one was open for 10% -> 2% of each run, Pallas kernels for 0% -> 6%
where the time goes in v1:
time: 83 us; the launch traced here: 81.9 us
  Pallas kernels  31.6 us (38%)
  local copies, waits for them, and re-layouts  22.4 us (27%)
  starting transfers between devices  13 us (16%)
  waiting for transfers between devices  12.6 us (15%)
  other arithmetic  2.12 us (3%)
    pallas_call x4, Pallas kernels, per_device(): pl.pallas_call(functools.partial(section_kernel, last), out_shape=tuple(s...  26.6 us
    unnamed x47, local copies, waits for them, and re-layouts  21.5 us
    ppermute x4, waiting for transfers between devices, exchange(): return lax.ppermute(value, ('cuts', 'tr'), pairs)  12.6 us
    ppermute x3, starting transfers between devices, per_device(): lax.ppermute(sent, 'tr', [(i, (i + step) % shards) for i in range(shards)])  6.99 us
    ppermute x4, starting transfers between devices, exchange(): return lax.ppermute(value, ('cuts', 'tr'), pairs)  6.04 us
    pallas_call x1, Pallas kernels, per_device(): pl.pallas_call(setup_kernel, out_shape=(jax.ShapeDtypeStruct((2 * extent,...  5.02 us
  transfers between devices with their start and end apart: 7, of which 4 were waited for; matrix products, arithmetic and copies ran while one was open for 2% of the time, Pallas kernels for 6%

profile of v1, /device:TPU:0, one launch (start us, length us, event | category | flops | bytes accessed | tf_op | source)
XLA Modules:
  0.0 81.9 jit_solution(7328626095002163697)
XLA Ops:
  0.0 0.8 fusion.2
  0.8 3.1 %collective-permute-start.2 = (f32[2,256]{1,0:T(2,128)S(1)}, f32[2,256]{1,0:T(2,128)S(1)}, u32[]{:S(2)}, u32[]{:S(2)}) collective-permute-start(f32[2,256]{1,0:T(2,128)S(1)} %get-tuple-element.29), channel_id=1, source_target_pairs={{0,1},{1,2},{2,3},{3,0},{4,5},{5,6},{6,7},{7,4},{8,9},{9,10},{10,1... | collective-permute-start | bytes 6152 | tf_op jit(solution)/shard_map/ppermute | solution.py:255
  3.8 2.6 %collective-permute-start.1 = (f32[2,256]{1,0:T(2,128)S(1)}, f32[2,256]{1,0:T(2,128)S(1)}, u32[]{:S(2)}, u32[]{:S(2)}) collective-permute-start(f32[2,256]{1,0:T(2,128)S(1)} %get-tuple-element.30), channel_id=1, source_target_pairs={{0,2},{1,3},{2,0},{3,1},{4,6},{5,7},{6,4},{7,5},{8,10},{9,11},{10,... | collective-permute-start | bytes 6152 | tf_op jit(solution)/shard_map/ppermute | solution.py:255
  6.4 1.3 %collective-permute-start = (f32[2,256]{1,0:T(2,128)S(1)}, f32[2,256]{1,0:T(2,128)S(1)}, u32[]{:S(2)}, u32[]{:S(2)}) collective-permute-start(f32[2,256]{1,0:T(2,128)S(1)} %get-tuple-element.31), channel_id=1, source_target_pairs={{0,3},{1,0},{2,1},{3,2},{4,7},{5,4},{6,5},{7,6},{8,11},{9,8},{10,9... | collective-permute-start | bytes 6152 | tf_op jit(solution)/shard_map/ppermute | solution.py:255
  8.6 0.8 maximum_maximum_fusion
  9.3 2.2 %copy-done = f32[1024,1024]{1,0:T(8,128)S(1)} copy-done((f32[1024,1024]{1,0:T(8,128)S(1)}, f32[1024,1024]{1,0:T(8,128)}, u32[]{:S(2)}) %copy-start) | copy-done | bytes 4194328
  11.5 0.8 %copy-done.1 = f32[64,256]{1,0:T(8,128)S(1)} copy-done((f32[64,256]{1,0:T(8,128)S(1)}, f32[64,256]{1,0:T(8,128)}, u32[]{:S(2)}) %copy-start.1) | copy-done | bytes 65560
  12.4 0.8 %copy-done.2 = f32[64,256]{1,0:T(8,128)S(1)} copy-done((f32[64,256]{1,0:T(8,128)S(1)}, f32[64,256]{1,0:T(8,128)}, u32[]{:S(2)}) %copy-start.2) | copy-done | bytes 65560
  13.2 0.8 %copy-done.3 = f32[32,512]{1,0:T(8,128)S(1)} copy-done((f32[32,512]{1,0:T(8,128)S(1)}, f32[32,512]{1,0:T(8,128)}, u32[]{:S(2)}) %copy-start.3) | copy-done | bytes 65560
  14.1 0.8 %copy-done.4 = f32[32,512]{1,0:T(8,128)S(1)} copy-done((f32[32,512]{1,0:T(8,128)S(1)}, f32[32,512]{1,0:T(8,128)}, u32[]{:S(2)}) %copy-start.4) | copy-done | bytes 65560
  14.9 0.8 %copy-done.5 = f32[32,512]{1,0:T(8,128)S(1)} copy-done((f32[32,512]{1,0:T(8,128)S(1)}, f32[32,512]{1,0:T(8,128)}, u32[]{:S(2)}) %copy-start.5) | copy-done | bytes 65560
  15.7 0.8 %copy-done.6 = f32[32,512]{1,0:T(8,128)S(1)} copy-done((f32[32,512]{1,0:T(8,128)S(1)}, f32[32,512]{1,0:T(8,128)}, u32[]{:S(2)}) %copy-start.6) | copy-done | bytes 65560
  16.6 0.8 copy-done.7
  21.0 5.0 %setup.1 = (bf16[1024,512]{1,0:T(8,128)(2,1)S(1)}, bf16[512,1024]{1,0:T(8,128)(2,1)S(1)}, bf16[4,512,512]{2,1,0:T(8,128)(2,1)S(1)}, f32[4,512,512]{2,1,0:T(8,128)S(1)}) custom-call(f32[1024,1024]{1,0:T(8,128)S(1)} %copy-done, f32[32,512]{1,0:T(8,128)S(1)} %copy-done.6, f32[32,512]{1,0:T(8,128)S(1)} %copy-done.5, f32[16,512]{1,0:T(8,128)S(1)} %copy-done.10, ...), custom_call_target="tpu_custom_call" | custom-call | flops 3221225472 | bytes 8388608 | tf_op jit(solution)/shard_map/setup/pallas_call | solution.py:267
  26.1 1.9 %copy-done.13 = f32[4,512,512]{2,1,0:T(8,128)} copy-done((f32[4,512,512]{2,1,0:T(8,128)}, f32[4,512,512]{2,1,0:T(8,128)S(1)}, u32[]{:S(2)}) %copy-start.13) | copy-done | bytes 4194328
  28.0 1.0 %copy-done.16 = bf16[512,1024]{1,0:T(8,128)(2,1)} copy-done((bf16[512,1024]{1,0:T(8,128)(2,1)}, bf16[512,1024]{1,0:T(8,128)(2,1)S(1)}, u32[]{:S(2)}) %copy-start.16) | copy-done | bytes 1048600
  29.2 2.2 %copy-done.14 = f32[4,512,512]{2,1,0:T(8,128)S(1)} copy-done((f32[4,512,512]{2,1,0:T(8,128)S(1)}, f32[4,512,512]{2,1,0:T(8,128)}, u32[]{:S(2)}) %copy-start.14) | copy-done | bytes 4194328
  31.4 1.2 %copy-done.17 = bf16[512,1024]{1,0:T(8,128)(2,1)S(1)} copy-done((bf16[512,1024]{1,0:T(8,128)(2,1)S(1)}, bf16[512,1024]{1,0:T(8,128)(2,1)}, u32[]{:S(2)}) %copy-start.17) | copy-done | bytes 1048600
  32.6 6.6 %section.4 = (f32[2,1024]{1,0:T(2,128)S(1)}, f32[4,1024]{1,0:T(4,128)S(1)}) custom-call(f32[4,1024]{1,0:T(4,128)S(1)} %get-tuple-element.26.guest_ref, f32[4,1024]{1,0:T(4,128)S(1)} %get-tuple-element.25.own_ref, f32[2,1024]{1,0:T(2,128)S(1)} %constant_dynamic-slice_fusion.2.moment_ref, bf16[1024,512]{1,0:T(8,128)(2,1)S(1)} %get-tuple-element.15.col_ref, ...), custom_call_target="tpu_custom_call" | custom-call | flops 5368709120 | bytes 8388608 | tf_op jit(solution)/shard_map/section/pallas_call | solution.py:295
  39.3 2.6 %collective-permute-start.3 = (f32[4,1024]{1,0:T(4,128)S(1)}, f32[4,1024]{1,0:T(4,128)S(1)}, u32[]{:S(2)}, u32[]{:S(2)}) collective-permute-start(f32[4,1024]{1,0:T(4,128)S(1)} %get-tuple-element.19.own_ref), channel_id=1, source_target_pairs={{0,25},{1,8},{2,27},{3,10},{4,29},{5,12},{6,31},{7,14},{8,1},{9,16... | collective-permute-start | bytes 49160 | tf_op jit(solution)/shard_map/ppermute | solution.py:248
  41.8 3.0 %collective-permute-done.3.guest_ref = f32[4,1024]{1,0:T(4,128)S(1)} collective-permute-done((f32[4,1024]{1,0:T(4,128)S(1)}, f32[4,1024]{1,0:T(4,128)S(1)}, u32[]{:S(2)}, u32[]{:S(2)}) %collective-permute-start.3) | collective-permute-done | bytes 16416 | tf_op jit(solution)/shard_map/ppermute | solution.py:248
  44.9 6.8 %section.5 = (f32[2,1024]{1,0:T(2,128)S(1)}, f32[4,1024]{1,0:T(4,128)S(1)}) custom-call(f32[4,1024]{1,0:T(4,128)S(1)} %collective-permute-done.3.guest_ref, f32[4,1024]{1,0:T(4,128)S(1)} %get-tuple-element.19.own_ref, f32[2,1024]{1,0:T(2,128)S(1)} %get-tuple-element.20.moment_ref, bf16[1024,512]{1,0:T(8,128)(2,1)S(1)} %get-tuple-element.15.col_ref, ...), custom_call_target="tpu_custom_call" | custom-call | flops 5368709120 | bytes 8388608 | tf_op jit(solution)/shard_map/section/pallas_call | solution.py:295
  51.6 0.8 collective-permute-start.4
  52.4 3.9 %collective-permute-done.4.guest_ref = f32[4,1024]{1,0:T(4,128)S(1)} collective-permute-done((f32[4,1024]{1,0:T(4,128)S(1)}, f32[4,1024]{1,0:T(4,128)S(1)}, u32[]{:S(2)}, u32[]{:S(2)}) %collective-permute-start.4) | collective-permute-done | bytes 16416 | tf_op jit(solution)/shard_map/ppermute | solution.py:248
  56.3 6.6 %section.6 = (f32[2,1024]{1,0:T(2,128)S(1)}, f32[4,1024]{1,0:T(4,128)S(1)}) custom-call(f32[4,1024]{1,0:T(4,128)S(1)} %collective-permute-done.4.guest_ref, f32[4,1024]{1,0:T(4,128)S(1)} %get-tuple-element.21.own_ref, f32[2,1024]{1,0:T(2,128)S(1)} %get-tuple-element.22.moment_ref, bf16[1024,512]{1,0:T(8,128)(2,1)S(1)} %get-tuple-element.15.col_ref, ...), custom_call_target="tpu_custom_call" | custom-call | flops 5368709120 | bytes 8388608 | tf_op jit(solution)/shard_map/section/pallas_call | solution.py:295
  62.9 1.6 %collective-permute-start.5 = (f32[4,1024]{1,0:T(4,128)S(1)}, f32[4,1024]{1,0:T(4,128)S(1)}, u32[]{:S(2)}, u32[]{:S(2)}) collective-permute-start(f32[4,1024]{1,0:T(4,128)S(1)} %get-tuple-element.23.own_ref), channel_id=1, source_target_pairs={{0,9},{1,24},{2,11},{3,26},{4,13},{5,28},{6,15},{7,30},{8,17},{9,0... | collective-permute-start | bytes 49160 | tf_op jit(solution)/shard_map/ppermute | solution.py:248
  64.6 3.1 %collective-permute-done.5.guest_ref = f32[4,1024]{1,0:T(4,128)S(1)} collective-permute-done((f32[4,1024]{1,0:T(4,128)S(1)}, f32[4,1024]{1,0:T(4,128)S(1)}, u32[]{:S(2)}, u32[]{:S(2)}) %collective-permute-start.5) | collective-permute-done | bytes 16416 | tf_op jit(solution)/shard_map/ppermute | solution.py:248
  67.6 2.2 %copy-done.15 = f32[4,512,512]{2,1,0:T(8,128)S(1)} copy-done((f32[4,512,512]{2,1,0:T(8,128)S(1)}, f32[4,512,512]{2,1,0:T(8,128)}, u32[]{:S(2)}) %copy-start.15) | copy-done | bytes 4194328
  69.8 1.2 %copy-done.18 = bf16[512,1024]{1,0:T(8,128)(2,1)S(1)} copy-done((bf16[512,1024]{1,0:T(8,128)(2,1)S(1)}, bf16[512,1024]{1,0:T(8,128)(2,1)}, u32[]{:S(2)}) %copy-start.18) | copy-done | bytes 1048600
  71.1 6.6 %section.7 = f32[2,1024]{1,0:T(2,128)S(1)} custom-call(f32[4,1024]{1,0:T(4,128)S(1)} %collective-permute-done.5.guest_ref, f32[4,1024]{1,0:T(4,128)S(1)} %get-tuple-element.23.own_ref, f32[2,1024]{1,0:T(2,128)S(1)} %get-tuple-element.24.moment_ref, bf16[1024,512]{1,0:T(8,128)(2,1)S(1)} %get-tuple-element.15.col_ref, bf16[512,1024]{1,0:T(8,128)(2,1)S(1)} %copy-done.18, ...), custom_call_target="tpu_custom_call" | custom-call | flops 5368709120 | bytes 8388608 | tf_op jit(solution)/shard_map/section/pallas_call | solution.py:295
  77.7 1.0 %collective-permute-start.6 = (f32[2,256]{1,0:T(2,128)S(1)}, f32[2,256]{1,0:T(2,128)S(1)}, u32[]{:S(2)}, u32[]{:S(2)}) collective-permute-start(f32[2,256]{1,0:T(2,128)S(1)} %constant_dynamic-slice_fusion), channel_id=1, source_target_pairs={{0,1},{1,0},{2,3},{3,2},{4,5},{5,4},{6,7},{7,6},{8,9},{9,8},{10,11... | collective-permute-start | bytes 6152 | tf_op jit(solution)/shard_map/ppermute | solution.py:248
  78.7 2.6 %collective-permute-done.6 = f32[2,256]{1,0:T(2,128)S(1)} collective-permute-done((f32[2,256]{1,0:T(2,128)S(1)}, f32[2,256]{1,0:T(2,128)S(1)}, u32[]{:S(2)}, u32[]{:S(2)}) %collective-permute-start.6) | collective-permute-done | bytes 2080 | tf_op jit(solution)/shard_map/ppermute | solution.py:248
  (44 shorter events, 5.3 us)
Async XLA Ops:
  0.8 28.3 %collective-permute-start.2 = (f32[2,256]{1,0:T(2,128)S(1)}, f32[2,256]{1,0:T(2,128)S(1)}, u32[]{:S(2)}, u32[]{:S(2)}) collective-permute-start(f32[2,256]{1,0:T(2,128)S(1)} %get-tuple-element.29), channel_id=1, source_target_pairs={{0,1},{1,2},{2,3},{3,0},{4,5},{5,6},{6,7},{7,4},{8,9},{9,10},{10,1... | collective-permute-start | bytes 6152 | tf_op jit(solution)/shard_map/ppermute | solution.py:255
  3.8 25.3 %collective-permute-start.1 = (f32[2,256]{1,0:T(2,128)S(1)}, f32[2,256]{1,0:T(2,128)S(1)}, u32[]{:S(2)}, u32[]{:S(2)}) collective-permute-start(f32[2,256]{1,0:T(2,128)S(1)} %get-tuple-element.30), channel_id=1, source_target_pairs={{0,2},{1,3},{2,0},{3,1},{4,6},{5,7},{6,4},{7,5},{8,10},{9,11},{10,... | collective-permute-start | bytes 6152 | tf_op jit(solution)/shard_map/ppermute | solution.py:255
  6.4 22.7 %collective-permute-start = (f32[2,256]{1,0:T(2,128)S(1)}, f32[2,256]{1,0:T(2,128)S(1)}, u32[]{:S(2)}, u32[]{:S(2)}) collective-permute-start(f32[2,256]{1,0:T(2,128)S(1)} %get-tuple-element.31), channel_id=1, source_target_pairs={{0,3},{1,0},{2,1},{3,2},{4,7},{5,4},{6,5},{7,6},{8,11},{9,8},{10,9... | collective-permute-start | bytes 6152 | tf_op jit(solution)/shard_map/ppermute | solution.py:255
  9.3 2.2 %copy-start = (f32[1024,1024]{1,0:T(8,128)S(1)}, f32[1024,1024]{1,0:T(8,128)}, u32[]{:S(2)}) copy-start(f32[1024,1024]{1,0:T(8,128)} %green_ref.1) | copy-start | bytes 12582916
  11.5 0.8 %copy-start.1 = (f32[64,256]{1,0:T(8,128)S(1)}, f32[64,256]{1,0:T(8,128)}, u32[]{:S(2)}) copy-start(f32[64,256]{1,0:T(8,128)} %constant.118.clone.rf_sin) | copy-start | bytes 196612
  12.4 0.8 %copy-start.2 = (f32[64,256]{1,0:T(8,128)S(1)}, f32[64,256]{1,0:T(8,128)}, u32[]{:S(2)}) copy-start(f32[64,256]{1,0:T(8,128)} %constant.117.clone.rf_cos) | copy-start | bytes 196612
  13.2 0.8 %copy-start.3 = (f32[32,512]{1,0:T(8,128)S(1)}, f32[32,512]{1,0:T(8,128)}, u32[]{:S(2)}) copy-start(f32[32,512]{1,0:T(8,128)} %constant.112.clone.ic_sin) | copy-start | bytes 196612
  14.1 0.8 %copy-start.4 = (f32[32,512]{1,0:T(8,128)S(1)}, f32[32,512]{1,0:T(8,128)}, u32[]{:S(2)}) copy-start(f32[32,512]{1,0:T(8,128)} %constant.111.clone.ic_cos) | copy-start | bytes 196612
  14.9 0.8 %copy-start.5 = (f32[32,512]{1,0:T(8,128)S(1)}, f32[32,512]{1,0:T(8,128)}, u32[]{:S(2)}) copy-start(f32[32,512]{1,0:T(8,128)} %constant.108.clone.cc_sin) | copy-start | bytes 196612
  15.7 0.8 %copy-start.6 = (f32[32,512]{1,0:T(8,128)S(1)}, f32[32,512]{1,0:T(8,128)}, u32[]{:S(2)}) copy-start(f32[32,512]{1,0:T(8,128)} %constant.107.clone.cc_cos) | copy-start | bytes 196612
  16.6 0.8 copy-start.7
  17.3 0.8 copy-start.8
  18.1 0.8 copy-start.9
  18.9 0.8 copy-start.10
  19.6 0.7 copy-start.11
  20.3 0.7 copy-start.12
  21.0 8.1 %copy-start.19 = (f32[2,1,2,256]{3,2,1,0:T(2,128)S(1)}, f32[2,1,2,256]{3,2,1,0:T(2,128)}, u32[]{:S(2)}) copy-start(f32[2,1,2,256]{3,2,1,0:T(2,128)} %param.20) | copy-start | bytes 12292
  26.1 2.0 %copy-start.13 = (f32[4,512,512]{2,1,0:T(8,128)}, f32[4,512,512]{2,1,0:T(8,128)S(1)}, u32[]{:S(2)}) copy-start(f32[4,512,512]{2,1,0:T(8,128)S(1)} %get-tuple-element.18.spec_ref) | copy-start | bytes 12582916
  28.0 1.0 %copy-start.16 = (bf16[512,1024]{1,0:T(8,128)(2,1)}, bf16[512,1024]{1,0:T(8,128)(2,1)S(1)}, u32[]{:S(2)}) copy-start(bf16[512,1024]{1,0:T(8,128)(2,1)S(1)} %get-tuple-element.16.inv_ref) | copy-start | bytes 3145732
  29.2 2.2 %copy-start.14 = (f32[4,512,512]{2,1,0:T(8,128)S(1)}, f32[4,512,512]{2,1,0:T(8,128)}, u32[]{:S(2)}) copy-start(f32[4,512,512]{2,1,0:T(8,128)} %copy-done.13) | copy-start | bytes 12582916
  31.4 1.2 %copy-start.17 = (bf16[512,1024]{1,0:T(8,128)(2,1)S(1)}, bf16[512,1024]{1,0:T(8,128)(2,1)}, u32[]{:S(2)}) copy-start(bf16[512,1024]{1,0:T(8,128)(2,1)} %copy-done.16) | copy-start | bytes 3145732
  39.3 5.6 %collective-permute-start.3 = (f32[4,1024]{1,0:T(4,128)S(1)}, f32[4,1024]{1,0:T(4,128)S(1)}, u32[]{:S(2)}, u32[]{:S(2)}) collective-permute-start(f32[4,1024]{1,0:T(4,128)S(1)} %get-tuple-element.19.own_ref), channel_id=1, source_target_pairs={{0,25},{1,8},{2,27},{3,10},{4,29},{5,12},{6,31},{7,14},{8,1},{9,16... | collective-permute-start | bytes 49160 | tf_op jit(solution)/shard_map/ppermute | solution.py:248
  51.6 4.7 %collective-permute-start.4 = (f32[4,1024]{1,0:T(4,128)S(1)}, f32[4,1024]{1,0:T(4,128)S(1)}, u32[]{:S(2)}, u32[]{:S(2)}) collective-permute-start(f32[4,1024]{1,0:T(4,128)S(1)} %get-tuple-element.21.own_ref), channel_id=1, source_target_pairs={{0,17},{1,16},{2,19},{3,18},{4,21},{5,20},{6,23},{7,22},{8,25},{9,... | collective-permute-start | bytes 49160 | tf_op jit(solution)/shard_map/ppermute | solution.py:248
  62.9 4.7 %collective-permute-start.5 = (f32[4,1024]{1,0:T(4,128)S(1)}, f32[4,1024]{1,0:T(4,128)S(1)}, u32[]{:S(2)}, u32[]{:S(2)}) collective-permute-start(f32[4,1024]{1,0:T(4,128)S(1)} %get-tuple-element.23.own_ref), channel_id=1, source_target_pairs={{0,9},{1,24},{2,11},{3,26},{4,13},{5,28},{6,15},{7,30},{8,17},{9,0... | collective-permute-start | bytes 49160 | tf_op jit(solution)/shard_map/ppermute | solution.py:248
  67.6 2.2 %copy-start.15 = (f32[4,512,512]{2,1,0:T(8,128)S(1)}, f32[4,512,512]{2,1,0:T(8,128)}, u32[]{:S(2)}) copy-start(f32[4,512,512]{2,1,0:T(8,128)} %copy-done.13) | copy-start | bytes 12582916
  69.8 1.2 %copy-start.18 = (bf16[512,1024]{1,0:T(8,128)(2,1)S(1)}, bf16[512,1024]{1,0:T(8,128)(2,1)}, u32[]{:S(2)}) copy-start(bf16[512,1024]{1,0:T(8,128)(2,1)} %copy-done.16) | copy-start | bytes 3145732
  77.7 3.7 %collective-permute-start.6 = (f32[2,256]{1,0:T(2,128)S(1)}, f32[2,256]{1,0:T(2,128)S(1)}, u32[]{:S(2)}, u32[]{:S(2)}) collective-permute-start(f32[2,256]{1,0:T(2,128)S(1)} %constant_dynamic-slice_fusion), channel_id=1, source_target_pairs={{0,1},{1,0},{2,3},{3,2},{4,5},{5,4},{6,7},{7,6},{8,9},{9,8},{10,11... | collective-permute-start | bytes 6152 | tf_op jit(solution)/shard_map/ppermute | solution.py:248

commit v2 on v1

v2 whole, which is shorter than its diff:
```python
import functools
import math

import jax
import jax.numpy as jnp
import numpy as np
from jax import lax
from jax.experimental import pallas as pl
from jax.experimental.pallas import tpu as pltpu
from jax.sharding import PartitionSpec as P

SECTIONS = 4
DRIFT_STEP = 0.5
GROUP = 16
SETUP_VMEM = 54 * 1024 * 1024
SECTION_VMEM = 28 * 1024 * 1024
HALF_ROOT = math.sqrt(0.5)

VMEM = pl.BlockSpec(memory_space=pltpu.VMEM)
HBM = pl.BlockSpec(memory_space=pltpu.MemorySpace.HBM)


def dot_nn(left, right):
    return jnp.dot(left, right, preferred_element_type=jnp.float32)


def dot_nt(left, right):
    return lax.dot_general(
        left, right, (((1,), (1,)), ((), ())), preferred_element_type=jnp.float32
    )


def phases(products, period):
    theta = 2.0 * np.pi / period * (products % period)
    return np.cos(theta).astype(np.float32), np.sin(theta).astype(np.float32)


def factors(extent):
    half = extent // 2
    eighth = extent // 4
    period = 2 * extent
    cells = np.arange(extent, dtype=np.int64)
    split = np.concatenate([cells[0::2], cells[1::2]])
    odd = 2 * cells[:half] + 1
    fine = np.arange(GROUP, dtype=np.int64)
    coarse = np.arange(half // GROUP, dtype=np.int64)
    few = np.arange(eighth // GROUP, dtype=np.int64)
    starts = (8 * fine[None, :] + np.arange(8)[:, None]).reshape(-1)
    pieces = []
    for order in (split, cells):
        pieces += phases(2 * GROUP * coarse[:, None] * order[None, :], 2 * period)
        pieces += phases((2 * fine + 1)[:, None] * order[None, :], 2 * period)
    for rows in (2 * GROUP * coarse, 2 * fine, 2 * fine + 1):
        pieces.append(np.concatenate(phases(rows[:, None] * odd[None, :], 2 * period), axis=1))
    for rows in (8 * GROUP * few, starts):
        both = np.concatenate(phases(rows[:, None] * cells[None, :eighth], period), axis=1)
        pieces.append(np.concatenate([both, both], axis=1))
    begins = np.cumsum([0] + [piece.shape[0] for piece in pieces])
    total = -(-int(begins[-1]) // 8) * 8
    packed = np.zeros((total, extent), np.float32)
    packed[: begins[-1]] = np.concatenate(pieces, axis=0)
    return packed, [int(begin) for begin in begins[:-1]]


def turned(cos_a, sin_a, cos_b, sin_b):
    return cos_a * cos_b - sin_a * sin_b, sin_a * cos_b + cos_a * sin_b


def added(left, right):
    return left[0] + right[0], left[1] + right[1]


def less(left, right):
    return left[0] - right[0], left[1] - right[1]


def times_i(value):
    return -value[1], value[0]


def four_points(values, turn):
    even, even_less = added(values[0], values[2]), less(values[0], values[2])
    odd, odd_less = added(values[1], values[3]), less(values[1], values[3])
    side = times_i(odd_less)
    up, down = added(even_less, side), less(even_less, side)
    if turn < 0:
        up, down = down, up
    return added(even, odd), up, less(even, odd), down


def eighths(values, turn):
    first, second, third, fourth = values
    plus = ((second[0] - turn * second[1]) * HALF_ROOT, (second[1] + turn * second[0]) * HALF_ROOT)
    third = times_i(third)
    if turn < 0:
        third = (-third[0], -third[1])
    minus = (
        (-fourth[0] - turn * fourth[1]) * HALF_ROOT,
        (turn * fourth[0] - fourth[1]) * HALF_ROOT,
    )
    return first, plus, third, minus


def joined(pair):
    return jnp.concatenate([pair[0].astype(jnp.bfloat16), pair[1].astype(jnp.bfloat16)], axis=1)


def spread(values):
    even = four_points(values, -1)
    odd = four_points(eighths(values, -1), -1)
    return [pair for couple in zip(even, odd) for pair in couple]


def gathered(values):
    even = four_points(values[0::2], 1)
    odd = eighths(four_points(values[1::2], 1), 1)
    return [added(left, right) for left, right in zip(even, odd)]


def setup_kernel(begins, green_ref, factor_ref, col_ref, inv_ref, row_ref, spec_ref,
                 wide_ref, green_vm, factor_vm, sem):
    extent = col_ref.shape[1]
    half = extent // 2
    eighth = extent // 4
    period = 2 * extent
    first = pltpu.make_async_copy(factor_ref, factor_vm, sem.at[8])
    first.start()
    copies = [
        pltpu.make_async_copy(
            green_ref.at[pl.ds(q * eighth, eighth)], green_vm.at[pl.ds(q * eighth, eighth)], sem.at[q]
        )
        for q in range(8)
    ]
    for copy in copies:
        copy.start()
    first.wait()

    def column_tables(base, i):
        cos_a = factor_vm[begins[base] + i : begins[base] + i + 1, :]
        sin_a = factor_vm[begins[base + 1] + i : begins[base + 1] + i + 1, :]
        cos_b = factor_vm[begins[base + 2] : begins[base + 2] + GROUP, :]
        sin_b = factor_vm[begins[base + 3] : begins[base + 3] + GROUP, :]
        return turned(cos_a, sin_a, cos_b, sin_b)

    parity = lax.broadcasted_iota(jnp.int32, (GROUP, extent), 1) % 2
    flip = jnp.where(parity == 0, 1.0, -1.0)
    for i in range(half // GROUP):
        rows = i * GROUP
        cosine, sine = column_tables(0, i)
        col_ref[rows : rows + GROUP, :] = cosine.astype(jnp.bfloat16)
        col_ref[half + rows : half + rows + GROUP, :] = (-sine).astype(jnp.bfloat16)
        cosine, sine = column_tables(4, i)
        block = rows // eighth * extent + rows % eighth
        for turn in range(2):
            if turn:
                cosine, sine = cosine * flip, sine * flip
            at = block + turn * eighth
            wide_ref[at : at + GROUP, :] = cosine.astype(jnp.bfloat16)
            wide_ref[at + half : at + half + GROUP, :] = (-sine).astype(jnp.bfloat16)
        coarse = factor_vm[begins[8] + i : begins[8] + i + 1, :]
        for turn in range(2):
            fine = factor_vm[begins[9 + turn] : begins[9 + turn] + GROUP, :]
            cosine, sine = turned(coarse[:, :half], coarse[:, half:], fine[:, :half], fine[:, half:])
            at = turn * half + rows
            inv_ref[at : at + GROUP, :half] = cosine.astype(jnp.bfloat16)
            inv_ref[at : at + GROUP, half:] = (-sine).astype(jnp.bfloat16)
    for j in range(8):
        fine = factor_vm[begins[12] + j * GROUP : begins[12] + (j + 1) * GROUP, :]
        for i in range(eighth // GROUP):
            coarse = factor_vm[begins[11] + i : begins[11] + i + 1, :]
            cosine, sine = turned(
                coarse[:, :eighth], coarse[:, eighth:half], fine[:, :eighth], fine[:, eighth:half]
            )
            upper = i * GROUP
            lower = eighth + i * GROUP
            row_ref[j, upper : upper + GROUP, :eighth] = cosine.astype(jnp.bfloat16)
            row_ref[j, upper : upper + GROUP, eighth:] = sine.astype(jnp.bfloat16)
            row_ref[j, lower : lower + GROUP, :eighth] = (-sine).astype(jnp.bfloat16)
            row_ref[j, lower : lower + GROUP, eighth:] = cosine.astype(jnp.bfloat16)

    for copy in copies:
        copy.wait()
    scale = 1.0 / (period * period)
    parity = lax.broadcasted_iota(jnp.int32, (half, eighth), 0) % 2
    sign = jnp.where(parity == 0, 1.0, -1.0)
    for begin in range(0, extent, half):
        table = wide_ref[2 * begin : 2 * begin + extent, :]
        parts = []
        for q in range(8):
            block = green_vm[q * eighth : (q + 1) * eighth, :].astype(jnp.bfloat16)
            near = dot_nt(table, block[:, :extent])
            far = dot_nt(table, block[:, extent:])
            parts.append((near[:half] - sign * far[half:], near[half:] + sign * far[:half]))
        even = four_points([added(parts[q], parts[q + 4]) for q in range(4)], -1)
        odd = four_points(eighths([less(parts[q], parts[q + 4]) for q in range(4)], -1), -1)
        sums = [pair for couple in zip(even, odd) for pair in couple]
        for j in range(8):
            spec_ref[j, begin : begin + half, :] = dot_nt(joined(sums[j]), row_ref[j]) * scale


def hats(nodes, position):
    return jnp.maximum(1.0 - jnp.abs(nodes - position), 0.0)


def row_hats(position, extent):
    nodes = lax.broadcasted_iota(jnp.int32, (extent, position.shape[1]), 0)
    return hats(nodes.astype(jnp.float32), position)


def column_hats(position, extent):
    nodes = 2 * lax.broadcasted_iota(jnp.int32, (extent // 2, position.shape[1]), 0)
    nodes = nodes.astype(jnp.float32)
    return jnp.concatenate([hats(nodes, position), hats(nodes + 1.0, position)], axis=0)


def kicks(guest_rows, guest_cols, guest_charge, rows, cols, col_ref, inv_ref, row_ref, spec_ref, back_ref):
    extent = col_ref.shape[1]
    half = extent // 2
    eighth = extent // 4
    weight_rows = row_hats(guest_rows, extent).astype(jnp.bfloat16)
    weight_cols = (guest_charge * column_hats(guest_cols, extent)).astype(jnp.bfloat16)
    grid = dot_nt(weight_cols, weight_rows).astype(jnp.bfloat16)
    for turn in range(2):
        at = turn * eighth
        re_rows = slice(at, at + eighth)
        im_rows = slice(half + at, half + at + eighth)
        table = jnp.concatenate([col_ref[re_rows, :], col_ref[im_rows, :]], axis=0)
        even = dot_nn(table[:, :half], grid[:half])
        odd = dot_nn(table[:, half:], grid[half:])
        plus, minus = even + odd, even - odd
        real = jnp.concatenate([plus[:eighth], minus[:eighth]], axis=0)
        imag = jnp.concatenate([plus[eighth:], minus[eighth:]], axis=0)
        blocks = [
            (real[:, q * eighth : (q + 1) * eighth], imag[:, q * eighth : (q + 1) * eighth])
            for q in range(4)
        ]
        here = slice(turn * half, (turn + 1) * half)
        backs = []
        for j, pair in enumerate(spread(blocks)):
            forward = dot_nt(joined(pair), row_ref[j])
            kernel_re = spec_ref[j, here, :eighth]
            kernel_im = spec_ref[j, here, eighth:]
            forward_re, forward_im = forward[:, :eighth], forward[:, eighth:]
            scaled = joined(
                (
                    forward_re * kernel_re - forward_im * kernel_im,
                    forward_re * kernel_im + forward_im * kernel_re,
                )
            )
            back = dot_nn(scaled, row_ref[j])
            backs.append((back[:, :eighth], back[:, eighth:]))
        for q, pair in enumerate(gathered(backs)):
            lanes = slice(q * eighth, (q + 1) * eighth)
            for value, where in zip(pair, (re_rows, im_rows)):
                low, high = value[:eighth], value[eighth:]
                back_ref[0, where, lanes] = (low + high).astype(jnp.bfloat16)
                back_ref[1, where, lanes] = (low - high).astype(jnp.bfloat16)
    even = dot_nn(inv_ref[:half, :], back_ref[0])
    odd = dot_nn(inv_ref[half:, :], back_ref[1])
    zero_lane = jnp.zeros((extent, 1), jnp.float32)
    zero_row = jnp.zeros((1, extent), jnp.float32)
    potential = jnp.concatenate([even, odd], axis=0)
    before = jnp.concatenate([zero_lane, potential[:, :-1]], axis=1)
    after = jnp.concatenate([potential[:, 1:], zero_lane], axis=1)
    along_rows = (before - after).astype(jnp.bfloat16)
    before = jnp.concatenate([zero_row, odd[:-1]], axis=0)
    after = jnp.concatenate([even[1:], zero_row], axis=0)
    along_cols = jnp.concatenate([before - odd, even - after], axis=0).astype(jnp.bfloat16)
    weight_rows = row_hats(rows, extent).astype(jnp.bfloat16)
    weight_cols = column_hats(cols, extent).astype(jnp.bfloat16).astype(jnp.float32)
    kick_rows = jnp.sum(dot_nn(along_rows, weight_rows) * weight_cols, axis=0, keepdims=True)
    kick_cols = jnp.sum(dot_nn(along_cols, weight_rows) * weight_cols, axis=0, keepdims=True)
    return kick_rows, kick_cols


def advance(position, moment, extent):
    return jnp.clip(position + DRIFT_STEP * moment, 1.0, extent - 2.0 - 1.0 / 64.0)


def store_moved(out_ref, moment_out_ref, rows, cols, charge, kick_rows, kick_cols, moment_rows, moment_cols, extent):
    moment_rows = moment_rows + kick_rows
    moment_cols = moment_cols + kick_cols
    moment_out_ref[0:1, :] = moment_rows
    moment_out_ref[1:2, :] = moment_cols
    out_ref[0:1, :] = advance(rows, moment_rows, extent)
    out_ref[1:2, :] = advance(cols, moment_cols, extent)
    out_ref[2:3, :] = charge
    out_ref[3:4, :] = charge


def first_kernel(shards, cells_ref, offsets_ref, charges_ref, momenta_ref, *rest):
    received = rest[:-8]
    col_ref, inv_ref, row_ref, spec_ref, out_ref, moment_out_ref, moment_ref, back_ref = rest[-8:]
    extent = col_ref.shape[1]
    shard = lax.axis_index("tr")
    role = lax.rem(shard, 2)
    own, guest = 1 - role, role
    count = momenta_ref.shape[-1]
    if count == moment_ref.shape[-1]:
        moment_ref[...] = momenta_ref[own]
    else:
        for step, piece in enumerate((momenta_ref, *received)):
            source = lax.rem(shard + shards - step, shards)
            begin = pl.multiple_of(source * count, count)
            moment_ref[:, pl.ds(begin, count)] = piece[own]
    own_place = cells_ref[own].astype(jnp.float32) + offsets_ref[own]
    guest_place = cells_ref[guest].astype(jnp.float32) + offsets_ref[guest]
    rows, cols = own_place[0:1], own_place[1:2]
    kick_rows, kick_cols = kicks(
        guest_place[0:1], guest_place[1:2], charges_ref[guest], rows, cols,
        col_ref, inv_ref, row_ref, spec_ref, back_ref,
    )
    store_moved(
        out_ref, moment_out_ref, rows, cols, charges_ref[own], kick_rows, kick_cols,
        moment_ref[0:1, :], moment_ref[1:2, :], extent,
    )


def middle_kernel(guest_ref, own_ref, moment_ref, col_ref, inv_ref, row_ref, spec_ref,
                  out_ref, moment_out_ref, back_ref):
    extent = col_ref.shape[1]
    rows, cols = own_ref[0:1, :], own_ref[1:2, :]
    kick_rows, kick_cols = kicks(
        guest_ref[0:1, :], guest_ref[1:2, :], guest_ref[2:3, :], rows, cols,
        col_ref, inv_ref, row_ref, spec_ref, back_ref,
    )
    store_moved(
        out_ref, moment_out_ref, rows, cols, own_ref[2:3, :], kick_rows, kick_cols,
        moment_ref[0:1, :], moment_ref[1:2, :], extent,
    )


def last_kernel(guest_ref, own_ref, moment_ref, col_ref, inv_ref, row_ref, spec_ref,
                mine_ref, theirs_ref, total_ref, back_ref):
    count = mine_ref.shape[1]
    kick_rows, kick_cols = kicks(
        guest_ref[0:1, :], guest_ref[1:2, :], guest_ref[2:3, :], own_ref[0:1, :], own_ref[1:2, :],
        col_ref, inv_ref, row_ref, spec_ref, back_ref,
    )
    total_ref[0:1, :] = moment_ref[0:1, :] + kick_rows
    total_ref[1:2, :] = moment_ref[1:2, :] + kick_cols
    if count == total_ref.shape[1]:
        mine_ref[...] = total_ref[...]
        theirs_ref[...] = total_ref[...]
        return
    shard = lax.axis_index("tr")
    partner = shard + 1 - 2 * lax.rem(shard, 2)
    mine_ref[...] = total_ref[:, pl.ds(pl.multiple_of(shard * count, count), count)]
    theirs_ref[...] = total_ref[:, pl.ds(pl.multiple_of(partner * count, count), count)]


def per_device(cells, offsets, charges, momenta, green):
    shards = lax.axis_size("tr")
    slices = lax.axis_size("cuts")
    period = green.shape[0]
    extent = period // 2
    particles = cells.shape[-1]
    own_count = momenta.shape[-1]

    def slot(cut, part):
        return (cut % slices) * shards + part

    def exchange(value, steps):
        pairs = []
        for cut in range(slices):
            for part in range(shards):
                turn = steps if part % 2 == 1 else -steps
                pairs.append((slot(cut, part), slot(cut + turn, part ^ 1)))
        return lax.ppermute(value, ("cuts", "tr"), pairs)

    momenta = momenta[:, 0]
    received = [
        lax.ppermute(momenta, "tr", [(i, (i + step) % shards) for i in range(shards)])
        for step in range(1, shards)
    ]
    aligned = own_count % 128 == 0
    shard = lax.axis_index("tr")
    if not aligned:
        momenta = jnp.concatenate([*received[::-1], momenta], axis=2)
        momenta = jnp.roll(momenta, (shard + 1) * own_count, axis=2)
        received = []

    packed, begins = factors(extent)
    tables = pl.pallas_call(
        functools.partial(setup_kernel, begins),
        out_shape=(
            jax.ShapeDtypeStruct((extent, extent), jnp.bfloat16),
            jax.ShapeDtypeStruct((extent, extent), jnp.bfloat16),
            jax.ShapeDtypeStruct((8, extent // 2, extent // 2), jnp.bfloat16),
            jax.ShapeDtypeStruct((8, extent, extent // 2), jnp.float32),
        ),
        in_specs=[HBM, HBM],
        out_specs=(VMEM,) * 4,
        scratch_shapes=[
            pltpu.VMEM((period, extent), jnp.bfloat16),
            pltpu.VMEM((period, period), jnp.float32),
            pltpu.VMEM(packed.shape, jnp.float32),
            pltpu.SemaphoreType.DMA((9,)),
        ],
        compiler_params=pltpu.CompilerParams(vmem_limit_bytes=SETUP_VMEM),
        cost_estimate=pl.CostEstimate(
            flops=3 * period**3, bytes_accessed=8 * period**2, transcendentals=0
        ),
        name="setup",
    )(green, jnp.asarray(packed))

    place = jax.ShapeDtypeStruct((4, particles), jnp.float32)
    moments = jax.ShapeDtypeStruct((2, particles), jnp.float32)
    piece = jax.ShapeDtypeStruct((2, own_count), jnp.float32)
    back = pltpu.VMEM((2, extent, extent), jnp.bfloat16)
    whole = pltpu.VMEM((2, particles), jnp.float32)

    def section(kernel, name, outs, scratch, arguments):
        return pl.pallas_call(
            kernel,
            out_shape=outs,
            in_specs=[VMEM] * (len(arguments) + 4),
            out_specs=(VMEM,) * len(outs),
            scratch_shapes=scratch,
            compiler_params=pltpu.CompilerParams(vmem_limit_bytes=SECTION_VMEM),
            cost_estimate=pl.CostEstimate(
                flops=3 * period**3, bytes_accessed=8 * period**2, transcendentals=0
            ),
            name=name,
        )(*arguments, *tables)

    own, moment = section(
        functools.partial(first_kernel, shards), "first", (place, moments), [whole, back],
        (cells[:, 0], offsets[:, 0], charges, momenta, *received),
    )
    for number in range(1, SECTIONS - 1):
        guest = exchange(own, 2 * number)
        own, moment = section(middle_kernel, "middle", (place, moments), [back], (guest, own, moment))
    guest = exchange(own, 2 * (SECTIONS - 1))
    role = shard % 2
    outs = (piece, piece) if aligned else (moments, moments)
    mine, theirs = section(last_kernel, "last", outs, [whole, back], (guest, own, moment))
    if not aligned:
        theirs = lax.dynamic_slice_in_dim(mine, (shard + 1 - 2 * role) * own_count, own_count, axis=1)
        mine = lax.dynamic_slice_in_dim(mine, shard * own_count, own_count, axis=1)
    received = exchange(theirs, 0)
    first = jnp.where(role == 1, mine, received)
    second = jnp.where(role == 1, received, mine)
    return jnp.stack([first, second])[:, None]


def solution(mesh):
    return jax.shard_map(
        per_device,
        mesh=mesh,
        in_specs=(
            P(None, "cuts", None, None),
            P(None, "cuts", None, None),
            P(None, "cuts", None),
            P(None, "cuts", None, "tr"),
            P(),
        ),
        out_specs=P(None, "cuts", None, "tr"),
        check_vma=False,
    )
```

time: 83 us -> 63.7 us (0.77)
  local copies, waits for them, and re-layouts: 22.4 us -> 5.5 us
  other arithmetic: 2.12 us -> 0.6 us
    unnamed x47 -> x16, local copies, waits for them, and re-layouts: 21.5 us -> 5.5 us
  transfers between devices with their start and end apart: 7 -> 7, of which waited for: 4 -> 4; matrix products, arithmetic and copies ran while one was open for 2% -> 0% of each run, Pallas kernels for 6% -> 16%
where the time goes in v2:
time: 63.7 us; the launch traced here: 63.4 us
  Pallas kernels  31.5 us (49%)
  starting transfers between devices  13.2 us (21%)
  waiting for transfers between devices  12.5 us (20%)
  local copies, waits for them, and re-layouts  5.5 us (9%)
    pallas_call x4, Pallas kernels, section(): pl.pallas_call(kernel, out_shape=outs, in_specs=[VMEM] * (len(arguments)...  21.6 us
    ppermute x4, waiting for transfers between devices, exchange(): return lax.ppermute(value, ('cuts', 'tr'), pairs)  12.5 us
    pallas_call x1, Pallas kernels, per_device(): pl.pallas_call(functools.partial(setup_kernel, begins), out_shape=(jax.Sh...  9.89 us
    ppermute x3, starting transfers between devices, per_device(): lax.ppermute(momenta, 'tr', [(i, (i + step) % shards) for i in range(shar...  7.05 us
    ppermute x4, starting transfers between devices, exchange(): return lax.ppermute(value, ('cuts', 'tr'), pairs)  6.14 us
    unnamed x16, local copies, waits for them, and re-layouts  5.5 us
  transfers between devices with their start and end apart: 7, of which 4 were waited for; matrix products, arithmetic and copies ran while one was open for 0% of the time, Pallas kernels for 16%

profile of v2, /device:TPU:0, one launch (start us, length us, event | category | flops | bytes accessed | tf_op | source)
XLA Modules:
  0.0 63.4 jit_solution(14338963122601132821)
XLA Ops:
  0.0 0.0 copy-start
  0.0 0.0 copy-start.1
  0.0 0.0 copy-start.2
  0.0 3.1 %collective-permute-start = (f32[2,2,256]{2,1,0:T(2,128)}, f32[2,2,256]{2,1,0:T(2,128)S(1)}, u32[]{:S(2)}, u32[]{:S(2)}) collective-permute-start(f32[2,2,256]{2,1,0:T(2,128)} %bitcast.13), channel_id=1, source_target_pairs={{0,1},{1,2},{2,3},{3,0},{4,5},{5,6},{6,7},{7,4},{8,9},{9,10},{10,1... | collective-permute-start | bytes 12296 | tf_op jit(solution)/shard_map/ppermute | solution.py:373
  3.1 2.6 %collective-permute-start.1 = (f32[2,2,256]{2,1,0:T(2,128)}, f32[2,2,256]{2,1,0:T(2,128)S(1)}, u32[]{:S(2)}, u32[]{:S(2)}) collective-permute-start(f32[2,2,256]{2,1,0:T(2,128)} %bitcast.14), channel_id=1, source_target_pairs={{0,2},{1,3},{2,0},{3,1},{4,6},{5,7},{6,4},{7,5},{8,10},{9,11},{10,... | collective-permute-start | bytes 12296 | tf_op jit(solution)/shard_map/ppermute | solution.py:373
  5.7 1.3 %collective-permute-start.2 = (f32[2,2,256]{2,1,0:T(2,128)}, f32[2,2,256]{2,1,0:T(2,128)S(1)}, u32[]{:S(2)}, u32[]{:S(2)}) collective-permute-start(f32[2,2,256]{2,1,0:T(2,128)} %bitcast.15), channel_id=1, source_target_pairs={{0,3},{1,0},{2,1},{3,2},{4,7},{5,4},{6,5},{7,6},{8,11},{9,8},{10,9... | collective-permute-start | bytes 12296 | tf_op jit(solution)/shard_map/ppermute | solution.py:373
  7.1 9.9 %setup.1 = (bf16[512,512]{1,0:T(8,128)(2,1)}, bf16[512,512]{1,0:T(8,128)(2,1)}, bf16[8,256,256]{2,1,0:T(8,128)(2,1)}, f32[8,512,256]{2,1,0:T(8,128)}) custom-call(f32[1024,1024]{1,0:T(8,128)} %green_ref.1, f32[312,512]{1,0:T(8,128)} %constant.20.clone.factor_ref), custom_call_target="tpu_custom_call" | custom-call | flops 3221225472 | bytes 8388608 | tf_op jit(solution)/shard_map/setup/pallas_call | solution.py:384
  17.0 0.0 collective-permute-done.rest_0_
  17.0 0.0 collective-permute-done.1.rest_1_
  17.0 0.0 collective-permute-done.2.rest_2_
  17.0 0.0 copy-done
  17.0 0.0 copy-done.1
  17.0 0.0 copy-done.2
  17.0 0.0 copy-done.3
  17.0 0.0 copy-start.4
  17.0 2.2 %copy-done.4 = f32[8,512,256]{2,1,0:T(8,128)S(1)} copy-done((f32[8,512,256]{2,1,0:T(8,128)S(1)}, f32[8,512,256]{2,1,0:T(8,128)}, u32[]{:S(2)}) %copy-start.4) | copy-done | bytes 4194328
  19.2 1.2 %copy-done.5 = bf16[8,256,256]{2,1,0:T(8,128)(2,1)S(1)} copy-done((bf16[8,256,256]{2,1,0:T(8,128)(2,1)S(1)}, bf16[8,256,256]{2,1,0:T(8,128)(2,1)}, u32[]{:S(2)}) %copy-start.5) | copy-done | bytes 1048600
  20.5 1.0 %copy-done.6 = bf16[512,512]{1,0:T(8,128)(2,1)S(1)} copy-done((bf16[512,512]{1,0:T(8,128)(2,1)S(1)}, bf16[512,512]{1,0:T(8,128)(2,1)}, u32[]{:S(2)}) %copy-start.6) | copy-done | bytes 524312
  21.5 1.0 %copy-done.7 = bf16[512,512]{1,0:T(8,128)(2,1)S(1)} copy-done((bf16[512,512]{1,0:T(8,128)(2,1)S(1)}, bf16[512,512]{1,0:T(8,128)(2,1)}, u32[]{:S(2)}) %copy-start.7) | copy-done | bytes 524312
  22.5 5.3 %first.1 = (f32[4,1024]{1,0:T(4,128)S(1)}, f32[2,1024]{1,0:T(2,128)S(1)}) custom-call(s32[2,2,1024]{2,1,0:T(2,128)S(1)} %bitcast.11, f32[2,2,1024]{2,1,0:T(2,128)S(1)} %bitcast.12, f32[2,1,1024]{2,1,0:T(1,128)S(1)} %copy-done.2, f32[2,2,256]{2,1,0:T(2,128)S(1)} %bitcast.16, f32[2,2,256]{2,1,0:T(2,128)S(1)} %collective-permute-done.rest_0_, ...), custom_call_target="tpu_custom_call" | custom-call | flops 3221225472 | bytes 8388608 | tf_op jit(solution)/shard_map/first/pallas_call | solution.py:414
  27.9 2.6 %collective-permute-start.3 = (f32[4,1024]{1,0:T(4,128)S(1)}, f32[4,1024]{1,0:T(4,128)S(1)}, u32[]{:S(2)}, u32[]{:S(2)}) collective-permute-start(f32[4,1024]{1,0:T(4,128)S(1)} %get-tuple-element.21.own_ref), channel_id=1, source_target_pairs={{0,25},{1,8},{2,27},{3,10},{4,29},{5,12},{6,31},{7,14},{8,1},{9,16... | collective-permute-start | bytes 49160 | tf_op jit(solution)/shard_map/ppermute | solution.py:369
  30.5 3.0 %collective-permute-done.3.guest_ref = f32[4,1024]{1,0:T(4,128)S(1)} collective-permute-done((f32[4,1024]{1,0:T(4,128)S(1)}, f32[4,1024]{1,0:T(4,128)S(1)}, u32[]{:S(2)}, u32[]{:S(2)}) %collective-permute-start.3) | collective-permute-done | bytes 16416 | tf_op jit(solution)/shard_map/ppermute | solution.py:369
  33.5 5.5 %middle.2 = (f32[4,1024]{1,0:T(4,128)S(1)}, f32[2,1024]{1,0:T(2,128)S(1)}) custom-call(f32[4,1024]{1,0:T(4,128)S(1)} %collective-permute-done.3.guest_ref, f32[4,1024]{1,0:T(4,128)S(1)} %get-tuple-element.21.own_ref, f32[2,1024]{1,0:T(2,128)S(1)} %get-tuple-element.22.moment_ref, bf16[512,512]{1,0:T(8,128)(2,1)S(1)} %copy-done.6, ...), custom_call_target="tpu_custom_call" | custom-call | flops 3221225472 | bytes 8388608 | tf_op jit(solution)/shard_map/middle/pallas_call | solution.py:414
  39.0 0.8 %collective-permute-start.4 = (f32[4,1024]{1,0:T(4,128)S(1)}, f32[4,1024]{1,0:T(4,128)S(1)}, u32[]{:S(2)}, u32[]{:S(2)}) collective-permute-start(f32[4,1024]{1,0:T(4,128)S(1)} %get-tuple-element.23.own_ref), channel_id=1, source_target_pairs={{0,17},{1,16},{2,19},{3,18},{4,21},{5,20},{6,23},{7,22},{8,25},{9,... | collective-permute-start | bytes 49160 | tf_op jit(solution)/shard_map/ppermute | solution.py:369
  39.8 3.9 %collective-permute-done.4.guest_ref = f32[4,1024]{1,0:T(4,128)S(1)} collective-permute-done((f32[4,1024]{1,0:T(4,128)S(1)}, f32[4,1024]{1,0:T(4,128)S(1)}, u32[]{:S(2)}, u32[]{:S(2)}) %collective-permute-start.4) | collective-permute-done | bytes 16416 | tf_op jit(solution)/shard_map/ppermute | solution.py:369
  43.7 5.3 %middle.3 = (f32[4,1024]{1,0:T(4,128)S(1)}, f32[2,1024]{1,0:T(2,128)S(1)}) custom-call(f32[4,1024]{1,0:T(4,128)S(1)} %collective-permute-done.4.guest_ref, f32[4,1024]{1,0:T(4,128)S(1)} %get-tuple-element.23.own_ref, f32[2,1024]{1,0:T(2,128)S(1)} %get-tuple-element.24.moment_ref, bf16[512,512]{1,0:T(8,128)(2,1)S(1)} %copy-done.6, ...), custom_call_target="tpu_custom_call" | custom-call | flops 3221225472 | bytes 8388608 | tf_op jit(solution)/shard_map/middle/pallas_call | solution.py:414
  49.0 1.7 %collective-permute-start.5 = (f32[4,1024]{1,0:T(4,128)S(1)}, f32[4,1024]{1,0:T(4,128)S(1)}, u32[]{:S(2)}, u32[]{:S(2)}) collective-permute-start(f32[4,1024]{1,0:T(4,128)S(1)} %get-tuple-element.25.own_ref), channel_id=1, source_target_pairs={{0,9},{1,24},{2,11},{3,26},{4,13},{5,28},{6,15},{7,30},{8,17},{9,0... | collective-permute-start | bytes 49160 | tf_op jit(solution)/shard_map/ppermute | solution.py:369
  50.6 3.0 %collective-permute-done.5.guest_ref = f32[4,1024]{1,0:T(4,128)S(1)} collective-permute-done((f32[4,1024]{1,0:T(4,128)S(1)}, f32[4,1024]{1,0:T(4,128)S(1)}, u32[]{:S(2)}, u32[]{:S(2)}) %collective-permute-start.5) | collective-permute-done | bytes 16416 | tf_op jit(solution)/shard_map/ppermute | solution.py:369
  53.7 5.5 %last.1 = (f32[2,256]{1,0:T(2,128)S(1)}, f32[2,256]{1,0:T(2,128)S(1)}) custom-call(f32[4,1024]{1,0:T(4,128)S(1)} %collective-permute-done.5.guest_ref, f32[4,1024]{1,0:T(4,128)S(1)} %get-tuple-element.25.own_ref, f32[2,1024]{1,0:T(2,128)S(1)} %get-tuple-element.26.moment_ref, bf16[512,512]{1,0:T(8,128)(2,1)S(1)} %copy-done.6, ...), custom_call_target="tpu_custom_call" | custom-call | flops 3221225472 | bytes 8388608 | tf_op jit(solution)/shard_map/last/pallas_call | solution.py:414
  59.2 1.0 %collective-permute-start.6 = (f32[2,256]{1,0:T(2,128)S(1)}, f32[2,256]{1,0:T(2,128)S(1)}, u32[]{:S(2)}, u32[]{:S(2)}) collective-permute-start(f32[2,256]{1,0:T(2,128)S(1)} %get-tuple-element.28), channel_id=1, source_target_pairs={{0,1},{1,0},{2,3},{3,2},{4,5},{5,4},{6,7},{7,6},{8,9},{9,8},{10,11... | collective-permute-start | bytes 6152 | tf_op jit(solution)/shard_map/ppermute | solution.py:369
  60.2 2.6 %collective-permute-done.6 = f32[2,256]{1,0:T(2,128)S(1)} collective-permute-done((f32[2,256]{1,0:T(2,128)S(1)}, f32[2,256]{1,0:T(2,128)S(1)}, u32[]{:S(2)}, u32[]{:S(2)}) %collective-permute-start.6) | collective-permute-done | bytes 2080 | tf_op jit(solution)/shard_map/ppermute | solution.py:369
  62.8 0.6 maximum_bitcast_fusion
  (5 shorter events, 0.0 us)
Async XLA Ops:
  0.0 17.0 %copy-start = (s32[2,1,2,1024]{3,2,1,0:T(2,128)S(1)}, s32[2,1,2,1024]{3,2,1,0:T(2,128)}, u32[]{:S(2)}) copy-start(s32[2,1,2,1024]{3,2,1,0:T(2,128)} %param.6) | copy-start | bytes 49156
  0.0 17.0 %copy-start.1 = (f32[2,1,2,1024]{3,2,1,0:T(2,128)S(1)}, f32[2,1,2,1024]{3,2,1,0:T(2,128)}, u32[]{:S(2)}) copy-start(f32[2,1,2,1024]{3,2,1,0:T(2,128)} %param.7) | copy-start | bytes 49156
  0.0 17.0 %copy-start.2 = (f32[2,1,1024]{2,1,0:T(1,128)S(1)}, f32[2,1,1024]{2,1,0:T(1,128)}, u32[]{:S(2)}) copy-start(f32[2,1,1024]{2,1,0:T(1,128)} %charges_ref.1) | copy-start | bytes 24580
  0.0 17.0 %copy-start.3 = (f32[2,1,2,256]{3,2,1,0:T(2,128)S(1)}, f32[2,1,2,256]{3,2,1,0:T(2,128)}, u32[]{:S(2)}) copy-start(f32[2,1,2,256]{3,2,1,0:T(2,128)} %param.9) | copy-start | bytes 12292
  0.0 17.0 %collective-permute-start = (f32[2,2,256]{2,1,0:T(2,128)}, f32[2,2,256]{2,1,0:T(2,128)S(1)}, u32[]{:S(2)}, u32[]{:S(2)}) collective-permute-start(f32[2,2,256]{2,1,0:T(2,128)} %bitcast.13), channel_id=1, source_target_pairs={{0,1},{1,2},{2,3},{3,0},{4,5},{5,6},{6,7},{7,4},{8,9},{9,10},{10,1... | collective-permute-start | bytes 12296 | tf_op jit(solution)/shard_map/ppermute | solution.py:373
  3.1 13.9 %collective-permute-start.1 = (f32[2,2,256]{2,1,0:T(2,128)}, f32[2,2,256]{2,1,0:T(2,128)S(1)}, u32[]{:S(2)}, u32[]{:S(2)}) collective-permute-start(f32[2,2,256]{2,1,0:T(2,128)} %bitcast.14), channel_id=1, source_target_pairs={{0,2},{1,3},{2,0},{3,1},{4,6},{5,7},{6,4},{7,5},{8,10},{9,11},{10,... | collective-permute-start | bytes 12296 | tf_op jit(solution)/shard_map/ppermute | solution.py:373
  5.7 11.3 %collective-permute-start.2 = (f32[2,2,256]{2,1,0:T(2,128)}, f32[2,2,256]{2,1,0:T(2,128)S(1)}, u32[]{:S(2)}, u32[]{:S(2)}) collective-permute-start(f32[2,2,256]{2,1,0:T(2,128)} %bitcast.15), channel_id=1, source_target_pairs={{0,3},{1,0},{2,1},{3,2},{4,7},{5,4},{6,5},{7,6},{8,11},{9,8},{10,9... | collective-permute-start | bytes 12296 | tf_op jit(solution)/shard_map/ppermute | solution.py:373
  17.0 2.2 %copy-start.4 = (f32[8,512,256]{2,1,0:T(8,128)S(1)}, f32[8,512,256]{2,1,0:T(8,128)}, u32[]{:S(2)}) copy-start(f32[8,512,256]{2,1,0:T(8,128)} %get-tuple-element.20.rest_6_.spec_ref) | copy-start | bytes 12582916
  19.2 1.2 %copy-start.5 = (bf16[8,256,256]{2,1,0:T(8,128)(2,1)S(1)}, bf16[8,256,256]{2,1,0:T(8,128)(2,1)}, u32[]{:S(2)}) copy-start(bf16[8,256,256]{2,1,0:T(8,128)(2,1)} %get-tuple-element.19.rest_5_.row_ref) | copy-start | bytes 3145732
  20.5 1.0 %copy-start.6 = (bf16[512,512]{1,0:T(8,128)(2,1)S(1)}, bf16[512,512]{1,0:T(8,128)(2,1)}, u32[]{:S(2)}) copy-start(bf16[512,512]{1,0:T(8,128)(2,1)} %get-tuple-element.17.rest_3_.col_ref) | copy-start | bytes 1572868
  21.5 1.0 %copy-start.7 = (bf16[512,512]{1,0:T(8,128)(2,1)S(1)}, bf16[512,512]{1,0:T(8,128)(2,1)}, u32[]{:S(2)}) copy-start(bf16[512,512]{1,0:T(8,128)(2,1)} %get-tuple-element.18.rest_4_.inv_ref) | copy-start | bytes 1572868
  27.9 5.6 %collective-permute-start.3 = (f32[4,1024]{1,0:T(4,128)S(1)}, f32[4,1024]{1,0:T(4,128)S(1)}, u32[]{:S(2)}, u32[]{:S(2)}) collective-permute-start(f32[4,1024]{1,0:T(4,128)S(1)} %get-tuple-element.21.own_ref), channel_id=1, source_target_pairs={{0,25},{1,8},{2,27},{3,10},{4,29},{5,12},{6,31},{7,14},{8,1},{9,16... | collective-permute-start | bytes 49160 | tf_op jit(solution)/shard_map/ppermute | solution.py:369
  39.0 4.7 %collective-permute-start.4 = (f32[4,1024]{1,0:T(4,128)S(1)}, f32[4,1024]{1,0:T(4,128)S(1)}, u32[]{:S(2)}, u32[]{:S(2)}) collective-permute-start(f32[4,1024]{1,0:T(4,128)S(1)} %get-tuple-element.23.own_ref), channel_id=1, source_target_pairs={{0,17},{1,16},{2,19},{3,18},{4,21},{5,20},{6,23},{7,22},{8,25},{9,... | collective-permute-start | bytes 49160 | tf_op jit(solution)/shard_map/ppermute | solution.py:369
  49.0 4.7 %collective-permute-start.5 = (f32[4,1024]{1,0:T(4,128)S(1)}, f32[4,1024]{1,0:T(4,128)S(1)}, u32[]{:S(2)}, u32[]{:S(2)}) collective-permute-start(f32[4,1024]{1,0:T(4,128)S(1)} %get-tuple-element.25.own_ref), channel_id=1, source_target_pairs={{0,9},{1,24},{2,11},{3,26},{4,13},{5,28},{6,15},{7,30},{8,17},{9,0... | collective-permute-start | bytes 49160 | tf_op jit(solution)/shard_map/ppermute | solution.py:369
  59.2 3.6 %collective-permute-start.6 = (f32[2,256]{1,0:T(2,128)S(1)}, f32[2,256]{1,0:T(2,128)S(1)}, u32[]{:S(2)}, u32[]{:S(2)}) collective-permute-start(f32[2,256]{1,0:T(2,128)S(1)} %get-tuple-element.28), channel_id=1, source_target_pairs={{0,1},{1,0},{2,3},{3,2},{4,5},{5,4},{6,7},{7,6},{8,9},{9,8},{10,11... | collective-permute-start | bytes 6152 | tf_op jit(solution)/shard_map/ppermute | solution.py:369

commit v3 on v2

--- a/solution.py
+++ b/solution.py
@@ -12,7 +12,7 @@
 SECTIONS = 4
 DRIFT_STEP = 0.5
 GROUP = 16
-SETUP_VMEM = 54 * 1024 * 1024
+SETUP_VMEM = 50 * 1024 * 1024
 SECTION_VMEM = 28 * 1024 * 1024
 HALF_ROOT = math.sqrt(0.5)
 
@@ -195,30 +195,42 @@
         odd = four_points(eighths([less(parts[q], parts[q + 4]) for q in range(4)], -1), -1)
         sums = [pair for couple in zip(even, odd) for pair in couple]
         for j in range(8):
-            spec_ref[j, begin : begin + half, :] = dot_nt(joined(sums[j]), row_ref[j]) * scale
-
-
-def hats(nodes, position):
-    return jnp.maximum(1.0 - jnp.abs(nodes - position), 0.0)
-
-
-def row_hats(position, extent):
-    nodes = lax.broadcasted_iota(jnp.int32, (extent, position.shape[1]), 0)
-    return hats(nodes.astype(jnp.float32), position)
-
-
-def column_hats(position, extent):
-    nodes = 2 * lax.broadcasted_iota(jnp.int32, (extent // 2, position.shape[1]), 0)
-    nodes = nodes.astype(jnp.float32)
-    return jnp.concatenate([hats(nodes, position), hats(nodes + 1.0, position)], axis=0)
+            spec = dot_nt(joined(sums[j]), row_ref[j]) * scale
+            spec_ref[j, begin : begin + half, :] = spec.astype(jnp.bfloat16)
+
+
+def codes(cells, half):
+    return jnp.where(cells < half, cells, half - 1.0 - cells).astype(jnp.bfloat16)
+
+
+def row_nodes(extent, width):
+    return lax.broadcasted_iota(jnp.int32, (extent, width), 0).astype(jnp.float32)
+
+
+def column_nodes(extent, width):
+    nodes = (2 * lax.broadcasted_iota(jnp.int32, (extent // 2, width), 0)).astype(jnp.float32)
+    return jnp.concatenate([nodes, nodes + 1.0], axis=0)
+
+
+def hats(nodes, position, weight=1.0):
+    half = nodes.shape[0] // 2
+    cell = jnp.floor(position)
+    part = position - cell
+    here = codes(nodes, half)
+    low = (weight * (1.0 - part)).astype(jnp.bfloat16)
+    high = (weight * part).astype(jnp.bfloat16)
+    zero = jnp.zeros_like(here)
+    above = jnp.where(here == codes(cell + 1.0, half), high, zero)
+    return jnp.where(here == codes(cell, half), low, above)
 
 
 def kicks(guest_rows, guest_cols, guest_charge, rows, cols, col_ref, inv_ref, row_ref, spec_ref, back_ref):
     extent = col_ref.shape[1]
     half = extent // 2
     eighth = extent // 4
-    weight_rows = row_hats(guest_rows, extent).astype(jnp.bfloat16)
-    weight_cols = (guest_charge * column_hats(guest_cols, extent)).astype(jnp.bfloat16)
+    particles = rows.shape[1]
+    weight_rows = hats(row_nodes(extent, particles), guest_rows)
+    weight_cols = hats(column_nodes(extent, particles), guest_cols, guest_charge)
     grid = dot_nt(weight_cols, weight_rows).astype(jnp.bfloat16)
     for turn in range(2):
         at = turn * eighth
@@ -228,8 +240,8 @@
         even = dot_nn(table[:, :half], grid[:half])
         odd = dot_nn(table[:, half:], grid[half:])
         plus, minus = even + odd, even - odd
-        real = jnp.concatenate([plus[:eighth], minus[:eighth]], axis=0)
-        imag = jnp.concatenate([plus[eighth:], minus[eighth:]], axis=0)
+        real = jnp.concatenate([plus[:eighth], minus[:eighth]], axis=0).astype(jnp.bfloat16)
+        imag = jnp.concatenate([plus[eighth:], minus[eighth:]], axis=0).astype(jnp.bfloat16)
         blocks = [
             (real[:, q * eighth : (q + 1) * eighth], imag[:, q * eighth : (q + 1) * eighth])
             for q in range(4)
@@ -237,7 +249,7 @@
         here = slice(turn * half, (turn + 1) * half)
         backs = []
         for j, pair in enumerate(spread(blocks)):
-            forward = dot_nt(joined(pair), row_ref[j])
+            forward = dot_nt(joined(pair), row_ref[j]).astype(jnp.bfloat16)
             kernel_re = spec_ref[j, here, :eighth]
             kernel_im = spec_ref[j, here, eighth:]
             forward_re, forward_im = forward[:, :eighth], forward[:, eighth:]
@@ -247,14 +259,14 @@
                     forward_re * kernel_im + forward_im * kernel_re,
                 )
             )
-            back = dot_nn(scaled, row_ref[j])
+            back = dot_nn(scaled, row_ref[j]).astype(jnp.bfloat16)
             backs.append((back[:, :eighth], back[:, eighth:]))
         for q, pair in enumerate(gathered(backs)):
             lanes = slice(q * eighth, (q + 1) * eighth)
             for value, where in zip(pair, (re_rows, im_rows)):
                 low, high = value[:eighth], value[eighth:]
-                back_ref[0, where, lanes] = (low + high).astype(jnp.bfloat16)
-                back_ref[1, where, lanes] = (low - high).astype(jnp.bfloat16)
+                back_ref[0, where, lanes] = low + high
+                back_ref[1, where, lanes] = low - high
     even = dot_nn(inv_ref[:half, :], back_ref[0])
     odd = dot_nn(inv_ref[half:, :], back_ref[1])
     zero_lane = jnp.zeros((extent, 1), jnp.float32)
@@ -266,10 +278,19 @@
     before = jnp.concatenate([zero_row, odd[:-1]], axis=0)
     after = jnp.concatenate([even[1:], zero_row], axis=0)
     along_cols = jnp.concatenate([before - odd, even - after], axis=0).astype(jnp.bfloat16)
-    weight_rows = row_hats(rows, extent).astype(jnp.bfloat16)
-    weight_cols = column_hats(cols, extent).astype(jnp.bfloat16).astype(jnp.float32)
-    kick_rows = jnp.sum(dot_nn(along_rows, weight_rows) * weight_cols, axis=0, keepdims=True)
-    kick_cols = jnp.sum(dot_nn(along_cols, weight_rows) * weight_cols, axis=0, keepdims=True)
+    weight_rows = hats(row_nodes(extent, particles), rows)
+    weight_cols = hats(column_nodes(extent, particles), cols)
+
+    def sampled(field):
+        terms = dot_nn(field, weight_rows).astype(jnp.bfloat16) * weight_cols
+        count = extent
+        while count > 16:
+            count //= 2
+            terms = terms[:count] + terms[count:]
+        return jnp.sum(terms.astype(jnp.float32), axis=0, keepdims=True)
+
+    kick_rows = sampled(along_rows)
+    kick_cols = sampled(along_cols)
     return kick_rows, kick_cols
 
 
@@ -387,7 +408,7 @@
             jax.ShapeDtypeStruct((extent, extent), jnp.bfloat16),
             jax.ShapeDtypeStruct((extent, extent), jnp.bfloat16),
             jax.ShapeDtypeStruct((8, extent // 2, extent // 2), jnp.bfloat16),
-            jax.ShapeDtypeStruct((8, extent, extent // 2), jnp.float32),
+            jax.ShapeDtypeStruct((8, extent, extent // 2), jnp.bfloat16),
         ),
         in_specs=[HBM, HBM],
         out_specs=(VMEM,) * 4,

time: 63.7 us -> 57.6 us (0.904)
  Pallas kernels: 31.5 us -> 28.4 us
  local copies, waits for them, and re-layouts: 5.5 us -> 2.68 us
    unnamed x16 -> x12, local copies, waits for them, and re-layouts: 5.5 us -> 2.68 us
    pallas_call x4, Pallas kernels: 21.6 us -> 19.1 us  [section(): pl.pallas_call(kernel, out_shape=outs, in_specs=[VMEM] * (len(arguments)...]
    pallas_call x1, Pallas kernels: 9.89 us -> 9.25 us  [per_device(): pl.pallas_call(functools.partial(setup_kernel, begins), out_shape=(jax.Sh...]
where the time goes in v3:
time: 57.6 us; the launch traced here: 57.4 us
  Pallas kernels  28.4 us (49%)
  starting transfers between devices  13.2 us (23%)
  waiting for transfers between devices  12.6 us (22%)
  local copies, waits for them, and re-layouts  2.68 us (5%)
  other arithmetic  0.6 us (1%)
    pallas_call x4, Pallas kernels, section(): pl.pallas_call(kernel, out_shape=outs, in_specs=[VMEM] * (len(arguments)...  19.1 us
    ppermute x4, waiting for transfers between devices, exchange(): return lax.ppermute(value, ('cuts', 'tr'), pairs)  12.6 us
    pallas_call x1, Pallas kernels, per_device(): pl.pallas_call(functools.partial(setup_kernel, begins), out_shape=(jax.Sh...  9.25 us
    ppermute x3, starting transfers between devices, per_device(): lax.ppermute(momenta, 'tr', [(i, (i + step) % shards) for i in range(shar...  7.05 us
    ppermute x4, starting transfers between devices, exchange(): return lax.ppermute(value, ('cuts', 'tr'), pairs)  6.11 us
    unnamed x12, local copies, waits for them, and re-layouts  2.68 us
  transfers between devices with their start and end apart: 7, of which 4 were waited for; matrix products, arithmetic and copies ran while one was open for 0% of the time, Pallas kernels for 16%

profile of v3, /device:TPU:0, one launch (start us, length us, event | category | flops | bytes accessed | tf_op | source)
XLA Modules:
  0.0 57.4 jit_solution(10244296961044588929)
XLA Ops:
  0.0 0.0 copy-start
  0.0 0.0 copy-start.1
  0.0 0.0 copy-start.2
  0.0 0.0 copy-start.3
  0.0 3.1 %collective-permute-start = (f32[2,2,256]{2,1,0:T(2,128)}, f32[2,2,256]{2,1,0:T(2,128)S(1)}, u32[]{:S(2)}, u32[]{:S(2)}) collective-permute-start(f32[2,2,256]{2,1,0:T(2,128)} %bitcast.13), channel_id=1, source_target_pairs={{0,1},{1,2},{2,3},{3,0},{4,5},{5,6},{6,7},{7,4},{8,9},{9,10},{10,1... | collective-permute-start | bytes 12296 | tf_op jit(solution)/shard_map/ppermute | solution.py:394
  3.1 2.6 %collective-permute-start.1 = (f32[2,2,256]{2,1,0:T(2,128)}, f32[2,2,256]{2,1,0:T(2,128)S(1)}, u32[]{:S(2)}, u32[]{:S(2)}) collective-permute-start(f32[2,2,256]{2,1,0:T(2,128)} %bitcast.14), channel_id=1, source_target_pairs={{0,2},{1,3},{2,0},{3,1},{4,6},{5,7},{6,4},{7,5},{8,10},{9,11},{10,... | collective-permute-start | bytes 12296 | tf_op jit(solution)/shard_map/ppermute | solution.py:394
  5.7 1.3 %collective-permute-start.2 = (f32[2,2,256]{2,1,0:T(2,128)}, f32[2,2,256]{2,1,0:T(2,128)S(1)}, u32[]{:S(2)}, u32[]{:S(2)}) collective-permute-start(f32[2,2,256]{2,1,0:T(2,128)} %bitcast.15), channel_id=1, source_target_pairs={{0,3},{1,0},{2,1},{3,2},{4,7},{5,4},{6,5},{7,6},{8,11},{9,8},{10,9... | collective-permute-start | bytes 12296 | tf_op jit(solution)/shard_map/ppermute | solution.py:394
  7.1 0.0 copy-start.4
  7.1 1.1 %copy-done.4 = f32[312,512]{1,0:T(8,128)S(1)} copy-done((f32[312,512]{1,0:T(8,128)S(1)}, f32[312,512]{1,0:T(8,128)}, u32[]{:S(2)}) %copy-start.4) | copy-done | bytes 639000
  8.1 9.2 %setup.1 = (bf16[512,512]{1,0:T(8,128)(2,1)S(1)}, bf16[512,512]{1,0:T(8,128)(2,1)S(1)}, bf16[8,256,256]{2,1,0:T(8,128)(2,1)S(1)}, bf16[8,512,256]{2,1,0:T(8,128)(2,1)}) custom-call(f32[1024,1024]{1,0:T(8,128)} %green_ref.1, f32[312,512]{1,0:T(8,128)S(1)} %copy-done.4), custom_call_target="tpu_custom_call" | custom-call | flops 3221225472 | bytes 8388608 | tf_op jit(solution)/shard_map/setup/pallas_call | solution.py:405
  17.4 0.0 collective-permute-done.rest_0_
  17.4 0.0 collective-permute-done.1.rest_1_
  17.4 0.0 collective-permute-done.2.rest_2_
  17.4 0.0 copy-done
  17.4 0.0 copy-done.1
  17.5 0.0 copy-done.2
  17.5 0.0 copy-done.3
  17.5 0.0 copy-start.5
  17.5 1.6 %copy-done.5 = bf16[8,512,256]{2,1,0:T(8,128)(2,1)S(1)} copy-done((bf16[8,512,256]{2,1,0:T(8,128)(2,1)S(1)}, bf16[8,512,256]{2,1,0:T(8,128)(2,1)}, u32[]{:S(2)}) %copy-start.5) | copy-done | bytes 2097176
  19.1 4.7 %first.1 = (f32[4,1024]{1,0:T(4,128)S(1)}, f32[2,1024]{1,0:T(2,128)S(1)}) custom-call(s32[2,2,1024]{2,1,0:T(2,128)S(1)} %bitcast.11, f32[2,2,1024]{2,1,0:T(2,128)S(1)} %bitcast.12, f32[2,1,1024]{2,1,0:T(1,128)S(1)} %copy-done.2, f32[2,2,256]{2,1,0:T(2,128)S(1)} %bitcast.16, f32[2,2,256]{2,1,0:T(2,128)S(1)} %collective-permute-done.rest_0_, ...), custom_call_target="tpu_custom_call" | custom-call | flops 3221225472 | bytes 8388608 | tf_op jit(solution)/shard_map/first/pallas_call | solution.py:435
  23.8 2.6 %collective-permute-start.3 = (f32[4,1024]{1,0:T(4,128)S(1)}, f32[4,1024]{1,0:T(4,128)S(1)}, u32[]{:S(2)}, u32[]{:S(2)}) collective-permute-start(f32[4,1024]{1,0:T(4,128)S(1)} %get-tuple-element.21.own_ref), channel_id=1, source_target_pairs={{0,25},{1,8},{2,27},{3,10},{4,29},{5,12},{6,31},{7,14},{8,1},{9,16... | collective-permute-start | bytes 49160 | tf_op jit(solution)/shard_map/ppermute | solution.py:390
  26.4 3.0 %collective-permute-done.3.guest_ref = f32[4,1024]{1,0:T(4,128)S(1)} collective-permute-done((f32[4,1024]{1,0:T(4,128)S(1)}, f32[4,1024]{1,0:T(4,128)S(1)}, u32[]{:S(2)}, u32[]{:S(2)}) %collective-permute-start.3) | collective-permute-done | bytes 16416 | tf_op jit(solution)/shard_map/ppermute | solution.py:390
  29.4 4.9 %middle.2 = (f32[4,1024]{1,0:T(4,128)S(1)}, f32[2,1024]{1,0:T(2,128)S(1)}) custom-call(f32[4,1024]{1,0:T(4,128)S(1)} %collective-permute-done.3.guest_ref, f32[4,1024]{1,0:T(4,128)S(1)} %get-tuple-element.21.own_ref, f32[2,1024]{1,0:T(2,128)S(1)} %get-tuple-element.22.moment_ref, bf16[512,512]{1,0:T(8,128)(2,1)S(1)} %get-tuple-element.17.rest_3_.col_ref, ...), custom_call_target="tpu_custom_call" | custom-call | flops 3221225472 | bytes 8388608 | tf_op jit(solution)/shard_map/middle/pallas_call | solution.py:435
  34.3 0.8 %collective-permute-start.4 = (f32[4,1024]{1,0:T(4,128)S(1)}, f32[4,1024]{1,0:T(4,128)S(1)}, u32[]{:S(2)}, u32[]{:S(2)}) collective-permute-start(f32[4,1024]{1,0:T(4,128)S(1)} %get-tuple-element.23.own_ref), channel_id=1, source_target_pairs={{0,17},{1,16},{2,19},{3,18},{4,21},{5,20},{6,23},{7,22},{8,25},{9,... | collective-permute-start | bytes 49160 | tf_op jit(solution)/shard_map/ppermute | solution.py:390
  35.1 3.9 %collective-permute-done.4.guest_ref = f32[4,1024]{1,0:T(4,128)S(1)} collective-permute-done((f32[4,1024]{1,0:T(4,128)S(1)}, f32[4,1024]{1,0:T(4,128)S(1)}, u32[]{:S(2)}, u32[]{:S(2)}) %collective-permute-start.4) | collective-permute-done | bytes 16416 | tf_op jit(solution)/shard_map/ppermute | solution.py:390
  39.0 4.7 %middle.3 = (f32[4,1024]{1,0:T(4,128)S(1)}, f32[2,1024]{1,0:T(2,128)S(1)}) custom-call(f32[4,1024]{1,0:T(4,128)S(1)} %collective-permute-done.4.guest_ref, f32[4,1024]{1,0:T(4,128)S(1)} %get-tuple-element.23.own_ref, f32[2,1024]{1,0:T(2,128)S(1)} %get-tuple-element.24.moment_ref, bf16[512,512]{1,0:T(8,128)(2,1)S(1)} %get-tuple-element.17.rest_3_.col_ref, ...), custom_call_target="tpu_custom_call" | custom-call | flops 3221225472 | bytes 8388608 | tf_op jit(solution)/shard_map/middle/pallas_call | solution.py:435
  43.8 1.7 %collective-permute-start.5 = (f32[4,1024]{1,0:T(4,128)S(1)}, f32[4,1024]{1,0:T(4,128)S(1)}, u32[]{:S(2)}, u32[]{:S(2)}) collective-permute-start(f32[4,1024]{1,0:T(4,128)S(1)} %get-tuple-element.25.own_ref), channel_id=1, source_target_pairs={{0,9},{1,24},{2,11},{3,26},{4,13},{5,28},{6,15},{7,30},{8,17},{9,0... | collective-permute-start | bytes 49160 | tf_op jit(solution)/shard_map/ppermute | solution.py:390
  45.4 3.0 %collective-permute-done.5.guest_ref = f32[4,1024]{1,0:T(4,128)S(1)} collective-permute-done((f32[4,1024]{1,0:T(4,128)S(1)}, f32[4,1024]{1,0:T(4,128)S(1)}, u32[]{:S(2)}, u32[]{:S(2)}) %collective-permute-start.5) | collective-permute-done | bytes 16416 | tf_op jit(solution)/shard_map/ppermute | solution.py:390
  48.5 4.7 %last.1 = (f32[2,256]{1,0:T(2,128)S(1)}, f32[2,256]{1,0:T(2,128)S(1)}) custom-call(f32[4,1024]{1,0:T(4,128)S(1)} %collective-permute-done.5.guest_ref, f32[4,1024]{1,0:T(4,128)S(1)} %get-tuple-element.25.own_ref, f32[2,1024]{1,0:T(2,128)S(1)} %get-tuple-element.26.moment_ref, bf16[512,512]{1,0:T(8,128)(2,1)S(1)} %get-tuple-element.17.rest_3_.col_ref, ...), custom_call_target="tpu_custom_call" | custom-call | flops 3221225472 | bytes 8388608 | tf_op jit(solution)/shard_map/last/pallas_call | solution.py:435
  53.2 1.0 %collective-permute-start.6 = (f32[2,256]{1,0:T(2,128)S(1)}, f32[2,256]{1,0:T(2,128)S(1)}, u32[]{:S(2)}, u32[]{:S(2)}) collective-permute-start(f32[2,256]{1,0:T(2,128)S(1)} %get-tuple-element.28), channel_id=1, source_target_pairs={{0,1},{1,0},{2,3},{3,2},{4,5},{5,4},{6,7},{7,6},{8,9},{9,8},{10,11... | collective-permute-start | bytes 6152 | tf_op jit(solution)/shard_map/ppermute | solution.py:390
  54.2 2.6 %collective-permute-done.6 = f32[2,256]{1,0:T(2,128)S(1)} collective-permute-done((f32[2,256]{1,0:T(2,128)S(1)}, f32[2,256]{1,0:T(2,128)S(1)}, u32[]{:S(2)}, u32[]{:S(2)}) %collective-permute-start.6) | collective-permute-done | bytes 2080 | tf_op jit(solution)/shard_map/ppermute | solution.py:390
  56.8 0.6 %maximum_bitcast_fusion = f32[2,1,2,256]{3,2,1,0:T(2,128)} fusion(f32[1,2,256]{2,1,0:T(2,128)S(1)} %get-tuple-element.30, f32[1,2,256]{2,1,0:T(2,128)S(1)} %get-tuple-element.29), kind=kLoop, calls=%fused_computation | loop fusion | flops 1024 | bytes 8192 | tf_op jit(solution)/shard_map/broadcast_in_dim | solution.py:465
  (1 shorter events, 0.0 us)
Async XLA Ops:
  0.0 17.4 %copy-start = (s32[2,1,2,1024]{3,2,1,0:T(2,128)S(1)}, s32[2,1,2,1024]{3,2,1,0:T(2,128)}, u32[]{:S(2)}) copy-start(s32[2,1,2,1024]{3,2,1,0:T(2,128)} %param.6) | copy-start | bytes 49156
  0.0 17.4 %copy-start.1 = (f32[2,1,2,1024]{3,2,1,0:T(2,128)S(1)}, f32[2,1,2,1024]{3,2,1,0:T(2,128)}, u32[]{:S(2)}) copy-start(f32[2,1,2,1024]{3,2,1,0:T(2,128)} %param.7) | copy-start | bytes 49156
  0.0 17.5 %copy-start.2 = (f32[2,1,1024]{2,1,0:T(1,128)S(1)}, f32[2,1,1024]{2,1,0:T(1,128)}, u32[]{:S(2)}) copy-start(f32[2,1,1024]{2,1,0:T(1,128)} %charges_ref.1) | copy-start | bytes 24580
  0.0 17.5 %copy-start.3 = (f32[2,1,2,256]{3,2,1,0:T(2,128)S(1)}, f32[2,1,2,256]{3,2,1,0:T(2,128)}, u32[]{:S(2)}) copy-start(f32[2,1,2,256]{3,2,1,0:T(2,128)} %param.9) | copy-start | bytes 12292
  0.0 17.4 %collective-permute-start = (f32[2,2,256]{2,1,0:T(2,128)}, f32[2,2,256]{2,1,0:T(2,128)S(1)}, u32[]{:S(2)}, u32[]{:S(2)}) collective-permute-start(f32[2,2,256]{2,1,0:T(2,128)} %bitcast.13), channel_id=1, source_target_pairs={{0,1},{1,2},{2,3},{3,0},{4,5},{5,6},{6,7},{7,4},{8,9},{9,10},{10,1... | collective-permute-start | bytes 12296 | tf_op jit(solution)/shard_map/ppermute | solution.py:394
  3.1 14.3 %collective-permute-start.1 = (f32[2,2,256]{2,1,0:T(2,128)}, f32[2,2,256]{2,1,0:T(2,128)S(1)}, u32[]{:S(2)}, u32[]{:S(2)}) collective-permute-start(f32[2,2,256]{2,1,0:T(2,128)} %bitcast.14), channel_id=1, source_target_pairs={{0,2},{1,3},{2,0},{3,1},{4,6},{5,7},{6,4},{7,5},{8,10},{9,11},{10,... | collective-permute-start | bytes 12296 | tf_op jit(solution)/shard_map/ppermute | solution.py:394
  5.7 11.7 %collective-permute-start.2 = (f32[2,2,256]{2,1,0:T(2,128)}, f32[2,2,256]{2,1,0:T(2,128)S(1)}, u32[]{:S(2)}, u32[]{:S(2)}) collective-permute-start(f32[2,2,256]{2,1,0:T(2,128)} %bitcast.15), channel_id=1, source_target_pairs={{0,3},{1,0},{2,1},{3,2},{4,7},{5,4},{6,5},{7,6},{8,11},{9,8},{10,9... | collective-permute-start | bytes 12296 | tf_op jit(solution)/shard_map/ppermute | solution.py:394
  7.1 1.1 %copy-start.4 = (f32[312,512]{1,0:T(8,128)S(1)}, f32[312,512]{1,0:T(8,128)}, u32[]{:S(2)}) copy-start(f32[312,512]{1,0:T(8,128)} %constant.20.clone.factor_ref) | copy-start | bytes 1916932
  17.5 1.6 %copy-start.5 = (bf16[8,512,256]{2,1,0:T(8,128)(2,1)S(1)}, bf16[8,512,256]{2,1,0:T(8,128)(2,1)}, u32[]{:S(2)}) copy-start(bf16[8,512,256]{2,1,0:T(8,128)(2,1)} %get-tuple-element.20.rest_6_.spec_ref) | copy-start | bytes 6291460
  23.8 5.6 %collective-permute-start.3 = (f32[4,1024]{1,0:T(4,128)S(1)}, f32[4,1024]{1,0:T(4,128)S(1)}, u32[]{:S(2)}, u32[]{:S(2)}) collective-permute-start(f32[4,1024]{1,0:T(4,128)S(1)} %get-tuple-element.21.own_ref), channel_id=1, source_target_pairs={{0,25},{1,8},{2,27},{3,10},{4,29},{5,12},{6,31},{7,14},{8,1},{9,16... | collective-permute-start | bytes 49160 | tf_op jit(solution)/shard_map/ppermute | solution.py:390
  34.3 4.7 %collective-permute-start.4 = (f32[4,1024]{1,0:T(4,128)S(1)}, f32[4,1024]{1,0:T(4,128)S(1)}, u32[]{:S(2)}, u32[]{:S(2)}) collective-permute-start(f32[4,1024]{1,0:T(4,128)S(1)} %get-tuple-element.23.own_ref), channel_id=1, source_target_pairs={{0,17},{1,16},{2,19},{3,18},{4,21},{5,20},{6,23},{7,22},{8,25},{9,... | collective-permute-start | bytes 49160 | tf_op jit(solution)/shard_map/ppermute | solution.py:390
  43.8 4.7 %collective-permute-start.5 = (f32[4,1024]{1,0:T(4,128)S(1)}, f32[4,1024]{1,0:T(4,128)S(1)}, u32[]{:S(2)}, u32[]{:S(2)}) collective-permute-start(f32[4,1024]{1,0:T(4,128)S(1)} %get-tuple-element.25.own_ref), channel_id=1, source_target_pairs={{0,9},{1,24},{2,11},{3,26},{4,13},{5,28},{6,15},{7,30},{8,17},{9,0... | collective-permute-start | bytes 49160 | tf_op jit(solution)/shard_map/ppermute | solution.py:390
  53.2 3.7 %collective-permute-start.6 = (f32[2,256]{1,0:T(2,128)S(1)}, f32[2,256]{1,0:T(2,128)S(1)}, u32[]{:S(2)}, u32[]{:S(2)}) collective-permute-start(f32[2,256]{1,0:T(2,128)S(1)} %get-tuple-element.28), channel_id=1, source_target_pairs={{0,1},{1,0},{2,3},{3,2},{4,5},{5,4},{6,7},{7,6},{8,9},{9,8},{10,11... | collective-permute-start | bytes 6152 | tf_op jit(solution)/shard_map/ppermute | solution.py:390

commit v4 on v3

v4 whole, which is shorter than its diff:
```python
import functools
import math

import jax
import jax.numpy as jnp
import numpy as np
from jax import lax
from jax.experimental import pallas as pl
from jax.experimental.pallas import tpu as pltpu
from jax.sharding import PartitionSpec as P

SECTIONS = 4
DRIFT_STEP = 0.5
GROUP = 16
SETUP_VMEM = 32 * 1024 * 1024
WEIGHTS_VMEM = 16 * 1024 * 1024
SECTION_VMEM = 28 * 1024 * 1024
HALF_ROOT = math.sqrt(0.5)

VMEM = pl.BlockSpec(memory_space=pltpu.VMEM)
HBM = pl.BlockSpec(memory_space=pltpu.MemorySpace.HBM)


def dot_nn(left, right):
    return jnp.dot(left, right, preferred_element_type=jnp.float32)


def dot_nt(left, right):
    return lax.dot_general(
        left, right, (((1,), (1,)), ((), ())), preferred_element_type=jnp.float32
    )


def phases(products, period):
    theta = 2.0 * np.pi / period * (products % period)
    return np.cos(theta).astype(np.float32), np.sin(theta).astype(np.float32)


def factors(extent):
    half = extent // 2
    eighth = extent // 4
    period = 2 * extent
    cells = np.arange(extent, dtype=np.int64)
    split = np.concatenate([cells[0::2], cells[1::2]])
    odd = 2 * cells[:half] + 1
    fine = np.arange(GROUP, dtype=np.int64)
    coarse = np.arange(half // GROUP, dtype=np.int64)
    few = np.arange(eighth // GROUP, dtype=np.int64)
    starts = (8 * fine[None, :] + np.arange(8)[:, None]).reshape(-1)
    pieces = []
    pieces += phases(2 * GROUP * coarse[:, None] * split[None, :], 2 * period)
    pieces += phases((2 * fine + 1)[:, None] * split[None, :], 2 * period)
    for rows in (2 * GROUP * coarse, 2 * fine, 2 * fine + 1):
        pieces.append(np.concatenate(phases(rows[:, None] * odd[None, :], 2 * period), axis=1))
    for rows in (8 * GROUP * few, starts):
        both = np.concatenate(phases(rows[:, None] * cells[None, :eighth], period), axis=1)
        pieces.append(np.concatenate([both, both], axis=1))
    begins = np.cumsum([0] + [piece.shape[0] for piece in pieces])
    total = -(-int(begins[-1]) // 8) * 8
    packed = np.zeros((total, extent), np.float32)
    packed[: begins[-1]] = np.concatenate(pieces, axis=0)
    return packed, [int(begin) for begin in begins[:-1]]


def turned(cos_a, sin_a, cos_b, sin_b):
    return cos_a * cos_b - sin_a * sin_b, sin_a * cos_b + cos_a * sin_b


def added(left, right):
    return left[0] + right[0], left[1] + right[1]


def less(left, right):
    return left[0] - right[0], left[1] - right[1]


def times_i(value):
    return -value[1], value[0]


def four_points(values, turn):
    even, even_less = added(values[0], values[2]), less(values[0], values[2])
    odd, odd_less = added(values[1], values[3]), less(values[1], values[3])
    side = times_i(odd_less)
    up, down = added(even_less, side), less(even_less, side)
    if turn < 0:
        up, down = down, up
    return added(even, odd), up, less(even, odd), down


def eighths(values, turn):
    first, second, third, fourth = values
    plus = ((second[0] - turn * second[1]) * HALF_ROOT, (second[1] + turn * second[0]) * HALF_ROOT)
    third = times_i(third)
    if turn < 0:
        third = (-third[0], -third[1])
    minus = (
        (-fourth[0] - turn * fourth[1]) * HALF_ROOT,
        (turn * fourth[0] - fourth[1]) * HALF_ROOT,
    )
    return first, plus, third, minus


def joined(pair):
    return jnp.concatenate([pair[0].astype(jnp.bfloat16), pair[1].astype(jnp.bfloat16)], axis=1)


def spread(values):
    even = four_points(values, -1)
    odd = four_points(eighths(values, -1), -1)
    return [pair for couple in zip(even, odd) for pair in couple]


def gathered(values):
    even = four_points(values[0::2], 1)
    odd = eighths(four_points(values[1::2], 1), 1)
    return [added(left, right) for left, right in zip(even, odd)]


def setup_kernel(begins, green_ref, factor_ref, cells_ref, offsets_ref,
                 col_ref, inv_ref, row_ref, spec_ref, even_ref, slope_ref, split_ref,
                 green_vm, factor_vm, cells_vm, offsets_vm, sem):
    extent = col_ref.shape[1]
    half = extent // 2
    eighth = extent // 4
    period = 2 * extent
    small = [
        pltpu.make_async_copy(source, target, sem.at[8 + number])
        for number, (source, target) in enumerate(
            [(cells_ref, cells_vm), (offsets_ref, offsets_vm), (factor_ref, factor_vm)]
        )
    ]
    for copy in small:
        copy.start()
    copies = [
        pltpu.make_async_copy(
            green_ref.at[:, pl.ds(b * eighth, eighth)], green_vm.at[b], sem.at[b]
        )
        for b in range(8)
    ]
    for copy in copies:
        copy.start()
    own = 1 - lax.rem(lax.axis_index("tr"), 2)
    small[0].wait()
    small[1].wait()
    place = cells_vm[own].astype(jnp.float32) + offsets_vm[own]
    store_weights(place, even_ref, slope_ref, split_ref)
    small[2].wait()

    for i in range(half // GROUP):
        rows = i * GROUP
        cosine, sine = turned(
            factor_vm[begins[0] + i : begins[0] + i + 1, :],
            factor_vm[begins[1] + i : begins[1] + i + 1, :],
            factor_vm[begins[2] : begins[2] + GROUP, :],
            factor_vm[begins[3] : begins[3] + GROUP, :],
        )
        col_ref[rows : rows + GROUP, :] = cosine.astype(jnp.bfloat16)
        col_ref[half + rows : half + rows + GROUP, :] = (-sine).astype(jnp.bfloat16)
        coarse = factor_vm[begins[4] + i : begins[4] + i + 1, :]
        for turn in range(2):
            fine = factor_vm[begins[5 + turn] : begins[5 + turn] + GROUP, :]
            cosine, sine = turned(coarse[:, :half], coarse[:, half:], fine[:, :half], fine[:, half:])
            at = turn * half + rows
            inv_ref[at : at + GROUP, :half] = cosine.astype(jnp.bfloat16)
            inv_ref[at : at + GROUP, half:] = (-sine).astype(jnp.bfloat16)
    for j in range(8):
        fine = factor_vm[begins[8] + j * GROUP : begins[8] + (j + 1) * GROUP, :]
        for i in range(eighth // GROUP):
            coarse = factor_vm[begins[7] + i : begins[7] + i + 1, :]
            cosine, sine = turned(
                coarse[:, :eighth], coarse[:, eighth:half], fine[:, :eighth], fine[:, eighth:half]
            )
            upper = i * GROUP
            lower = eighth + i * GROUP
            row_ref[j, upper : upper + GROUP, :eighth] = cosine.astype(jnp.bfloat16)
            row_ref[j, upper : upper + GROUP, eighth:] = sine.astype(jnp.bfloat16)
            row_ref[j, lower : lower + GROUP, :eighth] = (-sine).astype(jnp.bfloat16)
            row_ref[j, lower : lower + GROUP, eighth:] = cosine.astype(jnp.bfloat16)

    scale = 1.0 / (period * period)
    parity = lax.broadcasted_iota(jnp.int32, (half, eighth), 0) % 2
    sign = jnp.where(parity == 0, 1.0, -1.0)
    parts = [[], []]
    for b in range(4):
        copies[2 * b].wait()
        copies[2 * b + 1].wait()
        blocks = [
            joined([green_vm[2 * b + q, pl.ds(begin, half, stride=2), :] for q in range(2)])
            for begin in (0, 1, extent, extent + 1)
        ]
        for turn in range(2):
            table = frequency_rows(col_ref, turn)
            near = both_halves(table, blocks[0], blocks[1])
            far = both_halves(table, blocks[2], blocks[3])
            for q in range(2):
                cut = slice(q * eighth, (q + 1) * eighth)
                parts[turn].append(
                    (
                        near[0][:, cut] - sign * far[1][:, cut],
                        near[1][:, cut] + sign * far[0][:, cut],
                    )
                )
    for turn in range(2):
        part = parts[turn]
        even = four_points([added(part[q], part[q + 4]) for q in range(4)], -1)
        odd = four_points(eighths([less(part[q], part[q + 4]) for q in range(4)], -1), -1)
        sums = [pair for couple in zip(even, odd) for pair in couple]
        for j in range(8):
            spec = dot_nt(joined(sums[j]), row_ref[j]) * scale
            spec_ref[j, turn * half : (turn + 1) * half, :] = spec.astype(jnp.bfloat16)


def frequency_rows(col_ref, turn):
    half = col_ref.shape[0] // 2
    eighth = half // 2
    at = turn * eighth
    return jnp.concatenate(
        [col_ref[at : at + eighth, :], col_ref[half + at : half + at + eighth, :]], axis=0
    )


def both_halves(table, even_rows, odd_rows):
    half = table.shape[1] // 2
    eighth = half // 2
    even = dot_nn(table[:, :half], even_rows)
    odd = dot_nn(table[:, half:], odd_rows)
    plus, minus = even + odd, even - odd
    return (
        jnp.concatenate([plus[:eighth], minus[:eighth]], axis=0),
        jnp.concatenate([plus[eighth:], minus[eighth:]], axis=0),
    )


def codes(cells, half):
    return jnp.where(cells < half, cells, half - 1.0 - cells)


def chosen(extent, split, pairs):
    half = extent // 2
    width = pairs[0][0].shape[1]

    def raised(row):
        return jnp.broadcast_to(row, (GROUP, width)).astype(jnp.bfloat16)

    cells = [raised(codes(cell, half)) for cell, _ in pairs]
    weights = [raised(weight) for _, weight in pairs]
    count = lax.broadcasted_iota(jnp.int32, (GROUP, width), 0)
    blocks = []
    for begin in range(0, extent, GROUP):
        if split:
            nodes = 2 * (begin % half) + begin // half + 2 * count
        else:
            nodes = begin + count
        here = codes(nodes.astype(jnp.float32), half).astype(jnp.bfloat16)
        result = jnp.zeros_like(here)
        for cell, weight in zip(reversed(cells), reversed(weights)):
            result = jnp.where(here == cell, weight, result)
        blocks.append(result)
    return jnp.concatenate(blocks, axis=0)


def parted(position):
    cell = jnp.floor(position)
    return cell, position - cell


def hats(extent, split, position, weight=1.0):
    cell, part = parted(position)
    return chosen(extent, split, [(cell, weight * (1.0 - part)), (cell + 1.0, weight * part)])


def slopes(extent, position):
    cell, part = parted(position)
    return chosen(
        extent,
        False,
        [(cell - 1.0, 1.0 - part), (cell, part), (cell + 1.0, part - 1.0), (cell + 2.0, -part)],
    )


def store_weights(place, even_ref, slope_ref, split_ref):
    extent = even_ref.shape[0]
    even_ref[...] = hats(extent, False, place[1:2])
    slope_ref[...] = slopes(extent, place[1:2])
    split_ref[...] = hats(extent, True, place[0:1])


def weights_kernel(own_ref, even_ref, slope_ref, split_ref):
    store_weights(own_ref[0:2, :], even_ref, slope_ref, split_ref)


def kicks(guest, charge, even_ref, slope_ref, split_ref, col_ref, inv_ref, row_ref, spec_ref, back_ref):
    extent = col_ref.shape[1]
    half = extent // 2
    eighth = extent // 4
    weights_second = hats(extent, False, guest[1:2])
    weights_first = hats(extent, True, guest[0:1], charge)
    grid = dot_nt(weights_first, weights_second).astype(jnp.bfloat16)
    spreads = []
    for turn in range(2):
        real, imag = both_halves(frequency_rows(col_ref, turn), grid[:half], grid[half:])
        real, imag = real.astype(jnp.bfloat16), imag.astype(jnp.bfloat16)
        blocks = [
            (real[:, q * eighth : (q + 1) * eighth], imag[:, q * eighth : (q + 1) * eighth])
            for q in range(4)
        ]
        spreads.append(spread(blocks))
    for turn in range(2):
        here = slice(turn * half, (turn + 1) * half)
        backs = []
        for j, pair in enumerate(spreads[turn]):
            forward = dot_nt(joined(pair), row_ref[j]).astype(jnp.bfloat16)
            kernel_re = spec_ref[j, here, :eighth]
            kernel_im = spec_ref[j, here, eighth:]
            forward_re, forward_im = forward[:, :eighth], forward[:, eighth:]
            scaled = joined(
                (
                    forward_re * kernel_re - forward_im * kernel_im,
                    forward_re * kernel_im + forward_im * kernel_re,
                )
            )
            back = dot_nn(scaled, row_ref[j]).astype(jnp.bfloat16)
            backs.append((back[:, :eighth], back[:, eighth:]))
        for q, pair in enumerate(gathered(backs)):
            lanes = slice(q * eighth, (q + 1) * eighth)
            for part, value in enumerate(pair):
                where = slice(part * half + turn * eighth, part * half + (turn + 1) * eighth)
                low, high = value[:eighth], value[eighth:]
                back_ref[0, where, lanes] = low + high
                back_ref[1, where, lanes] = low - high
    even = dot_nn(inv_ref[:half, :], back_ref[0])
    odd = dot_nn(inv_ref[half:, :], back_ref[1])
    zero_row = jnp.zeros((1, extent), jnp.float32)
    before = jnp.concatenate([zero_row, odd[:-1]], axis=0)
    after = jnp.concatenate([even[1:], zero_row], axis=0)
    field = jnp.concatenate([before - odd, even - after], axis=0).astype(jnp.bfloat16)
    potential = jnp.concatenate([even, odd], axis=0).astype(jnp.bfloat16)

    def sampled(values, weights_ref):
        terms = dot_nn(values, weights_ref[...]).astype(jnp.bfloat16) * split_ref[...]
        count = extent
        while count > 16:
            count //= 2
            terms = terms[:count] + terms[count:]
        return jnp.sum(terms.astype(jnp.float32), axis=0, keepdims=True)

    return sampled(field, even_ref), sampled(potential, slope_ref)


def advance(position, moment, extent):
    return jnp.clip(position + DRIFT_STEP * moment, 1.0, extent - 2.0 - 1.0 / 64.0)


def store_moved(out_ref, moment_out_ref, place, charge, kick, moment, extent):
    for dim in range(2):
        line = slice(dim, dim + 1)
        total = moment[line] + kick[dim]
        moment_out_ref[line, :] = total
        out_ref[line, :] = advance(place[line], total, extent)
    out_ref[2:3, :] = charge
    out_ref[3:4, :] = charge


def first_kernel(shards, cells_ref, offsets_ref, charges_ref, momenta_ref, *rest):
    received = rest[:-11]
    common = rest[-11:-4]
    out_ref, moment_out_ref, moment_ref, back_ref = rest[-4:]
    shard = lax.axis_index("tr")
    role = lax.rem(shard, 2)
    own, guest = 1 - role, role
    count = momenta_ref.shape[-1]
    if count == moment_ref.shape[-1]:
        moment_ref[...] = momenta_ref[own]
    else:
        for step, piece in enumerate((momenta_ref, *received)):
            source = lax.rem(shard + shards - step, shards)
            begin = pl.multiple_of(source * count, count)
            moment_ref[:, pl.ds(begin, count)] = piece[own]
    own_place = cells_ref[own].astype(jnp.float32) + offsets_ref[own]
    guest_place = cells_ref[guest].astype(jnp.float32) + offsets_ref[guest]
    kick = kicks(guest_place, charges_ref[guest], *common, back_ref)
    extent = common[0].shape[0]
    store_moved(out_ref, moment_out_ref, own_place, charges_ref[own], kick, moment_ref[...], extent)


def middle_kernel(guest_ref, own_ref, moment_ref, *rest):
    common = rest[:7]
    out_ref, moment_out_ref, back_ref = rest[7:]
    kick = kicks(guest_ref[0:2, :], guest_ref[2:3, :], *common, back_ref)
    own, extent = own_ref[...], common[0].shape[0]
    store_moved(out_ref, moment_out_ref, own[0:2], own[2:3], kick, moment_ref[...], extent)


def last_kernel(guest_ref, moment_ref, *rest):
    common = rest[:7]
    mine_ref, theirs_ref, total_ref, back_ref = rest[7:]
    count = mine_ref.shape[1]
    kick = kicks(guest_ref[0:2, :], guest_ref[2:3, :], *common, back_ref)
    total_ref[0:1, :] = moment_ref[0:1, :] + kick[0]
    total_ref[1:2, :] = moment_ref[1:2, :] + kick[1]
    if count == total_ref.shape[1]:
        mine_ref[...] = total_ref[...]
        theirs_ref[...] = total_ref[...]
        return
    shard = lax.axis_index("tr")
    partner = shard + 1 - 2 * lax.rem(shard, 2)
    mine_ref[...] = total_ref[:, pl.ds(pl.multiple_of(shard * count, count), count)]
    theirs_ref[...] = total_ref[:, pl.ds(pl.multiple_of(partner * count, count), count)]


def per_device(cells, offsets, charges, momenta, green):
    shards = lax.axis_size("tr")
    slices = lax.axis_size("cuts")
    period = green.shape[0]
    extent = period // 2
    particles = cells.shape[-1]
    own_count = momenta.shape[-1]

    def slot(cut, part):
        return (cut % slices) * shards + part

    def exchange(value, steps):
        pairs = []
        for cut in range(slices):
            for part in range(shards):
                turn = steps if part % 2 == 1 else -steps
                pairs.append((slot(cut, part), slot(cut + turn, part ^ 1)))
        return lax.ppermute(value, ("cuts", "tr"), pairs)

    momenta = momenta[:, 0]
    received = [
        lax.ppermute(momenta, "tr", [(i, (i + step) % shards) for i in range(shards)])
        for step in range(1, shards)
    ]
    aligned = own_count % 128 == 0
    shard = lax.axis_index("tr")
    if not aligned:
        momenta = jnp.concatenate([*received[::-1], momenta], axis=2)
        momenta = jnp.roll(momenta, (shard + 1) * own_count, axis=2)
        received = []

    packed, begins = factors(extent)
    weight = jax.ShapeDtypeStruct((extent, particles), jnp.bfloat16)
    *tables, even, slope, split = pl.pallas_call(
        functools.partial(setup_kernel, begins),
        out_shape=(
            jax.ShapeDtypeStruct((extent, extent), jnp.bfloat16),
            jax.ShapeDtypeStruct((extent, extent), jnp.bfloat16),
            jax.ShapeDtypeStruct((8, extent // 2, extent // 2), jnp.bfloat16),
            jax.ShapeDtypeStruct((8, extent, extent // 2), jnp.bfloat16),
            weight, weight, weight,
        ),
        in_specs=[HBM] * 4,
        out_specs=(VMEM,) * 7,
        scratch_shapes=[
            pltpu.VMEM((8, period, extent // 4), jnp.float32),
            pltpu.VMEM(packed.shape, jnp.float32),
            pltpu.VMEM((2, 2, particles), jnp.int32),
            pltpu.VMEM((2, 2, particles), jnp.float32),
            pltpu.SemaphoreType.DMA((11,)),
        ],
        compiler_params=pltpu.CompilerParams(vmem_limit_bytes=SETUP_VMEM),
        cost_estimate=pl.CostEstimate(
            flops=2 * period**3, bytes_accessed=8 * period**2, transcendentals=0
        ),
        name="setup",
    )(*[
        pltpu.with_memory_space_constraint(value, pltpu.MemorySpace.HBM)
        for value in (green, jnp.asarray(packed), cells[:, 0], offsets[:, 0])
    ])

    place = jax.ShapeDtypeStruct((4, particles), jnp.float32)
    moments = jax.ShapeDtypeStruct((2, particles), jnp.float32)
    piece = jax.ShapeDtypeStruct((2, own_count), jnp.float32)
    back = pltpu.VMEM((2, extent, extent), jnp.bfloat16)
    whole = pltpu.VMEM((2, particles), jnp.float32)

    def weights(own):
        return pl.pallas_call(
            weights_kernel,
            out_shape=(weight,) * 3,
            in_specs=[VMEM],
            out_specs=(VMEM,) * 3,
            compiler_params=pltpu.CompilerParams(vmem_limit_bytes=WEIGHTS_VMEM),
            cost_estimate=pl.CostEstimate(
                flops=period**3 // 2, bytes_accessed=6 * period**2, transcendentals=0
            ),
            name="weights",
        )(own)

    def section(kernel, name, outs, scratch, arguments):
        return pl.pallas_call(
            kernel,
            out_shape=outs,
            in_specs=[VMEM] * (len(arguments) + 4),
            out_specs=(VMEM,) * len(outs),
            scratch_shapes=scratch,
            compiler_params=pltpu.CompilerParams(vmem_limit_bytes=SECTION_VMEM),
            cost_estimate=pl.CostEstimate(
                flops=3 * period**3, bytes_accessed=8 * period**2, transcendentals=0
            ),
            name=name,
        )(*arguments, *tables)

    own, moment = section(
        functools.partial(first_kernel, shards), "first", (place, moments), [whole, back],
        (cells[:, 0], offsets[:, 0], charges, momenta, *received, even, slope, split),
    )
    for number in range(1, SECTIONS - 1):
        guest = exchange(own, 2 * number)
        own, moment = section(
            middle_kernel, "middle", (place, moments), [back], (guest, own, moment, *weights(own))
        )
    guest = exchange(own, 2 * (SECTIONS - 1))
    role = shard % 2
    outs = (piece, piece) if aligned else (moments, moments)
    mine, theirs = section(
        last_kernel, "last", outs, [whole, back], (guest, moment, *weights(own))
    )
    if not aligned:
        theirs = lax.dynamic_slice_in_dim(mine, (shard + 1 - 2 * role) * own_count, own_count, axis=1)
        mine = lax.dynamic_slice_in_dim(mine, shard * own_count, own_count, axis=1)
    received = exchange(theirs, 0)
    first = jnp.where(role == 1, mine, received)
    second = jnp.where(role == 1, received, mine)
    return jnp.stack([first, second])[:, None]


def solution(mesh):
    return jax.shard_map(
        per_device,
        mesh=mesh,
        in_specs=(
            P(None, "cuts", None, None),
            P(None, "cuts", None, None),
            P(None, "cuts", None),
            P(None, "cuts", None, "tr"),
            P(),
        ),
        out_specs=P(None, "cuts", None, "tr"),
        check_vma=False,
    )
```

time: 57.6 us -> 50.5 us (0.88)
  local copies, waits for them, and re-layouts: 2.68 us -> 0.01 us
  waiting for transfers between devices: 12.6 us -> 10.2 us
  Pallas kernels: 28.4 us -> 26.4 us
    pallas_call x1, Pallas kernels: 9.25 us -> 5.28 us  [per_device(): pl.pallas_call(functools.partial(setup_kernel, begins), out_shape=(jax.Sh...]
    unnamed x12 -> x8, local copies, waits for them, and re-layouts: 2.68 us -> 0.01 us
    pallas_call x0 -> x3, Pallas kernels: none -> 2.4 us  [weights(): pl.pallas_call(weights_kernel, out_shape=(weight,) * 3, in_specs=[VMEM],...]
    ppermute x4, waiting for transfers between devices: 12.6 us -> 10.2 us  [exchange(): return lax.ppermute(value, ('cuts', 'tr'), pairs)]
  transfers between devices with their start and end apart: 7 -> 7, of which waited for: 4 -> 4; matrix products, arithmetic and copies ran while one was open for 0% -> 0% of each run, Pallas kernels for 16% -> 15%
where the time goes in v4:
time: 50.5 us; the launch traced here: 50.4 us
  Pallas kernels  26.4 us (52%)
  starting transfers between devices  13.1 us (26%)
  waiting for transfers between devices  10.2 us (20%)
  other arithmetic  0.6 us (1%)
    pallas_call x4, Pallas kernels, section(): pl.pallas_call(kernel, out_shape=outs, in_specs=[VMEM] * (len(arguments)...  18.7 us
    ppermute x4, waiting for transfers between devices, exchange(): return lax.ppermute(value, ('cuts', 'tr'), pairs)  10.2 us
    ppermute x3, starting transfers between devices, per_device(): lax.ppermute(momenta, 'tr', [(i, (i + step) % shards) for i in range(shar...  7.05 us
    ppermute x4, starting transfers between devices, exchange(): return lax.ppermute(value, ('cuts', 'tr'), pairs)  6.06 us
    pallas_call x1, Pallas kernels, per_device(): pl.pallas_call(functools.partial(setup_kernel, begins), out_shape=(jax.Sh...  5.28 us
    pallas_call x3, Pallas kernels, weights(): pl.pallas_call(weights_kernel, out_shape=(weight,) * 3, in_specs=[VMEM],...  2.4 us
  transfers between devices with their start and end apart: 7, of which 4 were waited for; matrix products, arithmetic and copies ran while one was open for 0% of the time, Pallas kernels for 15%

profile of v4, /device:TPU:0, one launch (start us, length us, event | category | flops | bytes accessed | tf_op | source)
XLA Modules:
  0.0 50.4 jit_solution(11290004572016575950)
XLA Ops:
  0.0 0.0 copy-start.3
  0.0 0.0 copy-start
  0.0 0.0 copy-start.1
  0.0 0.0 copy-start.2
  0.0 3.1 %collective-permute-start = (f32[2,2,256]{2,1,0:T(2,128)}, f32[2,2,256]{2,1,0:T(2,128)S(1)}, u32[]{:S(2)}, u32[]{:S(2)}) collective-permute-start(f32[2,2,256]{2,1,0:T(2,128)} %bitcast.15), channel_id=1, source_target_pairs={{0,1},{1,2},{2,3},{3,0},{4,5},{5,6},{6,7},{7,4},{8,9},{9,10},{10,1... | collective-permute-start | bytes 12296 | tf_op jit(solution)/shard_map/ppermute | solution.py:433
  3.1 2.6 %collective-permute-start.1 = (f32[2,2,256]{2,1,0:T(2,128)}, f32[2,2,256]{2,1,0:T(2,128)S(1)}, u32[]{:S(2)}, u32[]{:S(2)}) collective-permute-start(f32[2,2,256]{2,1,0:T(2,128)} %bitcast.16), channel_id=1, source_target_pairs={{0,2},{1,3},{2,0},{3,1},{4,6},{5,7},{6,4},{7,5},{8,10},{9,11},{10,... | collective-permute-start | bytes 12296 | tf_op jit(solution)/shard_map/ppermute | solution.py:433
  5.7 1.3 %collective-permute-start.2 = (f32[2,2,256]{2,1,0:T(2,128)}, f32[2,2,256]{2,1,0:T(2,128)S(1)}, u32[]{:S(2)}, u32[]{:S(2)}) collective-permute-start(f32[2,2,256]{2,1,0:T(2,128)} %bitcast.17), channel_id=1, source_target_pairs={{0,3},{1,0},{2,1},{3,2},{4,7},{5,4},{6,5},{7,6},{8,11},{9,8},{10,9... | collective-permute-start | bytes 12296 | tf_op jit(solution)/shard_map/ppermute | solution.py:433
  7.1 5.3 %setup.1 = (bf16[512,512]{1,0:T(8,128)(2,1)S(1)}, bf16[512,512]{1,0:T(8,128)(2,1)S(1)}, bf16[8,256,256]{2,1,0:T(8,128)(2,1)S(1)}, bf16[8,512,256]{2,1,0:T(8,128)...) custom-call(f32[1024,1024]{1,0:T(8,128)} %green_ref.1, ...), custom_call_target="tpu_custom_call" | custom-call | flops 2147483648 | bytes 8388608 | tf_op jit(solution)/shard_map/setup/pallas_call | solution.py:445
  12.4 0.0 collective-permute-done.rest_0_
  12.4 0.0 collective-permute-done.1.rest_1_
  12.4 0.0 collective-permute-done.2.rest_2_
  12.4 0.0 copy-done.3
  12.4 0.0 copy-done
  12.4 0.0 copy-done.1
  12.4 0.0 copy-done.2
  12.4 4.6 %first.1 = (f32[4,1024]{1,0:T(4,128)S(1)}, f32[2,1024]{1,0:T(2,128)S(1)}) custom-call(s32[2,2,1024]{2,1,0:T(2,128)S(1)} %bitcast.12, f32[2,2,1024]{2,1,0:T(2,128)S(1)} %bitcast.14, f32[2,1,1024]{2,1,0:T(1,128)S(1)} %copy-done.2, f32[2,2,256]{2,1,0:T(2,128)S(1)} %bitcast.18, f32[2,2,256]{2,1,0:T(2,128)S(1)} %collective-permute-done.rest_0_, ...), custom_call_target="tpu_custom_call" | custom-call | flops 3221225472 | bytes 8388608 | tf_op jit(solution)/shard_map/first/pallas_call | solution.py:493
  17.0 2.6 %collective-permute-start.3 = (f32[4,1024]{1,0:T(4,128)S(1)}, f32[4,1024]{1,0:T(4,128)S(1)}, u32[]{:S(2)}, u32[]{:S(2)}) collective-permute-start(f32[4,1024]{1,0:T(4,128)S(1)} %get-tuple-element.36.own_ref), channel_id=1, source_target_pairs={{0,25},{1,8},{2,27},{3,10},{4,29},{5,12},{6,31},{7,14},{8,1},{9,16... | collective-permute-start | bytes 49160 | tf_op jit(solution)/shard_map/ppermute | solution.py:429
  19.6 0.8 %weights.3 = (bf16[512,1024]{1,0:T(8,128)(2,1)S(1)}, bf16[512,1024]{1,0:T(8,128)(2,1)S(1)}, bf16[512,1024]{1,0:T(8,128)(2,1)S(1)}) custom-call(f32[4,1024]{1,0:T(4,128)S(1)} %get-tuple-element.36.own_ref), custom_call_target="tpu_custom_call" | custom-call | flops 536870912 | bytes 6291456 | tf_op jit(solution)/shard_map/weights/pallas_call | solution.py:480
  20.4 2.2 %collective-permute-done.3.guest_ref = f32[4,1024]{1,0:T(4,128)S(1)} collective-permute-done((f32[4,1024]{1,0:T(4,128)S(1)}, f32[4,1024]{1,0:T(4,128)S(1)}, u32[]{:S(2)}, u32[]{:S(2)}) %collective-permute-start.3) | collective-permute-done | bytes 16416 | tf_op jit(solution)/shard_map/ppermute | solution.py:429
  22.6 4.8 %middle.2 = (f32[4,1024]{1,0:T(4,128)S(1)}, f32[2,1024]{1,0:T(2,128)S(1)}) custom-call(f32[4,1024]{1,0:T(4,128)S(1)} %collective-permute-done.3.guest_ref, f32[4,1024]{1,0:T(4,128)S(1)} %get-tuple-element.36.own_ref, f32[2,1024]{1,0:T(2,128)S(1)} %get-tuple-element.37.moment_ref, bf16[512,1024]{1,0:T(8,128)(2,1)S(1)} %get-tuple-element.38.rest_0_, ...), custom_call_target="tpu_custom_call" | custom-call | flops 3221225472 | bytes 8388608 | tf_op jit(solution)/shard_map/middle/pallas_call | solution.py:493
  27.5 0.8 %collective-permute-start.4 = (f32[4,1024]{1,0:T(4,128)S(1)}, f32[4,1024]{1,0:T(4,128)S(1)}, u32[]{:S(2)}, u32[]{:S(2)}) collective-permute-start(f32[4,1024]{1,0:T(4,128)S(1)} %get-tuple-element.41.own_ref), channel_id=1, source_target_pairs={{0,17},{1,16},{2,19},{3,18},{4,21},{5,20},{6,23},{7,22},{8,25},{9,... | collective-permute-start | bytes 49160 | tf_op jit(solution)/shard_map/ppermute | solution.py:429
  28.2 0.8 %weights.4 = (bf16[512,1024]{1,0:T(8,128)(2,1)S(1)}, bf16[512,1024]{1,0:T(8,128)(2,1)S(1)}, bf16[512,1024]{1,0:T(8,128)(2,1)S(1)}) custom-call(f32[4,1024]{1,0:T(4,128)S(1)} %get-tuple-element.41.own_ref), custom_call_target="tpu_custom_call" | custom-call | flops 536870912 | bytes 6291456 | tf_op jit(solution)/shard_map/weights/pallas_call | solution.py:480
  29.0 3.1 %collective-permute-done.4.guest_ref = f32[4,1024]{1,0:T(4,128)S(1)} collective-permute-done((f32[4,1024]{1,0:T(4,128)S(1)}, f32[4,1024]{1,0:T(4,128)S(1)}, u32[]{:S(2)}, u32[]{:S(2)}) %collective-permute-start.4) | collective-permute-done | bytes 16416 | tf_op jit(solution)/shard_map/ppermute | solution.py:429
  32.2 4.7 %middle.3 = (f32[4,1024]{1,0:T(4,128)S(1)}, f32[2,1024]{1,0:T(2,128)S(1)}) custom-call(f32[4,1024]{1,0:T(4,128)S(1)} %collective-permute-done.4.guest_ref, f32[4,1024]{1,0:T(4,128)S(1)} %get-tuple-element.41.own_ref, f32[2,1024]{1,0:T(2,128)S(1)} %get-tuple-element.42.moment_ref, bf16[512,1024]{1,0:T(8,128)(2,1)S(1)} %get-tuple-element.43.rest_0_, ...), custom_call_target="tpu_custom_call" | custom-call | flops 3221225472 | bytes 8388608 | tf_op jit(solution)/shard_map/middle/pallas_call | solution.py:493
  36.8 1.6 %collective-permute-start.5 = (f32[4,1024]{1,0:T(4,128)S(1)}, f32[4,1024]{1,0:T(4,128)S(1)}, u32[]{:S(2)}, u32[]{:S(2)}) collective-permute-start(f32[4,1024]{1,0:T(4,128)S(1)} %get-tuple-element.46.own_ref), channel_id=1, source_target_pairs={{0,9},{1,24},{2,11},{3,26},{4,13},{5,28},{6,15},{7,30},{8,17},{9,0... | collective-permute-start | bytes 49160 | tf_op jit(solution)/shard_map/ppermute | solution.py:429
  38.5 0.8 %weights.5 = (bf16[512,1024]{1,0:T(8,128)(2,1)S(1)}, bf16[512,1024]{1,0:T(8,128)(2,1)S(1)}, bf16[512,1024]{1,0:T(8,128)(2,1)S(1)}) custom-call(f32[4,1024]{1,0:T(4,128)S(1)} %get-tuple-element.46.own_ref), custom_call_target="tpu_custom_call" | custom-call | flops 536870912 | bytes 6291456 | tf_op jit(solution)/shard_map/weights/pallas_call | solution.py:480
  39.3 2.3 %collective-permute-done.5.guest_ref = f32[4,1024]{1,0:T(4,128)S(1)} collective-permute-done((f32[4,1024]{1,0:T(4,128)S(1)}, f32[4,1024]{1,0:T(4,128)S(1)}, u32[]{:S(2)}, u32[]{:S(2)}) %collective-permute-start.5) | collective-permute-done | bytes 16416 | tf_op jit(solution)/shard_map/ppermute | solution.py:429
  41.5 4.6 %last.1 = (f32[2,256]{1,0:T(2,128)S(1)}, f32[2,256]{1,0:T(2,128)S(1)}) custom-call(f32[4,1024]{1,0:T(4,128)S(1)} %collective-permute-done.5.guest_ref, f32[2,1024]{1,0:T(2,128)S(1)} %get-tuple-element.47.moment_ref, bf16[512,1024]{1,0:T(8,128)(2,1)S(1)} %get-tuple-element.48.rest_0_, bf16[512,1024]{1,0:T(8,128)(2,1)S(1)} %get-tuple-element.49.rest_1_, ...), custom_call_target="tpu_custom_call" | custom-call | flops 3221225472 | bytes 8388608 | tf_op jit(solution)/shard_map/last/pallas_call | solution.py:493
  46.1 1.0 %collective-permute-start.6 = (f32[2,256]{1,0:T(2,128)S(1)}, f32[2,256]{1,0:T(2,128)S(1)}, u32[]{:S(2)}, u32[]{:S(2)}) collective-permute-start(f32[2,256]{1,0:T(2,128)S(1)} %get-tuple-element.52), channel_id=1, source_target_pairs={{0,1},{1,0},{2,3},{3,2},{4,5},{5,4},{6,7},{7,6},{8,9},{9,8},{10,11... | collective-permute-start | bytes 6152 | tf_op jit(solution)/shard_map/ppermute | solution.py:429
  47.1 2.6 %collective-permute-done.6 = f32[2,256]{1,0:T(2,128)S(1)} collective-permute-done((f32[2,256]{1,0:T(2,128)S(1)}, f32[2,256]{1,0:T(2,128)S(1)}, u32[]{:S(2)}, u32[]{:S(2)}) %collective-permute-start.6) | collective-permute-done | bytes 2080 | tf_op jit(solution)/shard_map/ppermute | solution.py:429
  49.8 0.6 %maximum_bitcast_fusion = f32[2,1,2,256]{3,2,1,0:T(2,128)} fusion(f32[1,2,256]{2,1,0:T(2,128)S(1)} %get-tuple-element.54, f32[1,2,256]{2,1,0:T(2,128)S(1)} %get-tuple-element.53), kind=kLoop, calls=%fused_computation | loop fusion | flops 1024 | bytes 8192 | tf_op jit(solution)/shard_map/broadcast_in_dim | solution.py:527
  (1 shorter events, 0.0 us)
Async XLA Ops:
  0.0 12.4 %copy-start.3 = (f32[2,1,2,256]{3,2,1,0:T(2,128)S(1)}, f32[2,1,2,256]{3,2,1,0:T(2,128)}, u32[]{:S(2)}) copy-start(f32[2,1,2,256]{3,2,1,0:T(2,128)} %param.9) | copy-start | bytes 12292
  0.0 12.4 %copy-start = (s32[2,1,2,1024]{3,2,1,0:T(2,128)S(1)}, s32[2,1,2,1024]{3,2,1,0:T(2,128)}, u32[]{:S(2)}) copy-start(s32[2,1,2,1024]{3,2,1,0:T(2,128)} %param.6) | copy-start | bytes 49156
  0.0 12.4 %copy-start.1 = (f32[2,1,2,1024]{3,2,1,0:T(2,128)S(1)}, f32[2,1,2,1024]{3,2,1,0:T(2,128)}, u32[]{:S(2)}) copy-start(f32[2,1,2,1024]{3,2,1,0:T(2,128)} %param.7) | copy-start | bytes 49156
  0.0 12.4 %copy-start.2 = (f32[2,1,1024]{2,1,0:T(1,128)S(1)}, f32[2,1,1024]{2,1,0:T(1,128)}, u32[]{:S(2)}) copy-start(f32[2,1,1024]{2,1,0:T(1,128)} %charges_ref.1) | copy-start | bytes 24580
  0.0 12.3 %collective-permute-start = (f32[2,2,256]{2,1,0:T(2,128)}, f32[2,2,256]{2,1,0:T(2,128)S(1)}, u32[]{:S(2)}, u32[]{:S(2)}) collective-permute-start(f32[2,2,256]{2,1,0:T(2,128)} %bitcast.15), channel_id=1, source_target_pairs={{0,1},{1,2},{2,3},{3,0},{4,5},{5,6},{6,7},{7,4},{8,9},{9,10},{10,1... | collective-permute-start | bytes 12296 | tf_op jit(solution)/shard_map/ppermute | solution.py:433
  3.1 9.2 %collective-permute-start.1 = (f32[2,2,256]{2,1,0:T(2,128)}, f32[2,2,256]{2,1,0:T(2,128)S(1)}, u32[]{:S(2)}, u32[]{:S(2)}) collective-permute-start(f32[2,2,256]{2,1,0:T(2,128)} %bitcast.16), channel_id=1, source_target_pairs={{0,2},{1,3},{2,0},{3,1},{4,6},{5,7},{6,4},{7,5},{8,10},{9,11},{10,... | collective-permute-start | bytes 12296 | tf_op jit(solution)/shard_map/ppermute | solution.py:433
  5.7 6.7 %collective-permute-start.2 = (f32[2,2,256]{2,1,0:T(2,128)}, f32[2,2,256]{2,1,0:T(2,128)S(1)}, u32[]{:S(2)}, u32[]{:S(2)}) collective-permute-start(f32[2,2,256]{2,1,0:T(2,128)} %bitcast.17), channel_id=1, source_target_pairs={{0,3},{1,0},{2,1},{3,2},{4,7},{5,4},{6,5},{7,6},{8,11},{9,8},{10,9... | collective-permute-start | bytes 12296 | tf_op jit(solution)/shard_map/ppermute | solution.py:433
  17.0 5.6 %collective-permute-start.3 = (f32[4,1024]{1,0:T(4,128)S(1)}, f32[4,1024]{1,0:T(4,128)S(1)}, u32[]{:S(2)}, u32[]{:S(2)}) collective-permute-start(f32[4,1024]{1,0:T(4,128)S(1)} %get-tuple-element.36.own_ref), channel_id=1, source_target_pairs={{0,25},{1,8},{2,27},{3,10},{4,29},{5,12},{6,31},{7,14},{8,1},{9,16... | collective-permute-start | bytes 49160 | tf_op jit(solution)/shard_map/ppermute | solution.py:429
  27.5 4.7 %collective-permute-start.4 = (f32[4,1024]{1,0:T(4,128)S(1)}, f32[4,1024]{1,0:T(4,128)S(1)}, u32[]{:S(2)}, u32[]{:S(2)}) collective-permute-start(f32[4,1024]{1,0:T(4,128)S(1)} %get-tuple-element.41.own_ref), channel_id=1, source_target_pairs={{0,17},{1,16},{2,19},{3,18},{4,21},{5,20},{6,23},{7,22},{8,25},{9,... | collective-permute-start | bytes 49160 | tf_op jit(solution)/shard_map/ppermute | solution.py:429
  36.8 4.7 %collective-permute-start.5 = (f32[4,1024]{1,0:T(4,128)S(1)}, f32[4,1024]{1,0:T(4,128)S(1)}, u32[]{:S(2)}, u32[]{:S(2)}) collective-permute-start(f32[4,1024]{1,0:T(4,128)S(1)} %get-tuple-element.46.own_ref), channel_id=1, source_target_pairs={{0,9},{1,24},{2,11},{3,26},{4,13},{5,28},{6,15},{7,30},{8,17},{9,0... | collective-permute-start | bytes 49160 | tf_op jit(solution)/shard_map/ppermute | solution.py:429
  46.1 3.7 %collective-permute-start.6 = (f32[2,256]{1,0:T(2,128)S(1)}, f32[2,256]{1,0:T(2,128)S(1)}, u32[]{:S(2)}, u32[]{:S(2)}) collective-permute-start(f32[2,256]{1,0:T(2,128)S(1)} %get-tuple-element.52), channel_id=1, source_target_pairs={{0,1},{1,0},{2,3},{3,2},{4,5},{5,4},{6,7},{7,6},{8,9},{9,8},{10,11... | collective-permute-start | bytes 6152 | tf_op jit(solution)/shard_map/ppermute | solution.py:429

commit v5 on v4

--- a/solution.py
+++ b/solution.py
@@ -117,6 +117,18 @@
     return [added(left, right) for left, right in zip(even, odd)]
 
 
+def places_along(shard):
+    copy, side = shard // 2, shard % 2
+    return copy, side, (side + copy) % 2
+
+
+def my_place():
+    shard = lax.axis_index("tr")
+    copy = lax.div(shard, 2)
+    side = lax.rem(shard, 2)
+    return copy, side, lax.rem(side + copy, 2)
+
+
 def setup_kernel(begins, green_ref, factor_ref, cells_ref, offsets_ref,
                  col_ref, inv_ref, row_ref, spec_ref, even_ref, slope_ref, split_ref,
                  green_vm, factor_vm, cells_vm, offsets_vm, sem):
@@ -140,10 +152,13 @@
     ]
     for copy in copies:
         copy.start()
-    own = 1 - lax.rem(lax.axis_index("tr"), 2)
+    copy_index, _, role = my_place()
+    own = 1 - role
     small[0].wait()
     small[1].wait()
-    place = cells_vm[own].astype(jnp.float32) + offsets_vm[own]
+    width = even_ref.shape[1]
+    lanes = pl.ds(pl.multiple_of(copy_index * width, width), width)
+    place = cells_vm[own, :, lanes].astype(jnp.float32) + offsets_vm[own, :, lanes]
     store_weights(place, even_ref, slope_ref, split_ref)
     small[2].wait()
 
@@ -286,17 +301,22 @@
     split_ref[...] = hats(extent, True, place[0:1])
 
 
-def weights_kernel(own_ref, even_ref, slope_ref, split_ref):
+def deposit(place, charge, extent):
+    weights_second = hats(extent, False, place[1:2])
+    weights_first = hats(extent, True, place[0:1], charge)
+    return dot_nt(weights_first, weights_second)
+
+
+def deposit_kernel(guest_ref, own_ref, grid_ref, even_ref, slope_ref, split_ref):
+    grid_ref[...] = deposit(guest_ref[0:2, :], guest_ref[2:3, :], grid_ref.shape[0])
     store_weights(own_ref[0:2, :], even_ref, slope_ref, split_ref)
 
 
-def kicks(guest, charge, even_ref, slope_ref, split_ref, col_ref, inv_ref, row_ref, spec_ref, back_ref):
+def kicks(grid, even_ref, slope_ref, split_ref, col_ref, inv_ref, row_ref, spec_ref, back_ref):
     extent = col_ref.shape[1]
     half = extent // 2
     eighth = extent // 4
-    weights_second = hats(extent, False, guest[1:2])
-    weights_first = hats(extent, True, guest[0:1], charge)
-    grid = dot_nt(weights_first, weights_second).astype(jnp.bfloat16)
+    grid = grid.astype(jnp.bfloat16)
     spreads = []
     for turn in range(2):
         real, imag = both_halves(frequency_rows(col_ref, turn), grid[:half], grid[half:])
@@ -362,51 +382,52 @@
     out_ref[3:4, :] = charge
 
 
-def first_kernel(shards, cells_ref, offsets_ref, charges_ref, momenta_ref, *rest):
-    received = rest[:-11]
-    common = rest[-11:-4]
-    out_ref, moment_out_ref, moment_ref, back_ref = rest[-4:]
-    shard = lax.axis_index("tr")
-    role = lax.rem(shard, 2)
-    own, guest = 1 - role, role
-    count = momenta_ref.shape[-1]
-    if count == moment_ref.shape[-1]:
-        moment_ref[...] = momenta_ref[own]
-    else:
-        for step, piece in enumerate((momenta_ref, *received)):
-            source = lax.rem(shard + shards - step, shards)
-            begin = pl.multiple_of(source * count, count)
-            moment_ref[:, pl.ds(begin, count)] = piece[own]
-    own_place = cells_ref[own].astype(jnp.float32) + offsets_ref[own]
-    guest_place = cells_ref[guest].astype(jnp.float32) + offsets_ref[guest]
-    kick = kicks(guest_place, charges_ref[guest], *common, back_ref)
-    extent = common[0].shape[0]
-    store_moved(out_ref, moment_out_ref, own_place, charges_ref[own], kick, moment_ref[...], extent)
-
-
-def middle_kernel(guest_ref, own_ref, moment_ref, *rest):
+def first_kernel(cells_ref, offsets_ref, charges_ref, momenta_ref, other_ref, *rest):
     common = rest[:7]
     out_ref, moment_out_ref, back_ref = rest[7:]
-    kick = kicks(guest_ref[0:2, :], guest_ref[2:3, :], *common, back_ref)
+    extent, width = common[0].shape
+    copy_index, side, role = my_place()
+    own, guest = 1 - role, role
+    mine, other = momenta_ref[own], other_ref[own]
+    moment = jnp.where(
+        side == 0, jnp.concatenate([mine, other], axis=1), jnp.concatenate([other, mine], axis=1)
+    )
+    lanes = pl.ds(pl.multiple_of(copy_index * width, width), width)
+    own_place = cells_ref[own, :, lanes].astype(jnp.float32) + offsets_ref[own, :, lanes]
+    guest_place = cells_ref[guest].astype(jnp.float32) + offsets_ref[guest]
+    grid = deposit(guest_place, charges_ref[guest], extent)
+    kick = kicks(grid, *common, back_ref)
+    charge = charges_ref[own, :, lanes]
+    store_moved(out_ref, moment_out_ref, own_place, charge, kick, moment, extent)
+
+
+def whole_grid(grid_ref, guest_refs):
+    guest = jnp.concatenate([piece[...] for piece in guest_refs], axis=1)
+    return grid_ref[...] + deposit(guest[0:2], guest[2:3], grid_ref.shape[0])
+
+
+def middle_kernel(copies, *refs):
+    grid = whole_grid(refs[0], refs[1:copies])
+    own_ref, moment_ref = refs[copies : copies + 2]
+    common = refs[copies + 2 : copies + 9]
+    out_ref, moment_out_ref, back_ref = refs[copies + 9 :]
+    kick = kicks(grid, *common, back_ref)
     own, extent = own_ref[...], common[0].shape[0]
     store_moved(out_ref, moment_out_ref, own[0:2], own[2:3], kick, moment_ref[...], extent)
 
 
-def last_kernel(guest_ref, moment_ref, *rest):
-    common = rest[:7]
-    mine_ref, theirs_ref, total_ref, back_ref = rest[7:]
+def last_kernel(copies, *refs):
+    grid = whole_grid(refs[0], refs[1:copies])
+    moment_ref = refs[copies]
+    common = refs[copies + 1 : copies + 8]
+    mine_ref, theirs_ref, back_ref = refs[copies + 8 :]
     count = mine_ref.shape[1]
-    kick = kicks(guest_ref[0:2, :], guest_ref[2:3, :], *common, back_ref)
-    total_ref[0:1, :] = moment_ref[0:1, :] + kick[0]
-    total_ref[1:2, :] = moment_ref[1:2, :] + kick[1]
-    if count == total_ref.shape[1]:
-        mine_ref[...] = total_ref[...]
-        theirs_ref[...] = total_ref[...]
-        return
-    shard = lax.axis_index("tr")
-    partner = shard + 1 - 2 * lax.rem(shard, 2)
-    mine_ref[...] = total_ref[:, pl.ds(pl.multiple_of(shard * count, count), count)]
-    theirs_ref[...] = total_ref[:, pl.ds(pl.multiple_of(partner * count, count), count)]
+    kick = kicks(grid, *common, back_ref)
+    total = jnp.concatenate([moment_ref[dim : dim + 1, :] + kick[dim] for dim in range(2)], axis=0)
+    low, high = total[:, :count], total[:, count:]
+    _, side, _ = my_place()
+    mine_ref[...] = jnp.where(side == 0, low, high)
+    theirs_ref[...] = jnp.where(side == 0, high, low)
 
 
 def per_device(cells, offsets, charges, momenta, green):
@@ -420,28 +441,24 @@
     def slot(cut, part):
         return (cut % slices) * shards + part
 
-    def exchange(value, steps):
+    copies = shards // 2
+
+    def exchange(value, steps, further=0):
         pairs = []
         for cut in range(slices):
             for part in range(shards):
-                turn = steps if part % 2 == 1 else -steps
-                pairs.append((slot(cut, part), slot(cut + turn, part ^ 1)))
+                copy, _, role = places_along(part)
+                turn = steps if role == 1 else -steps
+                goal = (copy + further) % copies
+                side = (1 - role + goal) % 2
+                pairs.append((slot(cut, part), slot(cut + turn, 2 * goal + side)))
         return lax.ppermute(value, ("cuts", "tr"), pairs)
 
     momenta = momenta[:, 0]
-    received = [
-        lax.ppermute(momenta, "tr", [(i, (i + step) % shards) for i in range(shards)])
-        for step in range(1, shards)
-    ]
-    aligned = own_count % 128 == 0
-    shard = lax.axis_index("tr")
-    if not aligned:
-        momenta = jnp.concatenate([*received[::-1], momenta], axis=2)
-        momenta = jnp.roll(momenta, (shard + 1) * own_count, axis=2)
-        received = []
-
+    other = exchange(momenta, 0)
     packed, begins = factors(extent)
-    weight = jax.ShapeDtypeStruct((extent, particles), jnp.bfloat16)
+    held = 2 * own_count
+    weight = jax.ShapeDtypeStruct((extent, held), jnp.bfloat16)
     *tables, even, slope, split = pl.pallas_call(
         functools.partial(setup_kernel, begins),
         out_shape=(
@@ -470,32 +487,31 @@
         for value in (green, jnp.asarray(packed), cells[:, 0], offsets[:, 0])
     ])
 
-    place = jax.ShapeDtypeStruct((4, particles), jnp.float32)
-    moments = jax.ShapeDtypeStruct((2, particles), jnp.float32)
+    place = jax.ShapeDtypeStruct((4, held), jnp.float32)
+    moments = jax.ShapeDtypeStruct((2, held), jnp.float32)
     piece = jax.ShapeDtypeStruct((2, own_count), jnp.float32)
     back = pltpu.VMEM((2, extent, extent), jnp.bfloat16)
-    whole = pltpu.VMEM((2, particles), jnp.float32)
-
-    def weights(own):
+
+    def deposited(guest, own):
         return pl.pallas_call(
-            weights_kernel,
-            out_shape=(weight,) * 3,
-            in_specs=[VMEM],
-            out_specs=(VMEM,) * 3,
+            deposit_kernel,
+            out_shape=(jax.ShapeDtypeStruct((extent, extent), jnp.float32), weight, weight, weight),
+            in_specs=[VMEM] * 2,
+            out_specs=(VMEM,) * 4,
             compiler_params=pltpu.CompilerParams(vmem_limit_bytes=WEIGHTS_VMEM),
             cost_estimate=pl.CostEstimate(
-                flops=period**3 // 2, bytes_accessed=6 * period**2, transcendentals=0
+                flops=period**3 // 4, bytes_accessed=4 * period**2, transcendentals=0
             ),
-            name="weights",
-        )(own)
-
-    def section(kernel, name, outs, scratch, arguments):
+            name="deposit",
+        )(guest, own)
+
+    def section(kernel, name, outs, arguments):
         return pl.pallas_call(
             kernel,
             out_shape=outs,
             in_specs=[VMEM] * (len(arguments) + 4),
             out_specs=(VMEM,) * len(outs),
-            scratch_shapes=scratch,
+            scratch_shapes=[back],
             compiler_params=pltpu.CompilerParams(vmem_limit_bytes=SECTION_VMEM),
             cost_estimate=pl.CostEstimate(
                 flops=3 * period**3, bytes_accessed=8 * period**2, transcendentals=0
@@ -504,24 +520,25 @@
         )(*arguments, *tables)
 
     own, moment = section(
-        functools.partial(first_kernel, shards), "first", (place, moments), [whole, back],
-        (cells[:, 0], offsets[:, 0], charges, momenta, *received, even, slope, split),
-    )
-    for number in range(1, SECTIONS - 1):
-        guest = exchange(own, 2 * number)
-        own, moment = section(
-            middle_kernel, "middle", (place, moments), [back], (guest, own, moment, *weights(own))
-        )
-    guest = exchange(own, 2 * (SECTIONS - 1))
-    role = shard % 2
-    outs = (piece, piece) if aligned else (moments, moments)
-    mine, theirs = section(
-        last_kernel, "last", outs, [whole, back], (guest, moment, *weights(own))
-    )
-    if not aligned:
-        theirs = lax.dynamic_slice_in_dim(mine, (shard + 1 - 2 * role) * own_count, own_count, axis=1)
-        mine = lax.dynamic_slice_in_dim(mine, shard * own_count, own_count, axis=1)
+        first_kernel, "first", (place, moments),
+        (cells[:, 0], offsets[:, 0], charges, momenta, other, even, slope, split),
+    )
+    for number in range(1, SECTIONS):
+        guests = [exchange(own, 2 * number, further) for further in reversed(range(copies))]
+        grid, *weights = deposited(guests.pop(0), own)
+        guests.insert(0, grid)
+        if number + 1 < SECTIONS:
+            own, moment = section(
+                functools.partial(middle_kernel, copies), "middle", (place, moments),
+                (*guests, own, moment, *weights),
+            )
+        else:
+            mine, theirs = section(
+                functools.partial(last_kernel, copies), "last", (piece, piece),
+                (*guests, moment, *weights),
+            )
     received = exchange(theirs, 0)
+    _, _, role = places_along(lax.axis_index("tr"))
     first = jnp.where(role == 1, mine, received)
     second = jnp.where(role == 1, received, mine)
     return jnp.stack([first, second])[:, None]

time: 50.5 us -> 49.6 us (0.982)
  Pallas kernels: 26.4 us -> 21.8 us
  waiting for transfers between devices: 10.2 us -> 13.7 us
    ppermute x4 -> x8, starting transfers between devices: 6.06 us -> 13.3 us  [exchange(): return lax.ppermute(value, ('cuts', 'tr'), pairs)]
    ppermute x3 -> x0, starting transfers between devices: 7.05 us -> none  [per_device(): lax.ppermute(momenta, 'tr', [(i, (i + step) % shards) for i in range(shar...]
    pallas_call x4, Pallas kernels: 18.7 us -> 14.4 us  [section(): pl.pallas_call(kernel, out_shape=outs, in_specs=[VMEM] * (len(arguments)...]
    ppermute x4 -> x8, waiting for transfers between devices: 10.2 us -> 13.7 us  [exchange(): return lax.ppermute(value, ('cuts', 'tr'), pairs)]
    pallas_call x1, Pallas kernels: 5.28 us -> 4.75 us  [per_device(): pl.pallas_call(functools.partial(setup_kernel, begins), out_shape=(jax.Sh...]
  transfers between devices with their start and end apart: 7 -> 8, of which waited for: 4 -> 5; matrix products, arithmetic and copies ran while one was open for 0% -> 0% of each run, Pallas kernels for 15% -> 15%
where the time goes in v5:
time: 49.6 us; the launch traced here: 49.5 us
  Pallas kernels  21.8 us (44%)
  waiting for transfers between devices  13.7 us (28%)
  starting transfers between devices  13.3 us (27%)
  other arithmetic  0.6 us (1%)
    pallas_call x4, Pallas kernels, section(): pl.pallas_call(kernel, out_shape=outs, in_specs=[VMEM] * (len(arguments)...  14.4 us
    ppermute x8, waiting for transfers between devices, exchange(): return lax.ppermute(value, ('cuts', 'tr'), pairs)  13.7 us
    ppermute x8, starting transfers between devices, exchange(): return lax.ppermute(value, ('cuts', 'tr'), pairs)  13.3 us
    pallas_call x1, Pallas kernels, per_device(): pl.pallas_call(functools.partial(setup_kernel, begins), out_shape=(jax.Sh...  4.75 us
    pallas_call x3, Pallas kernels, deposited(): pl.pallas_call(deposit_kernel, out_shape=(jax.ShapeDtypeStruct((extent, e...  2.61 us
  transfers between devices with their start and end apart: 8, of which 5 were waited for; matrix products, arithmetic and copies ran while one was open for 0% of the time, Pallas kernels for 15%

profile of v5, /device:TPU:0, one launch (start us, length us, event | category | flops | bytes accessed | tf_op | source)
XLA Modules:
  0.0 49.5 jit_solution(2418215138150594889)
XLA Ops:
  0.0 0.0 copy-start.3
  0.0 0.0 copy-start
  0.0 0.0 copy-start.1
  0.0 3.1 %collective-permute-start = (f32[2,2,256]{2,1,0:T(2,128)}, f32[2,2,256]{2,1,0:T(2,128)S(1)}, u32[]{:S(2)}, u32[]{:S(2)}) collective-permute-start(f32[2,2,256]{2,1,0:T(2,128)} %bitcast.15), channel_id=1, source_target_pairs={{0,1},{1,0},{2,3},{3,2},{4,5},{5,4},{6,7},{7,6},{8,9},{9,8},{10,11... | collective-permute-start | bytes 12296 | tf_op jit(solution)/shard_map/ppermute | solution.py:455
  3.1 4.8 %setup.1 = (bf16[512,512]{1,0:T(8,128)(2,1)S(1)}, bf16[512,512]{1,0:T(8,128)(2,1)S(1)}, bf16[8,256,256]{2,1,0:T(8,128)(2,1)S(1)}, bf16[8,512,256]{2,1,0:T(8,128)...) custom-call(f32[1024,1024]{1,0:T(8,128)} %green_ref.1, ...), custom_call_target="tpu_custom_call" | custom-call | flops 2147483648 | bytes 8388608 | tf_op jit(solution)/shard_map/setup/pallas_call | solution.py:462
  7.9 0.0 collective-permute-done.other_ref
  7.9 0.0 copy-done.3
  7.9 0.0 copy-done
  7.9 0.0 copy-done.1
  7.9 0.0 copy-done.2
  7.9 3.8 %first.1 = (f32[4,512]{1,0:T(4,128)S(1)}, f32[2,512]{1,0:T(2,128)S(1)}) custom-call(s32[2,2,1024]{2,1,0:T(2,128)S(1)} %bitcast.12, f32[2,2,1024]{2,1,0:T(2,128)S(1)} %bitcast.14, f32[2,1,1024]{2,1,0:T(1,128)S(1)} %copy-done.2, f32[2,2,256]{2,1,0:T(2,128)S(1)} %bitcast.16, f32[2,2,256]{2,1,0:T(2,128)S(1)} %collective-permute-done.other_ref, ...), custom_call_target="tpu_custom_call" | custom-call | flops 3221225472 | bytes 8388608 | tf_op jit(solution)/shard_map/first/pallas_call | solution.py:509
  11.7 4.5 %collective-permute-start.1 = (f32[4,512]{1,0:T(4,128)S(1)}, f32[4,512]{1,0:T(4,128)S(1)}, u32[]{:S(2)}, u32[]{:S(2)}) collective-permute-start(f32[4,512]{1,0:T(4,128)S(1)} %get-tuple-element.39.own_ref.refs_2_), channel_id=1, source_target_pairs={{0,26},{1,11},{2,8},{3,25},{4,30},{5,15},{6,12},{7,29},{8,2},{9,19... | collective-permute-start | bytes 24584 | tf_op jit(solution)/shard_map/ppermute | solution.py:455
  16.3 0.4 collective-permute-start.2
  16.6 1.6 %collective-permute-done.1.guest_ref = f32[4,512]{1,0:T(4,128)S(1)} collective-permute-done((f32[4,512]{1,0:T(4,128)S(1)}, f32[4,512]{1,0:T(4,128)S(1)}, u32[]{:S(2)}, u32[]{:S(2)}) %collective-permute-start.1) | collective-permute-done | bytes 8224 | tf_op jit(solution)/shard_map/ppermute | solution.py:455
  18.2 0.8 %deposit.3 = (f32[512,512]{1,0:T(8,128)S(1)}, bf16[512,512]{1,0:T(8,128)(2,1)S(1)}, bf16[512,512]{1,0:T(8,128)(2,1)S(1)}, bf16[512,512]{1,0:T(8,128)(2,1)S(1)}) custom-call(f32[4,512]{1,0:T(4,128)S(1)} %collective-permute-done.1.guest_ref, f32[4,512]{1,0:T(4,128)S(1)} %get-tuple-element.39.own_ref.refs_2_), custom_call_target="tpu_custom_call" | custom-call | flops 268435456 | bytes 4194304 | tf_op jit(solution)/shard_map/deposit/pallas_call | solution.py:496
  19.0 2.7 %collective-permute-done.2.refs_1_ = f32[4,512]{1,0:T(4,128)S(1)} collective-permute-done((f32[4,512]{1,0:T(4,128)S(1)}, f32[4,512]{1,0:T(4,128)S(1)}, u32[]{:S(2)}, u32[]{:S(2)}) %collective-permute-start.2) | collective-permute-done | bytes 8224 | tf_op jit(solution)/shard_map/ppermute | solution.py:455
  21.7 3.6 %middle.2 = (f32[4,512]{1,0:T(4,128)S(1)}, f32[2,512]{1,0:T(2,128)S(1)}) custom-call(f32[512,512]{1,0:T(8,128)S(1)} %get-tuple-element.40.refs_0_, f32[4,512]{1,0:T(4,128)S(1)} %collective-permute-done.2.refs_1_, f32[4,512]{1,0:T(4,128)S(1)} %get-tuple-element.39.own_ref.refs_2_, f32[2,512]{1,0:T(2,128)S(1)} %get-tuple-element.41.refs_3_, ...), custom_call_target="tpu_custom_call" | custom-call | flops 3221225472 | bytes 8388608 | tf_op jit(solution)/shard_map/middle/pallas_call | solution.py:509
  25.3 0.1 collective-permute-start.3
  25.4 1.7 %collective-permute-start.4 = (f32[4,512]{1,0:T(4,128)S(1)}, f32[4,512]{1,0:T(4,128)S(1)}, u32[]{:S(2)}, u32[]{:S(2)}) collective-permute-start(f32[4,512]{1,0:T(4,128)S(1)} %get-tuple-element.45.own_ref.refs_2_), channel_id=1, source_target_pairs={{0,17},{1,16},{2,19},{3,18},{4,21},{5,20},{6,23},{7,22},{8,25},{9,... | collective-permute-start | bytes 24584 | tf_op jit(solution)/shard_map/ppermute | solution.py:455
  27.0 3.8 %collective-permute-done.3.guest_ref = f32[4,512]{1,0:T(4,128)S(1)} collective-permute-done((f32[4,512]{1,0:T(4,128)S(1)}, f32[4,512]{1,0:T(4,128)S(1)}, u32[]{:S(2)}, u32[]{:S(2)}) %collective-permute-start.3) | collective-permute-done | bytes 8224 | tf_op jit(solution)/shard_map/ppermute | solution.py:455
  30.8 1.0 %deposit.4 = (f32[512,512]{1,0:T(8,128)S(1)}, bf16[512,512]{1,0:T(8,128)(2,1)S(1)}, bf16[512,512]{1,0:T(8,128)(2,1)S(1)}, bf16[512,512]{1,0:T(8,128)(2,1)S(1)}) custom-call(f32[4,512]{1,0:T(4,128)S(1)} %collective-permute-done.3.guest_ref, f32[4,512]{1,0:T(4,128)S(1)} %get-tuple-element.45.own_ref.refs_2_), custom_call_target="tpu_custom_call" | custom-call | flops 268435456 | bytes 4194304 | tf_op jit(solution)/shard_map/deposit/pallas_call | solution.py:496
  31.8 0.0 collective-permute-done.4.refs_1_
  31.8 3.6 %middle.3 = (f32[4,512]{1,0:T(4,128)S(1)}, f32[2,512]{1,0:T(2,128)S(1)}) custom-call(f32[512,512]{1,0:T(8,128)S(1)} %get-tuple-element.46.refs_0_, f32[4,512]{1,0:T(4,128)S(1)} %collective-permute-done.4.refs_1_, f32[4,512]{1,0:T(4,128)S(1)} %get-tuple-element.45.own_ref.refs_2_, f32[2,512]{1,0:T(2,128)S(1)} %get-tuple-element.47.refs_3_, ...), custom_call_target="tpu_custom_call" | custom-call | flops 3221225472 | bytes 8388608 | tf_op jit(solution)/shard_map/middle/pallas_call | solution.py:509
  35.4 0.8 %collective-permute-start.5 = (f32[4,512]{1,0:T(4,128)S(1)}, f32[4,512]{1,0:T(4,128)S(1)}, u32[]{:S(2)}, u32[]{:S(2)}) collective-permute-start(f32[4,512]{1,0:T(4,128)S(1)} %get-tuple-element.51.own_ref), channel_id=1, source_target_pairs={{0,10},{1,27},{2,24},{3,9},{4,14},{5,31},{6,28},{7,13},{8,18},{9,3... | collective-permute-start | bytes 24584 | tf_op jit(solution)/shard_map/ppermute | solution.py:455
  36.2 1.1 %collective-permute-start.6 = (f32[4,512]{1,0:T(4,128)S(1)}, f32[4,512]{1,0:T(4,128)S(1)}, u32[]{:S(2)}, u32[]{:S(2)}) collective-permute-start(f32[4,512]{1,0:T(4,128)S(1)} %get-tuple-element.51.own_ref), channel_id=1, source_target_pairs={{0,9},{1,24},{2,27},{3,10},{4,13},{5,28},{6,31},{7,14},{8,17},{9,0... | collective-permute-start | bytes 24584 | tf_op jit(solution)/shard_map/ppermute | solution.py:455
  37.4 3.5 %collective-permute-done.5.guest_ref = f32[4,512]{1,0:T(4,128)S(1)} collective-permute-done((f32[4,512]{1,0:T(4,128)S(1)}, f32[4,512]{1,0:T(4,128)S(1)}, u32[]{:S(2)}, u32[]{:S(2)}) %collective-permute-start.5) | collective-permute-done | bytes 8224 | tf_op jit(solution)/shard_map/ppermute | solution.py:455
  40.9 0.8 %deposit.5 = (f32[512,512]{1,0:T(8,128)S(1)}, bf16[512,512]{1,0:T(8,128)(2,1)S(1)}, bf16[512,512]{1,0:T(8,128)(2,1)S(1)}, bf16[512,512]{1,0:T(8,128)(2,1)S(1)}) custom-call(f32[4,512]{1,0:T(4,128)S(1)} %collective-permute-done.5.guest_ref, f32[4,512]{1,0:T(4,128)S(1)} %get-tuple-element.51.own_ref), custom_call_target="tpu_custom_call" | custom-call | flops 268435456 | bytes 4194304 | tf_op jit(solution)/shard_map/deposit/pallas_call | solution.py:496
  41.7 0.0 collective-permute-done.6.refs_1_
  41.7 3.5 %last.1 = (f32[2,256]{1,0:T(2,128)S(1)}, f32[2,256]{1,0:T(2,128)S(1)}) custom-call(f32[512,512]{1,0:T(8,128)S(1)} %get-tuple-element.52.refs_0_, f32[4,512]{1,0:T(4,128)S(1)} %collective-permute-done.6.refs_1_, f32[2,512]{1,0:T(2,128)S(1)} %get-tuple-element.53.refs_2_, bf16[512,512]{1,0:T(8,128)(2,1)S(1)} %get-tuple-element.54.refs_3_, ...), custom_call_target="tpu_custom_call" | custom-call | flops 3221225472 | bytes 8388608 | tf_op jit(solution)/shard_map/last/pallas_call | solution.py:509
  45.2 1.6 %collective-permute-start.7 = (f32[2,256]{1,0:T(2,128)S(1)}, f32[2,256]{1,0:T(2,128)S(1)}, u32[]{:S(2)}, u32[]{:S(2)}) collective-permute-start(f32[2,256]{1,0:T(2,128)S(1)} %get-tuple-element.58), channel_id=1, source_target_pairs={{0,1},{1,0},{2,3},{3,2},{4,5},{5,4},{6,7},{7,6},{8,9},{9,8},{10,11... | collective-permute-start | bytes 6152 | tf_op jit(solution)/shard_map/ppermute | solution.py:455
  46.8 2.1 %collective-permute-done.7 = f32[2,256]{1,0:T(2,128)S(1)} collective-permute-done((f32[2,256]{1,0:T(2,128)S(1)}, f32[2,256]{1,0:T(2,128)S(1)}, u32[]{:S(2)}, u32[]{:S(2)}) %collective-permute-start.7) | collective-permute-done | bytes 2080 | tf_op jit(solution)/shard_map/ppermute | solution.py:455
  48.9 0.6 %maximum_bitcast_fusion = f32[2,1,2,256]{3,2,1,0:T(2,128)} fusion(f32[1,2,256]{2,1,0:T(2,128)S(1)} %get-tuple-element.60, f32[1,2,256]{2,1,0:T(2,128)S(1)} %get-tuple-element.59), kind=kLoop, calls=%fused_computation | loop fusion | flops 1024 | bytes 8192 | tf_op jit(solution)/shard_map/broadcast_in_dim | solution.py:544
  (2 shorter events, 0.0 us)
Async XLA Ops:
  0.0 7.9 %copy-start.3 = (f32[2,1,2,256]{3,2,1,0:T(2,128)S(1)}, f32[2,1,2,256]{3,2,1,0:T(2,128)}, u32[]{:S(2)}) copy-start(f32[2,1,2,256]{3,2,1,0:T(2,128)} %param.9) | copy-start | bytes 12292
  0.0 7.9 %copy-start = (s32[2,1,2,1024]{3,2,1,0:T(2,128)S(1)}, s32[2,1,2,1024]{3,2,1,0:T(2,128)}, u32[]{:S(2)}) copy-start(s32[2,1,2,1024]{3,2,1,0:T(2,128)} %param.6) | copy-start | bytes 49156
  0.0 7.9 %copy-start.1 = (f32[2,1,2,1024]{3,2,1,0:T(2,128)S(1)}, f32[2,1,2,1024]{3,2,1,0:T(2,128)}, u32[]{:S(2)}) copy-start(f32[2,1,2,1024]{3,2,1,0:T(2,128)} %param.7) | copy-start | bytes 49156
  0.0 7.9 %copy-start.2 = (f32[2,1,1024]{2,1,0:T(1,128)S(1)}, f32[2,1,1024]{2,1,0:T(1,128)}, u32[]{:S(2)}) copy-start(f32[2,1,1024]{2,1,0:T(1,128)} %charges_ref.1) | copy-start | bytes 24580
  0.0 7.9 %collective-permute-start = (f32[2,2,256]{2,1,0:T(2,128)}, f32[2,2,256]{2,1,0:T(2,128)S(1)}, u32[]{:S(2)}, u32[]{:S(2)}) collective-permute-start(f32[2,2,256]{2,1,0:T(2,128)} %bitcast.15), channel_id=1, source_target_pairs={{0,1},{1,0},{2,3},{3,2},{4,5},{5,4},{6,7},{7,6},{8,9},{9,8},{10,11... | collective-permute-start | bytes 12296 | tf_op jit(solution)/shard_map/ppermute | solution.py:455
  11.7 6.4 %collective-permute-start.1 = (f32[4,512]{1,0:T(4,128)S(1)}, f32[4,512]{1,0:T(4,128)S(1)}, u32[]{:S(2)}, u32[]{:S(2)}) collective-permute-start(f32[4,512]{1,0:T(4,128)S(1)} %get-tuple-element.39.own_ref.refs_2_), channel_id=1, source_target_pairs={{0,26},{1,11},{2,8},{3,25},{4,30},{5,15},{6,12},{7,29},{8,2},{9,19... | collective-permute-start | bytes 24584 | tf_op jit(solution)/shard_map/ppermute | solution.py:455
  16.3 5.4 %collective-permute-start.2 = (f32[4,512]{1,0:T(4,128)S(1)}, f32[4,512]{1,0:T(4,128)S(1)}, u32[]{:S(2)}, u32[]{:S(2)}) collective-permute-start(f32[4,512]{1,0:T(4,128)S(1)} %get-tuple-element.39.own_ref.refs_2_), channel_id=1, source_target_pairs={{0,25},{1,8},{2,11},{3,26},{4,29},{5,12},{6,15},{7,30},{8,1},{9,16... | collective-permute-start | bytes 24584 | tf_op jit(solution)/shard_map/ppermute | solution.py:455
  25.3 5.5 %collective-permute-start.3 = (f32[4,512]{1,0:T(4,128)S(1)}, f32[4,512]{1,0:T(4,128)S(1)}, u32[]{:S(2)}, u32[]{:S(2)}) collective-permute-start(f32[4,512]{1,0:T(4,128)S(1)} %get-tuple-element.45.own_ref.refs_2_), channel_id=1, source_target_pairs={{0,18},{1,19},{2,16},{3,17},{4,22},{5,23},{6,20},{7,21},{8,26},{9,... | collective-permute-start | bytes 24584 | tf_op jit(solution)/shard_map/ppermute | solution.py:455
  25.4 6.4 %collective-permute-start.4 = (f32[4,512]{1,0:T(4,128)S(1)}, f32[4,512]{1,0:T(4,128)S(1)}, u32[]{:S(2)}, u32[]{:S(2)}) collective-permute-start(f32[4,512]{1,0:T(4,128)S(1)} %get-tuple-element.45.own_ref.refs_2_), channel_id=1, source_target_pairs={{0,17},{1,16},{2,19},{3,18},{4,21},{5,20},{6,23},{7,22},{8,25},{9,... | collective-permute-start | bytes 24584 | tf_op jit(solution)/shard_map/ppermute | solution.py:455
  35.4 5.5 %collective-permute-start.5 = (f32[4,512]{1,0:T(4,128)S(1)}, f32[4,512]{1,0:T(4,128)S(1)}, u32[]{:S(2)}, u32[]{:S(2)}) collective-permute-start(f32[4,512]{1,0:T(4,128)S(1)} %get-tuple-element.51.own_ref), channel_id=1, source_target_pairs={{0,10},{1,27},{2,24},{3,9},{4,14},{5,31},{6,28},{7,13},{8,18},{9,3... | collective-permute-start | bytes 24584 | tf_op jit(solution)/shard_map/ppermute | solution.py:455
  36.2 5.5 %collective-permute-start.6 = (f32[4,512]{1,0:T(4,128)S(1)}, f32[4,512]{1,0:T(4,128)S(1)}, u32[]{:S(2)}, u32[]{:S(2)}) collective-permute-start(f32[4,512]{1,0:T(4,128)S(1)} %get-tuple-element.51.own_ref), channel_id=1, source_target_pairs={{0,9},{1,24},{2,27},{3,10},{4,13},{5,28},{6,31},{7,14},{8,17},{9,0... | collective-permute-start | bytes 24584 | tf_op jit(solution)/shard_map/ppermute | solution.py:455
  45.2 3.7 %collective-permute-start.7 = (f32[2,256]{1,0:T(2,128)S(1)}, f32[2,256]{1,0:T(2,128)S(1)}, u32[]{:S(2)}, u32[]{:S(2)}) collective-permute-start(f32[2,256]{1,0:T(2,128)S(1)} %get-tuple-element.58), channel_id=1, source_target_pairs={{0,1},{1,0},{2,3},{3,2},{4,5},{5,4},{6,7},{7,6},{8,9},{9,8},{10,11... | collective-permute-start | bytes 6152 | tf_op jit(solution)/shard_map/ppermute | solution.py:455

commit v6 on v5

--- a/solution.py
+++ b/solution.py
@@ -212,8 +212,8 @@
                 cut = slice(q * eighth, (q + 1) * eighth)
                 parts[turn].append(
                     (
-                        near[0][:, cut] - sign * far[1][:, cut],
-                        near[1][:, cut] + sign * far[0][:, cut],
+                        (near[0][:, cut] - sign * far[1][:, cut]).astype(jnp.bfloat16),
+                        (near[1][:, cut] + sign * far[0][:, cut]).astype(jnp.bfloat16),
                     )
                 )
     for turn in range(2):

time: 49.6 us -> 49.2 us (level)
  waiting for transfers between devices: 13.7 us -> 13.2 us
  transfers between devices with their start and end apart: 8 -> 8, of which waited for: 5 -> 5; matrix products, arithmetic and copies ran while one was open for 0% -> 0% of each run, Pallas kernels for 15% -> 14%
where the time goes in v6:
time: 49.2 us; the launch traced here: 49.1 us
  Pallas kernels  21.4 us (43%)
  starting transfers between devices  13.7 us (28%)
  waiting for transfers between devices  13.2 us (27%)
  other arithmetic  0.6 us (1%)
    pallas_call x4, Pallas kernels, section(): pl.pallas_call(kernel, out_shape=outs, in_specs=[VMEM] * (len(arguments)...  14.6 us
    ppermute x8, starting transfers between devices, exchange(): return lax.ppermute(value, ('cuts', 'tr'), pairs)  13.7 us
    ppermute x8, waiting for transfers between devices, exchange(): return lax.ppermute(value, ('cuts', 'tr'), pairs)  13.2 us
    pallas_call x1, Pallas kernels, per_device(): pl.pallas_call(functools.partial(setup_kernel, begins), out_shape=(jax.Sh...  4.34 us
    pallas_call x3, Pallas kernels, deposited(): pl.pallas_call(deposit_kernel, out_shape=(jax.ShapeDtypeStruct((extent, e...  2.42 us
  transfers between devices with their start and end apart: 8, of which 5 were waited for; matrix products, arithmetic and copies ran while one was open for 0% of the time, Pallas kernels for 14%

profile of v6, /device:TPU:0, one launch (start us, length us, event | category | flops | bytes accessed | tf_op | source)
XLA Modules:
  0.0 49.1 jit_solution(15021200948024150834)
XLA Ops:
  0.0 0.0 copy-start.3
  0.0 0.0 copy-start.1
  0.0 0.0 copy-start.2
  0.0 3.1 %collective-permute-start = (f32[2,2,256]{2,1,0:T(2,128)}, f32[2,2,256]{2,1,0:T(2,128)S(1)}, u32[]{:S(2)}, u32[]{:S(2)}) collective-permute-start(f32[2,2,256]{2,1,0:T(2,128)} %bitcast.15), channel_id=1, source_target_pairs={{0,1},{1,0},{2,3},{3,2},{4,5},{5,4},{6,7},{7,6},{8,9},{9,8},{10,11... | collective-permute-start | bytes 12296 | tf_op jit(solution)/shard_map/ppermute | solution.py:455
  3.1 4.3 %setup.1 = (bf16[512,512]{1,0:T(8,128)(2,1)S(1)}, bf16[512,512]{1,0:T(8,128)(2,1)S(1)}, bf16[8,256,256]{2,1,0:T(8,128)(2,1)S(1)}, bf16[8,512,256]{2,1,0:T(8,128)...) custom-call(f32[1024,1024]{1,0:T(8,128)} %green_ref.1, ...), custom_call_target="tpu_custom_call" | custom-call | flops 2147483648 | bytes 8388608 | tf_op jit(solution)/shard_map/setup/pallas_call | solution.py:462
  7.5 0.0 collective-permute-done.other_ref
  7.5 0.0 copy-done.3
  7.5 0.0 copy-done
  7.5 0.0 copy-done.1
  7.5 0.0 copy-done.2
  7.5 3.8 %first.1 = (f32[4,512]{1,0:T(4,128)S(1)}, f32[2,512]{1,0:T(2,128)S(1)}) custom-call(s32[2,2,1024]{2,1,0:T(2,128)S(1)} %bitcast.12, f32[2,2,1024]{2,1,0:T(2,128)S(1)} %bitcast.14, f32[2,1,1024]{2,1,0:T(1,128)S(1)} %copy-done.2, f32[2,2,256]{2,1,0:T(2,128)S(1)} %bitcast.16, f32[2,2,256]{2,1,0:T(2,128)S(1)} %collective-permute-done.other_ref, ...), custom_call_target="tpu_custom_call" | custom-call | flops 3221225472 | bytes 8388608 | tf_op jit(solution)/shard_map/first/pallas_call | solution.py:509
  11.3 4.5 %collective-permute-start.1 = (f32[4,512]{1,0:T(4,128)S(1)}, f32[4,512]{1,0:T(4,128)S(1)}, u32[]{:S(2)}, u32[]{:S(2)}) collective-permute-start(f32[4,512]{1,0:T(4,128)S(1)} %get-tuple-element.39.own_ref.refs_2_), channel_id=1, source_target_pairs={{0,26},{1,11},{2,8},{3,25},{4,30},{5,15},{6,12},{7,29},{8,2},{9,19... | collective-permute-start | bytes 24584 | tf_op jit(solution)/shard_map/ppermute | solution.py:455
  15.9 0.4 collective-permute-start.2
  16.2 1.5 %collective-permute-done.1.guest_ref = f32[4,512]{1,0:T(4,128)S(1)} collective-permute-done((f32[4,512]{1,0:T(4,128)S(1)}, f32[4,512]{1,0:T(4,128)S(1)}, u32[]{:S(2)}, u32[]{:S(2)}) %collective-permute-start.1) | collective-permute-done | bytes 8224 | tf_op jit(solution)/shard_map/ppermute | solution.py:455
  17.8 0.8 %deposit.3 = (f32[512,512]{1,0:T(8,128)S(1)}, bf16[512,512]{1,0:T(8,128)(2,1)S(1)}, bf16[512,512]{1,0:T(8,128)(2,1)S(1)}, bf16[512,512]{1,0:T(8,128)(2,1)S(1)}) custom-call(f32[4,512]{1,0:T(4,128)S(1)} %collective-permute-done.1.guest_ref, f32[4,512]{1,0:T(4,128)S(1)} %get-tuple-element.39.own_ref.refs_2_), custom_call_target="tpu_custom_call" | custom-call | flops 268435456 | bytes 4194304 | tf_op jit(solution)/shard_map/deposit/pallas_call | solution.py:496
  18.6 2.7 %collective-permute-done.2.refs_1_ = f32[4,512]{1,0:T(4,128)S(1)} collective-permute-done((f32[4,512]{1,0:T(4,128)S(1)}, f32[4,512]{1,0:T(4,128)S(1)}, u32[]{:S(2)}, u32[]{:S(2)}) %collective-permute-start.2) | collective-permute-done | bytes 8224 | tf_op jit(solution)/shard_map/ppermute | solution.py:455
  21.3 3.6 %middle.2 = (f32[4,512]{1,0:T(4,128)S(1)}, f32[2,512]{1,0:T(2,128)S(1)}) custom-call(f32[512,512]{1,0:T(8,128)S(1)} %get-tuple-element.40.refs_0_, f32[4,512]{1,0:T(4,128)S(1)} %collective-permute-done.2.refs_1_, f32[4,512]{1,0:T(4,128)S(1)} %get-tuple-element.39.own_ref.refs_2_, f32[2,512]{1,0:T(2,128)S(1)} %get-tuple-element.41.refs_3_, ...), custom_call_target="tpu_custom_call" | custom-call | flops 3221225472 | bytes 8388608 | tf_op jit(solution)/shard_map/middle/pallas_call | solution.py:509
  24.9 0.1 collective-permute-start.3
  24.9 1.7 %collective-permute-start.4 = (f32[4,512]{1,0:T(4,128)S(1)}, f32[4,512]{1,0:T(4,128)S(1)}, u32[]{:S(2)}, u32[]{:S(2)}) collective-permute-start(f32[4,512]{1,0:T(4,128)S(1)} %get-tuple-element.45.own_ref.refs_2_), channel_id=1, source_target_pairs={{0,17},{1,16},{2,19},{3,18},{4,21},{5,20},{6,23},{7,22},{8,25},{9,... | collective-permute-start | bytes 24584 | tf_op jit(solution)/shard_map/ppermute | solution.py:455
  26.6 3.7 %collective-permute-done.3.guest_ref = f32[4,512]{1,0:T(4,128)S(1)} collective-permute-done((f32[4,512]{1,0:T(4,128)S(1)}, f32[4,512]{1,0:T(4,128)S(1)}, u32[]{:S(2)}, u32[]{:S(2)}) %collective-permute-start.3) | collective-permute-done | bytes 8224 | tf_op jit(solution)/shard_map/ppermute | solution.py:455
  30.4 0.8 %deposit.4 = (f32[512,512]{1,0:T(8,128)S(1)}, bf16[512,512]{1,0:T(8,128)(2,1)S(1)}, bf16[512,512]{1,0:T(8,128)(2,1)S(1)}, bf16[512,512]{1,0:T(8,128)(2,1)S(1)}) custom-call(f32[4,512]{1,0:T(4,128)S(1)} %collective-permute-done.3.guest_ref, f32[4,512]{1,0:T(4,128)S(1)} %get-tuple-element.45.own_ref.refs_2_), custom_call_target="tpu_custom_call" | custom-call | flops 268435456 | bytes 4194304 | tf_op jit(solution)/shard_map/deposit/pallas_call | solution.py:496
  31.2 0.0 collective-permute-done.4.refs_1_
  31.2 3.8 %middle.3 = (f32[4,512]{1,0:T(4,128)S(1)}, f32[2,512]{1,0:T(2,128)S(1)}) custom-call(f32[512,512]{1,0:T(8,128)S(1)} %get-tuple-element.46.refs_0_, f32[4,512]{1,0:T(4,128)S(1)} %collective-permute-done.4.refs_1_, f32[4,512]{1,0:T(4,128)S(1)} %get-tuple-element.45.own_ref.refs_2_, f32[2,512]{1,0:T(2,128)S(1)} %get-tuple-element.47.refs_3_, ...), custom_call_target="tpu_custom_call" | custom-call | flops 3221225472 | bytes 8388608 | tf_op jit(solution)/shard_map/middle/pallas_call | solution.py:509
  35.0 0.8 %collective-permute-start.5 = (f32[4,512]{1,0:T(4,128)S(1)}, f32[4,512]{1,0:T(4,128)S(1)}, u32[]{:S(2)}, u32[]{:S(2)}) collective-permute-start(f32[4,512]{1,0:T(4,128)S(1)} %get-tuple-element.51.own_ref), channel_id=1, source_target_pairs={{0,10},{1,27},{2,24},{3,9},{4,14},{5,31},{6,28},{7,13},{8,18},{9,3... | collective-permute-start | bytes 24584 | tf_op jit(solution)/shard_map/ppermute | solution.py:455
  35.8 1.3 %collective-permute-start.6 = (f32[4,512]{1,0:T(4,128)S(1)}, f32[4,512]{1,0:T(4,128)S(1)}, u32[]{:S(2)}, u32[]{:S(2)}) collective-permute-start(f32[4,512]{1,0:T(4,128)S(1)} %get-tuple-element.51.own_ref), channel_id=1, source_target_pairs={{0,9},{1,24},{2,27},{3,10},{4,13},{5,28},{6,31},{7,14},{8,17},{9,0... | collective-permute-start | bytes 24584 | tf_op jit(solution)/shard_map/ppermute | solution.py:455
  37.1 3.3 %collective-permute-done.5.guest_ref = f32[4,512]{1,0:T(4,128)S(1)} collective-permute-done((f32[4,512]{1,0:T(4,128)S(1)}, f32[4,512]{1,0:T(4,128)S(1)}, u32[]{:S(2)}, u32[]{:S(2)}) %collective-permute-start.5) | collective-permute-done | bytes 8224 | tf_op jit(solution)/shard_map/ppermute | solution.py:455
  40.5 0.8 %deposit.5 = (f32[512,512]{1,0:T(8,128)S(1)}, bf16[512,512]{1,0:T(8,128)(2,1)S(1)}, bf16[512,512]{1,0:T(8,128)(2,1)S(1)}, bf16[512,512]{1,0:T(8,128)(2,1)S(1)}) custom-call(f32[4,512]{1,0:T(4,128)S(1)} %collective-permute-done.5.guest_ref, f32[4,512]{1,0:T(4,128)S(1)} %get-tuple-element.51.own_ref), custom_call_target="tpu_custom_call" | custom-call | flops 268435456 | bytes 4194304 | tf_op jit(solution)/shard_map/deposit/pallas_call | solution.py:496
  41.3 0.0 collective-permute-done.6.refs_1_
  41.3 3.5 %last.1 = (f32[2,256]{1,0:T(2,128)S(1)}, f32[2,256]{1,0:T(2,128)S(1)}) custom-call(f32[512,512]{1,0:T(8,128)S(1)} %get-tuple-element.52.refs_0_, f32[4,512]{1,0:T(4,128)S(1)} %collective-permute-done.6.refs_1_, f32[2,512]{1,0:T(2,128)S(1)} %get-tuple-element.53.refs_2_, bf16[512,512]{1,0:T(8,128)(2,1)S(1)} %get-tuple-element.54.refs_3_, ...), custom_call_target="tpu_custom_call" | custom-call | flops 3221225472 | bytes 8388608 | tf_op jit(solution)/shard_map/last/pallas_call | solution.py:509
  44.8 1.8 %collective-permute-start.7 = (f32[2,256]{1,0:T(2,128)S(1)}, f32[2,256]{1,0:T(2,128)S(1)}, u32[]{:S(2)}, u32[]{:S(2)}) collective-permute-start(f32[2,256]{1,0:T(2,128)S(1)} %get-tuple-element.58), channel_id=1, source_target_pairs={{0,1},{1,0},{2,3},{3,2},{4,5},{5,4},{6,7},{7,6},{8,9},{9,8},{10,11... | collective-permute-start | bytes 6152 | tf_op jit(solution)/shard_map/ppermute | solution.py:455
  46.6 1.9 %collective-permute-done.7 = f32[2,256]{1,0:T(2,128)S(1)} collective-permute-done((f32[2,256]{1,0:T(2,128)S(1)}, f32[2,256]{1,0:T(2,128)S(1)}, u32[]{:S(2)}, u32[]{:S(2)}) %collective-permute-start.7) | collective-permute-done | bytes 2080 | tf_op jit(solution)/shard_map/ppermute | solution.py:455
  48.5 0.6 %maximum_bitcast_fusion = f32[2,1,2,256]{3,2,1,0:T(2,128)} fusion(f32[1,2,256]{2,1,0:T(2,128)S(1)} %get-tuple-element.60, f32[1,2,256]{2,1,0:T(2,128)S(1)} %get-tuple-element.59), kind=kLoop, calls=%fused_computation | loop fusion | flops 1024 | bytes 8192 | tf_op jit(solution)/shard_map/broadcast_in_dim | solution.py:544
  (2 shorter events, 0.0 us)
Async XLA Ops:
  0.0 7.5 %copy-start.3 = (f32[2,1,2,256]{3,2,1,0:T(2,128)S(1)}, f32[2,1,2,256]{3,2,1,0:T(2,128)}, u32[]{:S(2)}) copy-start(f32[2,1,2,256]{3,2,1,0:T(2,128)} %param.9) | copy-start | bytes 12292
  0.0 7.5 %copy-start = (s32[2,1,2,1024]{3,2,1,0:T(2,128)S(1)}, s32[2,1,2,1024]{3,2,1,0:T(2,128)}, u32[]{:S(2)}) copy-start(s32[2,1,2,1024]{3,2,1,0:T(2,128)} %param.6) | copy-start | bytes 49156
  0.0 7.5 %copy-start.1 = (f32[2,1,2,1024]{3,2,1,0:T(2,128)S(1)}, f32[2,1,2,1024]{3,2,1,0:T(2,128)}, u32[]{:S(2)}) copy-start(f32[2,1,2,1024]{3,2,1,0:T(2,128)} %param.7) | copy-start | bytes 49156
  0.0 7.5 %copy-start.2 = (f32[2,1,1024]{2,1,0:T(1,128)S(1)}, f32[2,1,1024]{2,1,0:T(1,128)}, u32[]{:S(2)}) copy-start(f32[2,1,1024]{2,1,0:T(1,128)} %charges_ref.1) | copy-start | bytes 24580
  0.0 7.5 %collective-permute-start = (f32[2,2,256]{2,1,0:T(2,128)}, f32[2,2,256]{2,1,0:T(2,128)S(1)}, u32[]{:S(2)}, u32[]{:S(2)}) collective-permute-start(f32[2,2,256]{2,1,0:T(2,128)} %bitcast.15), channel_id=1, source_target_pairs={{0,1},{1,0},{2,3},{3,2},{4,5},{5,4},{6,7},{7,6},{8,9},{9,8},{10,11... | collective-permute-start | bytes 12296 | tf_op jit(solution)/shard_map/ppermute | solution.py:455
  11.3 6.5 %collective-permute-start.1 = (f32[4,512]{1,0:T(4,128)S(1)}, f32[4,512]{1,0:T(4,128)S(1)}, u32[]{:S(2)}, u32[]{:S(2)}) collective-permute-start(f32[4,512]{1,0:T(4,128)S(1)} %get-tuple-element.39.own_ref.refs_2_), channel_id=1, source_target_pairs={{0,26},{1,11},{2,8},{3,25},{4,30},{5,15},{6,12},{7,29},{8,2},{9,19... | collective-permute-start | bytes 24584 | tf_op jit(solution)/shard_map/ppermute | solution.py:455
  15.9 5.4 %collective-permute-start.2 = (f32[4,512]{1,0:T(4,128)S(1)}, f32[4,512]{1,0:T(4,128)S(1)}, u32[]{:S(2)}, u32[]{:S(2)}) collective-permute-start(f32[4,512]{1,0:T(4,128)S(1)} %get-tuple-element.39.own_ref.refs_2_), channel_id=1, source_target_pairs={{0,25},{1,8},{2,11},{3,26},{4,29},{5,12},{6,15},{7,30},{8,1},{9,16... | collective-permute-start | bytes 24584 | tf_op jit(solution)/shard_map/ppermute | solution.py:455
  24.9 5.5 %collective-permute-start.3 = (f32[4,512]{1,0:T(4,128)S(1)}, f32[4,512]{1,0:T(4,128)S(1)}, u32[]{:S(2)}, u32[]{:S(2)}) collective-permute-start(f32[4,512]{1,0:T(4,128)S(1)} %get-tuple-element.45.own_ref.refs_2_), channel_id=1, source_target_pairs={{0,18},{1,19},{2,16},{3,17},{4,22},{5,23},{6,20},{7,21},{8,26},{9,... | collective-permute-start | bytes 24584 | tf_op jit(solution)/shard_map/ppermute | solution.py:455
  24.9 6.2 %collective-permute-start.4 = (f32[4,512]{1,0:T(4,128)S(1)}, f32[4,512]{1,0:T(4,128)S(1)}, u32[]{:S(2)}, u32[]{:S(2)}) collective-permute-start(f32[4,512]{1,0:T(4,128)S(1)} %get-tuple-element.45.own_ref.refs_2_), channel_id=1, source_target_pairs={{0,17},{1,16},{2,19},{3,18},{4,21},{5,20},{6,23},{7,22},{8,25},{9,... | collective-permute-start | bytes 24584 | tf_op jit(solution)/shard_map/ppermute | solution.py:455
  35.0 5.5 %collective-permute-start.5 = (f32[4,512]{1,0:T(4,128)S(1)}, f32[4,512]{1,0:T(4,128)S(1)}, u32[]{:S(2)}, u32[]{:S(2)}) collective-permute-start(f32[4,512]{1,0:T(4,128)S(1)} %get-tuple-element.51.own_ref), channel_id=1, source_target_pairs={{0,10},{1,27},{2,24},{3,9},{4,14},{5,31},{6,28},{7,13},{8,18},{9,3... | collective-permute-start | bytes 24584 | tf_op jit(solution)/shard_map/ppermute | solution.py:455
  35.8 5.5 %collective-permute-start.6 = (f32[4,512]{1,0:T(4,128)S(1)}, f32[4,512]{1,0:T(4,128)S(1)}, u32[]{:S(2)}, u32[]{:S(2)}) collective-permute-start(f32[4,512]{1,0:T(4,128)S(1)} %get-tuple-element.51.own_ref), channel_id=1, source_target_pairs={{0,9},{1,24},{2,27},{3,10},{4,13},{5,28},{6,31},{7,14},{8,17},{9,0... | collective-permute-start | bytes 24584 | tf_op jit(solution)/shard_map/ppermute | solution.py:455
  44.8 3.7 %collective-permute-start.7 = (f32[2,256]{1,0:T(2,128)S(1)}, f32[2,256]{1,0:T(2,128)S(1)}, u32[]{:S(2)}, u32[]{:S(2)}) collective-permute-start(f32[2,256]{1,0:T(2,128)S(1)} %get-tuple-element.58), channel_id=1, source_target_pairs={{0,1},{1,0},{2,3},{3,2},{4,5},{5,4},{6,7},{7,6},{8,9},{9,8},{10,11... | collective-permute-start | bytes 6152 | tf_op jit(solution)/shard_map/ppermute | solution.py:455

commit v7 on v6

--- a/solution.py
+++ b/solution.py
@@ -317,36 +317,38 @@
     half = extent // 2
     eighth = extent // 4
     grid = grid.astype(jnp.bfloat16)
-    spreads = []
-    for turn in range(2):
-        real, imag = both_halves(frequency_rows(col_ref, turn), grid[:half], grid[half:])
-        real, imag = real.astype(jnp.bfloat16), imag.astype(jnp.bfloat16)
-        blocks = [
-            (real[:, q * eighth : (q + 1) * eighth], imag[:, q * eighth : (q + 1) * eighth])
-            for q in range(4)
-        ]
-        spreads.append(spread(blocks))
-    for turn in range(2):
-        here = slice(turn * half, (turn + 1) * half)
-        backs = []
-        for j, pair in enumerate(spreads[turn]):
-            forward = dot_nt(joined(pair), row_ref[j]).astype(jnp.bfloat16)
-            kernel_re = spec_ref[j, here, :eighth]
-            kernel_im = spec_ref[j, here, eighth:]
-            forward_re, forward_im = forward[:, :eighth], forward[:, eighth:]
-            scaled = joined(
-                (
-                    forward_re * kernel_re - forward_im * kernel_im,
-                    forward_re * kernel_im + forward_im * kernel_re,
-                )
+    halves = [
+        both_halves(frequency_rows(col_ref, turn), grid[:half], grid[half:]) for turn in range(2)
+    ]
+    real, imag = (
+        jnp.concatenate([pair[part] for pair in halves], axis=0).astype(jnp.bfloat16)
+        for part in range(2)
+    )
+    blocks = [
+        (real[:, q * eighth : (q + 1) * eighth], imag[:, q * eighth : (q + 1) * eighth])
+        for q in range(4)
+    ]
+    backs = []
+    for j, pair in enumerate(spread(blocks)):
+        forward = dot_nt(joined(pair), row_ref[j]).astype(jnp.bfloat16)
+        kernel_re = spec_ref[j, :, :eighth]
+        kernel_im = spec_ref[j, :, eighth:]
+        forward_re, forward_im = forward[:, :eighth], forward[:, eighth:]
+        scaled = joined(
+            (
+                forward_re * kernel_re - forward_im * kernel_im,
+                forward_re * kernel_im + forward_im * kernel_re,
             )
-            back = dot_nn(scaled, row_ref[j]).astype(jnp.bfloat16)
-            backs.append((back[:, :eighth], back[:, eighth:]))
-        for q, pair in enumerate(gathered(backs)):
-            lanes = slice(q * eighth, (q + 1) * eighth)
-            for part, value in enumerate(pair):
+        )
+        back = dot_nn(scaled, row_ref[j]).astype(jnp.bfloat16)
+        backs.append((back[:, :eighth], back[:, eighth:]))
+    for q, pair in enumerate(gathered(backs)):
+        lanes = slice(q * eighth, (q + 1) * eighth)
+        for part, value in enumerate(pair):
+            for turn in range(2):
                 where = slice(part * half + turn * eighth, part * half + (turn + 1) * eighth)
-                low, high = value[:eighth], value[eighth:]
+                low = value[turn * half : turn * half + eighth]
+                high = value[turn * half + eighth : (turn + 1) * half]
                 back_ref[0, where, lanes] = low + high
                 back_ref[1, where, lanes] = low - high
     even = dot_nn(inv_ref[:half, :], back_ref[0])

time: 49.2 us -> 49 us (level)
  no operation moved by 1% of the time
where the time goes in v7:
time: 49 us; the launch traced here: 48.9 us
  Pallas kernels  21.2 us (43%)
  starting transfers between devices  13.7 us (28%)
  waiting for transfers between devices  13.3 us (27%)
  other arithmetic  0.6 us (1%)
    pallas_call x4, Pallas kernels, section(): pl.pallas_call(kernel, out_shape=outs, in_specs=[VMEM] * (len(arguments)...  14.4 us
    ppermute x8, starting transfers between devices, exchange(): return lax.ppermute(value, ('cuts', 'tr'), pairs)  13.7 us
    ppermute x8, waiting for transfers between devices, exchange(): return lax.ppermute(value, ('cuts', 'tr'), pairs)  13.3 us
    pallas_call x1, Pallas kernels, per_device(): pl.pallas_call(functools.partial(setup_kernel, begins), out_shape=(jax.Sh...  4.34 us
    pallas_call x3, Pallas kernels, deposited(): pl.pallas_call(deposit_kernel, out_shape=(jax.ShapeDtypeStruct((extent, e...  2.42 us
  transfers between devices with their start and end apart: 8, of which 5 were waited for; matrix products, arithmetic and copies ran while one was open for 0% of the time, Pallas kernels for 14%

profile of v7, /device:TPU:0, one launch (start us, length us, event | category | flops | bytes accessed | tf_op | source)
XLA Modules:
  0.0 48.9 jit_solution(5816269828173672066)
XLA Ops:
  0.0 0.0 copy-start.3
  0.0 0.0 copy-start
  0.0 0.0 copy-start.1
  0.0 3.1 %collective-permute-start = (f32[2,2,256]{2,1,0:T(2,128)}, f32[2,2,256]{2,1,0:T(2,128)S(1)}, u32[]{:S(2)}, u32[]{:S(2)}) collective-permute-start(f32[2,2,256]{2,1,0:T(2,128)} %bitcast.15), channel_id=1, source_target_pairs={{0,1},{1,0},{2,3},{3,2},{4,5},{5,4},{6,7},{7,6},{8,9},{9,8},{10,11... | collective-permute-start | bytes 12296 | tf_op jit(solution)/shard_map/ppermute | solution.py:457
  3.1 4.3 %setup.1 = (bf16[512,512]{1,0:T(8,128)(2,1)S(1)}, bf16[512,512]{1,0:T(8,128)(2,1)S(1)}, bf16[8,256,256]{2,1,0:T(8,128)(2,1)S(1)}, bf16[8,512,256]{2,1,0:T(8,128)...) custom-call(f32[1024,1024]{1,0:T(8,128)} %green_ref.1, ...), custom_call_target="tpu_custom_call" | custom-call | flops 2147483648 | bytes 8388608 | tf_op jit(solution)/shard_map/setup/pallas_call | solution.py:464
  7.5 0.0 collective-permute-done.other_ref
  7.5 0.0 copy-done.3
  7.5 0.0 copy-done
  7.5 0.0 copy-done.1
  7.5 0.0 copy-done.2
  7.5 3.7 %first.1 = (f32[4,512]{1,0:T(4,128)S(1)}, f32[2,512]{1,0:T(2,128)S(1)}) custom-call(s32[2,2,1024]{2,1,0:T(2,128)S(1)} %bitcast.12, f32[2,2,1024]{2,1,0:T(2,128)S(1)} %bitcast.14, f32[2,1,1024]{2,1,0:T(1,128)S(1)} %copy-done.2, f32[2,2,256]{2,1,0:T(2,128)S(1)} %bitcast.16, f32[2,2,256]{2,1,0:T(2,128)S(1)} %collective-permute-done.other_ref, ...), custom_call_target="tpu_custom_call" | custom-call | flops 3221225472 | bytes 8388608 | tf_op jit(solution)/shard_map/first/pallas_call | solution.py:511
  11.3 4.5 %collective-permute-start.1 = (f32[4,512]{1,0:T(4,128)S(1)}, f32[4,512]{1,0:T(4,128)S(1)}, u32[]{:S(2)}, u32[]{:S(2)}) collective-permute-start(f32[4,512]{1,0:T(4,128)S(1)} %get-tuple-element.39.own_ref.refs_2_), channel_id=1, source_target_pairs={{0,26},{1,11},{2,8},{3,25},{4,30},{5,15},{6,12},{7,29},{8,2},{9,19... | collective-permute-start | bytes 24584 | tf_op jit(solution)/shard_map/ppermute | solution.py:457
  15.8 0.4 collective-permute-start.2
  16.2 1.5 %collective-permute-done.1.guest_ref = f32[4,512]{1,0:T(4,128)S(1)} collective-permute-done((f32[4,512]{1,0:T(4,128)S(1)}, f32[4,512]{1,0:T(4,128)S(1)}, u32[]{:S(2)}, u32[]{:S(2)}) %collective-permute-start.1) | collective-permute-done | bytes 8224 | tf_op jit(solution)/shard_map/ppermute | solution.py:457
  17.7 0.8 %deposit.3 = (f32[512,512]{1,0:T(8,128)S(1)}, bf16[512,512]{1,0:T(8,128)(2,1)S(1)}, bf16[512,512]{1,0:T(8,128)(2,1)S(1)}, bf16[512,512]{1,0:T(8,128)(2,1)S(1)}) custom-call(f32[4,512]{1,0:T(4,128)S(1)} %collective-permute-done.1.guest_ref, f32[4,512]{1,0:T(4,128)S(1)} %get-tuple-element.39.own_ref.refs_2_), custom_call_target="tpu_custom_call" | custom-call | flops 268435456 | bytes 4194304 | tf_op jit(solution)/shard_map/deposit/pallas_call | solution.py:498
  18.5 2.7 %collective-permute-done.2.refs_1_ = f32[4,512]{1,0:T(4,128)S(1)} collective-permute-done((f32[4,512]{1,0:T(4,128)S(1)}, f32[4,512]{1,0:T(4,128)S(1)}, u32[]{:S(2)}, u32[]{:S(2)}) %collective-permute-start.2) | collective-permute-done | bytes 8224 | tf_op jit(solution)/shard_map/ppermute | solution.py:457
  21.3 3.5 %middle.2 = (f32[4,512]{1,0:T(4,128)S(1)}, f32[2,512]{1,0:T(2,128)S(1)}) custom-call(f32[512,512]{1,0:T(8,128)S(1)} %get-tuple-element.40.refs_0_, f32[4,512]{1,0:T(4,128)S(1)} %collective-permute-done.2.refs_1_, f32[4,512]{1,0:T(4,128)S(1)} %get-tuple-element.39.own_ref.refs_2_, f32[2,512]{1,0:T(2,128)S(1)} %get-tuple-element.41.refs_3_, ...), custom_call_target="tpu_custom_call" | custom-call | flops 3221225472 | bytes 8388608 | tf_op jit(solution)/shard_map/middle/pallas_call | solution.py:511
  24.8 0.1 collective-permute-start.3
  24.8 1.7 %collective-permute-start.4 = (f32[4,512]{1,0:T(4,128)S(1)}, f32[4,512]{1,0:T(4,128)S(1)}, u32[]{:S(2)}, u32[]{:S(2)}) collective-permute-start(f32[4,512]{1,0:T(4,128)S(1)} %get-tuple-element.45.own_ref.refs_2_), channel_id=1, source_target_pairs={{0,17},{1,16},{2,19},{3,18},{4,21},{5,20},{6,23},{7,22},{8,25},{9,... | collective-permute-start | bytes 24584 | tf_op jit(solution)/shard_map/ppermute | solution.py:457
  26.5 3.8 %collective-permute-done.3.guest_ref = f32[4,512]{1,0:T(4,128)S(1)} collective-permute-done((f32[4,512]{1,0:T(4,128)S(1)}, f32[4,512]{1,0:T(4,128)S(1)}, u32[]{:S(2)}, u32[]{:S(2)}) %collective-permute-start.3) | collective-permute-done | bytes 8224 | tf_op jit(solution)/shard_map/ppermute | solution.py:457
  30.3 0.8 %deposit.4 = (f32[512,512]{1,0:T(8,128)S(1)}, bf16[512,512]{1,0:T(8,128)(2,1)S(1)}, bf16[512,512]{1,0:T(8,128)(2,1)S(1)}, bf16[512,512]{1,0:T(8,128)(2,1)S(1)}) custom-call(f32[4,512]{1,0:T(4,128)S(1)} %collective-permute-done.3.guest_ref, f32[4,512]{1,0:T(4,128)S(1)} %get-tuple-element.45.own_ref.refs_2_), custom_call_target="tpu_custom_call" | custom-call | flops 268435456 | bytes 4194304 | tf_op jit(solution)/shard_map/deposit/pallas_call | solution.py:498
  31.1 0.0 collective-permute-done.4.refs_1_
  31.1 3.7 %middle.3 = (f32[4,512]{1,0:T(4,128)S(1)}, f32[2,512]{1,0:T(2,128)S(1)}) custom-call(f32[512,512]{1,0:T(8,128)S(1)} %get-tuple-element.46.refs_0_, f32[4,512]{1,0:T(4,128)S(1)} %collective-permute-done.4.refs_1_, f32[4,512]{1,0:T(4,128)S(1)} %get-tuple-element.45.own_ref.refs_2_, f32[2,512]{1,0:T(2,128)S(1)} %get-tuple-element.47.refs_3_, ...), custom_call_target="tpu_custom_call" | custom-call | flops 3221225472 | bytes 8388608 | tf_op jit(solution)/shard_map/middle/pallas_call | solution.py:511
  34.8 0.8 %collective-permute-start.5 = (f32[4,512]{1,0:T(4,128)S(1)}, f32[4,512]{1,0:T(4,128)S(1)}, u32[]{:S(2)}, u32[]{:S(2)}) collective-permute-start(f32[4,512]{1,0:T(4,128)S(1)} %get-tuple-element.51.own_ref), channel_id=1, source_target_pairs={{0,10},{1,27},{2,24},{3,9},{4,14},{5,31},{6,28},{7,13},{8,18},{9,3... | collective-permute-start | bytes 24584 | tf_op jit(solution)/shard_map/ppermute | solution.py:457
  35.6 1.3 %collective-permute-start.6 = (f32[4,512]{1,0:T(4,128)S(1)}, f32[4,512]{1,0:T(4,128)S(1)}, u32[]{:S(2)}, u32[]{:S(2)}) collective-permute-start(f32[4,512]{1,0:T(4,128)S(1)} %get-tuple-element.51.own_ref), channel_id=1, source_target_pairs={{0,9},{1,24},{2,27},{3,10},{4,13},{5,28},{6,31},{7,14},{8,17},{9,0... | collective-permute-start | bytes 24584 | tf_op jit(solution)/shard_map/ppermute | solution.py:457
  37.0 3.3 %collective-permute-done.5.guest_ref = f32[4,512]{1,0:T(4,128)S(1)} collective-permute-done((f32[4,512]{1,0:T(4,128)S(1)}, f32[4,512]{1,0:T(4,128)S(1)}, u32[]{:S(2)}, u32[]{:S(2)}) %collective-permute-start.5) | collective-permute-done | bytes 8224 | tf_op jit(solution)/shard_map/ppermute | solution.py:457
  40.3 0.8 %deposit.5 = (f32[512,512]{1,0:T(8,128)S(1)}, bf16[512,512]{1,0:T(8,128)(2,1)S(1)}, bf16[512,512]{1,0:T(8,128)(2,1)S(1)}, bf16[512,512]{1,0:T(8,128)(2,1)S(1)}) custom-call(f32[4,512]{1,0:T(4,128)S(1)} %collective-permute-done.5.guest_ref, f32[4,512]{1,0:T(4,128)S(1)} %get-tuple-element.51.own_ref), custom_call_target="tpu_custom_call" | custom-call | flops 268435456 | bytes 4194304 | tf_op jit(solution)/shard_map/deposit/pallas_call | solution.py:498
  41.1 0.0 collective-permute-done.6.refs_1_
  41.1 3.5 %last.1 = (f32[2,256]{1,0:T(2,128)S(1)}, f32[2,256]{1,0:T(2,128)S(1)}) custom-call(f32[512,512]{1,0:T(8,128)S(1)} %get-tuple-element.52.refs_0_, f32[4,512]{1,0:T(4,128)S(1)} %collective-permute-done.6.refs_1_, f32[2,512]{1,0:T(2,128)S(1)} %get-tuple-element.53.refs_2_, bf16[512,512]{1,0:T(8,128)(2,1)S(1)} %get-tuple-element.54.refs_3_, ...), custom_call_target="tpu_custom_call" | custom-call | flops 3221225472 | bytes 8388608 | tf_op jit(solution)/shard_map/last/pallas_call | solution.py:511
  44.6 1.8 %collective-permute-start.7 = (f32[2,256]{1,0:T(2,128)S(1)}, f32[2,256]{1,0:T(2,128)S(1)}, u32[]{:S(2)}, u32[]{:S(2)}) collective-permute-start(f32[2,256]{1,0:T(2,128)S(1)} %get-tuple-element.58), channel_id=1, source_target_pairs={{0,1},{1,0},{2,3},{3,2},{4,5},{5,4},{6,7},{7,6},{8,9},{9,8},{10,11... | collective-permute-start | bytes 6152 | tf_op jit(solution)/shard_map/ppermute | solution.py:457
  46.4 1.9 %collective-permute-done.7 = f32[2,256]{1,0:T(2,128)S(1)} collective-permute-done((f32[2,256]{1,0:T(2,128)S(1)}, f32[2,256]{1,0:T(2,128)S(1)}, u32[]{:S(2)}, u32[]{:S(2)}) %collective-permute-start.7) | collective-permute-done | bytes 2080 | tf_op jit(solution)/shard_map/ppermute | solution.py:457
  48.3 0.6 %maximum_bitcast_fusion = f32[2,1,2,256]{3,2,1,0:T(2,128)} fusion(f32[1,2,256]{2,1,0:T(2,128)S(1)} %get-tuple-element.60, f32[1,2,256]{2,1,0:T(2,128)S(1)} %get-tuple-element.59), kind=kLoop, calls=%fused_computation | loop fusion | flops 1024 | bytes 8192 | tf_op jit(solution)/shard_map/broadcast_in_dim | solution.py:546
  (2 shorter events, 0.0 us)
Async XLA Ops:
  0.0 7.5 %copy-start.3 = (f32[2,1,2,256]{3,2,1,0:T(2,128)S(1)}, f32[2,1,2,256]{3,2,1,0:T(2,128)}, u32[]{:S(2)}) copy-start(f32[2,1,2,256]{3,2,1,0:T(2,128)} %param.9) | copy-start | bytes 12292
  0.0 7.5 %copy-start = (s32[2,1,2,1024]{3,2,1,0:T(2,128)S(1)}, s32[2,1,2,1024]{3,2,1,0:T(2,128)}, u32[]{:S(2)}) copy-start(s32[2,1,2,1024]{3,2,1,0:T(2,128)} %param.6) | copy-start | bytes 49156
  0.0 7.5 %copy-start.1 = (f32[2,1,2,1024]{3,2,1,0:T(2,128)S(1)}, f32[2,1,2,1024]{3,2,1,0:T(2,128)}, u32[]{:S(2)}) copy-start(f32[2,1,2,1024]{3,2,1,0:T(2,128)} %param.7) | copy-start | bytes 49156
  0.0 7.5 %copy-start.2 = (f32[2,1,1024]{2,1,0:T(1,128)S(1)}, f32[2,1,1024]{2,1,0:T(1,128)}, u32[]{:S(2)}) copy-start(f32[2,1,1024]{2,1,0:T(1,128)} %charges_ref.1) | copy-start | bytes 24580
  0.0 7.5 %collective-permute-start = (f32[2,2,256]{2,1,0:T(2,128)}, f32[2,2,256]{2,1,0:T(2,128)S(1)}, u32[]{:S(2)}, u32[]{:S(2)}) collective-permute-start(f32[2,2,256]{2,1,0:T(2,128)} %bitcast.15), channel_id=1, source_target_pairs={{0,1},{1,0},{2,3},{3,2},{4,5},{5,4},{6,7},{7,6},{8,9},{9,8},{10,11... | collective-permute-start | bytes 12296 | tf_op jit(solution)/shard_map/ppermute | solution.py:457
  11.3 6.4 %collective-permute-start.1 = (f32[4,512]{1,0:T(4,128)S(1)}, f32[4,512]{1,0:T(4,128)S(1)}, u32[]{:S(2)}, u32[]{:S(2)}) collective-permute-start(f32[4,512]{1,0:T(4,128)S(1)} %get-tuple-element.39.own_ref.refs_2_), channel_id=1, source_target_pairs={{0,26},{1,11},{2,8},{3,25},{4,30},{5,15},{6,12},{7,29},{8,2},{9,19... | collective-permute-start | bytes 24584 | tf_op jit(solution)/shard_map/ppermute | solution.py:457
  15.8 5.4 %collective-permute-start.2 = (f32[4,512]{1,0:T(4,128)S(1)}, f32[4,512]{1,0:T(4,128)S(1)}, u32[]{:S(2)}, u32[]{:S(2)}) collective-permute-start(f32[4,512]{1,0:T(4,128)S(1)} %get-tuple-element.39.own_ref.refs_2_), channel_id=1, source_target_pairs={{0,25},{1,8},{2,11},{3,26},{4,29},{5,12},{6,15},{7,30},{8,1},{9,16... | collective-permute-start | bytes 24584 | tf_op jit(solution)/shard_map/ppermute | solution.py:457
  24.8 5.5 %collective-permute-start.3 = (f32[4,512]{1,0:T(4,128)S(1)}, f32[4,512]{1,0:T(4,128)S(1)}, u32[]{:S(2)}, u32[]{:S(2)}) collective-permute-start(f32[4,512]{1,0:T(4,128)S(1)} %get-tuple-element.45.own_ref.refs_2_), channel_id=1, source_target_pairs={{0,18},{1,19},{2,16},{3,17},{4,22},{5,23},{6,20},{7,21},{8,26},{9,... | collective-permute-start | bytes 24584 | tf_op jit(solution)/shard_map/ppermute | solution.py:457
  24.8 6.2 %collective-permute-start.4 = (f32[4,512]{1,0:T(4,128)S(1)}, f32[4,512]{1,0:T(4,128)S(1)}, u32[]{:S(2)}, u32[]{:S(2)}) collective-permute-start(f32[4,512]{1,0:T(4,128)S(1)} %get-tuple-element.45.own_ref.refs_2_), channel_id=1, source_target_pairs={{0,17},{1,16},{2,19},{3,18},{4,21},{5,20},{6,23},{7,22},{8,25},{9,... | collective-permute-start | bytes 24584 | tf_op jit(solution)/shard_map/ppermute | solution.py:457
  34.8 5.5 %collective-permute-start.5 = (f32[4,512]{1,0:T(4,128)S(1)}, f32[4,512]{1,0:T(4,128)S(1)}, u32[]{:S(2)}, u32[]{:S(2)}) collective-permute-start(f32[4,512]{1,0:T(4,128)S(1)} %get-tuple-element.51.own_ref), channel_id=1, source_target_pairs={{0,10},{1,27},{2,24},{3,9},{4,14},{5,31},{6,28},{7,13},{8,18},{9,3... | collective-permute-start | bytes 24584 | tf_op jit(solution)/shard_map/ppermute | solution.py:457
  35.6 5.5 %collective-permute-start.6 = (f32[4,512]{1,0:T(4,128)S(1)}, f32[4,512]{1,0:T(4,128)S(1)}, u32[]{:S(2)}, u32[]{:S(2)}) collective-permute-start(f32[4,512]{1,0:T(4,128)S(1)} %get-tuple-element.51.own_ref), channel_id=1, source_target_pairs={{0,9},{1,24},{2,27},{3,10},{4,13},{5,28},{6,31},{7,14},{8,17},{9,0... | collective-permute-start | bytes 24584 | tf_op jit(solution)/shard_map/ppermute | solution.py:457
  44.6 3.7 %collective-permute-start.7 = (f32[2,256]{1,0:T(2,128)S(1)}, f32[2,256]{1,0:T(2,128)S(1)}, u32[]{:S(2)}, u32[]{:S(2)}) collective-permute-start(f32[2,256]{1,0:T(2,128)S(1)} %get-tuple-element.58), channel_id=1, source_target_pairs={{0,1},{1,0},{2,3},{3,2},{4,5},{5,4},{6,7},{7,6},{8,9},{9,8},{10,11... | collective-permute-start | bytes 6152 | tf_op jit(solution)/shard_map/ppermute | solution.py:457

commit v8 on v7

--- a/solution.py
+++ b/solution.py
@@ -194,9 +194,9 @@
             row_ref[j, lower : lower + GROUP, eighth:] = cosine.astype(jnp.bfloat16)
 
     scale = 1.0 / (period * period)
-    parity = lax.broadcasted_iota(jnp.int32, (half, eighth), 0) % 2
+    parity = lax.broadcasted_iota(jnp.int32, (extent, eighth), 0) % 2
     sign = jnp.where(parity == 0, 1.0, -1.0)
-    parts = [[], []]
+    parts = []
     for b in range(4):
         copies[2 * b].wait()
         copies[2 * b + 1].wait()
@@ -204,47 +204,37 @@
             joined([green_vm[2 * b + q, pl.ds(begin, half, stride=2), :] for q in range(2)])
             for begin in (0, 1, extent, extent + 1)
         ]
-        for turn in range(2):
-            table = frequency_rows(col_ref, turn)
-            near = both_halves(table, blocks[0], blocks[1])
-            far = both_halves(table, blocks[2], blocks[3])
-            for q in range(2):
-                cut = slice(q * eighth, (q + 1) * eighth)
-                parts[turn].append(
-                    (
-                        (near[0][:, cut] - sign * far[1][:, cut]).astype(jnp.bfloat16),
-                        (near[1][:, cut] + sign * far[0][:, cut]).astype(jnp.bfloat16),
-                    )
+        near = both_halves(col_ref, blocks[0], blocks[1])
+        far = both_halves(col_ref, blocks[2], blocks[3])
+        for q in range(2):
+            cut = slice(q * eighth, (q + 1) * eighth)
+            parts.append(
+                (
+                    (near[0][:, cut] - sign * far[1][:, cut]).astype(jnp.bfloat16),
+                    (near[1][:, cut] + sign * far[0][:, cut]).astype(jnp.bfloat16),
                 )
-    for turn in range(2):
-        part = parts[turn]
-        even = four_points([added(part[q], part[q + 4]) for q in range(4)], -1)
-        odd = four_points(eighths([less(part[q], part[q + 4]) for q in range(4)], -1), -1)
-        sums = [pair for couple in zip(even, odd) for pair in couple]
-        for j in range(8):
-            spec = dot_nt(joined(sums[j]), row_ref[j]) * scale
-            spec_ref[j, turn * half : (turn + 1) * half, :] = spec.astype(jnp.bfloat16)
-
-
-def frequency_rows(col_ref, turn):
+            )
+    even = four_points([added(parts[q], parts[q + 4]) for q in range(4)], -1)
+    odd = four_points(eighths([less(parts[q], parts[q + 4]) for q in range(4)], -1), -1)
+    sums = [pair for couple in zip(even, odd) for pair in couple]
+    for j in range(8):
+        spec_ref[j] = (dot_nt(joined(sums[j]), row_ref[j]) * scale).astype(jnp.bfloat16)
+
+
+def both_halves(col_ref, even_rows, odd_rows):
     half = col_ref.shape[0] // 2
     eighth = half // 2
-    at = turn * eighth
-    return jnp.concatenate(
-        [col_ref[at : at + eighth, :], col_ref[half + at : half + at + eighth, :]], axis=0
-    )
-
-
-def both_halves(table, even_rows, odd_rows):
-    half = table.shape[1] // 2
-    eighth = half // 2
-    even = dot_nn(table[:, :half], even_rows)
-    odd = dot_nn(table[:, half:], odd_rows)
+    even = dot_nn(col_ref[:, :half], even_rows)
+    odd = dot_nn(col_ref[:, half:], odd_rows)
     plus, minus = even + odd, even - odd
-    return (
-        jnp.concatenate([plus[:eighth], minus[:eighth]], axis=0),
-        jnp.concatenate([plus[eighth:], minus[eighth:]], axis=0),
-    )
+
+    def ordered(begin):
+        pieces = []
+        for at in (begin, begin + eighth):
+            pieces += [plus[at : at + eighth], minus[at : at + eighth]]
+        return jnp.concatenate(pieces, axis=0)
+
+    return ordered(0), ordered(half)
 
 
 def codes(cells, half):
@@ -317,12 +307,8 @@
     half = extent // 2
     eighth = extent // 4
     grid = grid.astype(jnp.bfloat16)
-    halves = [
-        both_halves(frequency_rows(col_ref, turn), grid[:half], grid[half:]) for turn in range(2)
-    ]
     real, imag = (
-        jnp.concatenate([pair[part] for pair in halves], axis=0).astype(jnp.bfloat16)
-        for part in range(2)
+        part.astype(jnp.bfloat16) for part in both_halves(col_ref, grid[:half], grid[half:])
     )
     blocks = [
         (real[:, q * eighth : (q + 1) * eighth], imag[:, q * eighth : (q + 1) * eighth])

time: 49 us -> 49.2 us (level)
  no operation moved by 1% of the time
where the time goes in v8:
time: 49.2 us; the launch traced here: 49 us
  Pallas kernels  21.3 us (43%)
  starting transfers between devices  13.7 us (28%)
  waiting for transfers between devices  13.3 us (27%)
  other arithmetic  0.6 us (1%)
    pallas_call x4, Pallas kernels, section(): pl.pallas_call(kernel, out_shape=outs, in_specs=[VMEM] * (len(arguments)...  14.6 us
    ppermute x8, starting transfers between devices, exchange(): return lax.ppermute(value, ('cuts', 'tr'), pairs)  13.7 us
    ppermute x8, waiting for transfers between devices, exchange(): return lax.ppermute(value, ('cuts', 'tr'), pairs)  13.3 us
    pallas_call x1, Pallas kernels, per_device(): pl.pallas_call(functools.partial(setup_kernel, begins), out_shape=(jax.Sh...  4.36 us
    pallas_call x3, Pallas kernels, deposited(): pl.pallas_call(deposit_kernel, out_shape=(jax.ShapeDtypeStruct((extent, e...  2.42 us
  transfers between devices with their start and end apart: 8, of which 5 were waited for; matrix products, arithmetic and copies ran while one was open for 0% of the time, Pallas kernels for 14%

profile of v8, /device:TPU:0, one launch (start us, length us, event | category | flops | bytes accessed | tf_op | source)
XLA Modules:
  0.0 49.0 jit_solution(6344564684698170274)
XLA Ops:
  0.0 0.0 copy-start.3
  0.0 0.0 copy-start
  0.0 0.0 copy-start.1
  0.0 3.1 %collective-permute-start = (f32[2,2,256]{2,1,0:T(2,128)}, f32[2,2,256]{2,1,0:T(2,128)S(1)}, u32[]{:S(2)}, u32[]{:S(2)}) collective-permute-start(f32[2,2,256]{2,1,0:T(2,128)} %bitcast.15), channel_id=1, source_target_pairs={{0,1},{1,0},{2,3},{3,2},{4,5},{5,4},{6,7},{7,6},{8,9},{9,8},{10,11... | collective-permute-start | bytes 12296 | tf_op jit(solution)/shard_map/ppermute | solution.py:443
  3.1 4.4 %setup.1 = (bf16[512,512]{1,0:T(8,128)(2,1)S(1)}, bf16[512,512]{1,0:T(8,128)(2,1)S(1)}, bf16[8,256,256]{2,1,0:T(8,128)(2,1)S(1)}, bf16[8,512,256]{2,1,0:T(8,128)...) custom-call(f32[1024,1024]{1,0:T(8,128)} %green_ref.1, ...), custom_call_target="tpu_custom_call" | custom-call | flops 2147483648 | bytes 8388608 | tf_op jit(solution)/shard_map/setup/pallas_call | solution.py:450
  7.5 0.0 collective-permute-done.other_ref
  7.5 0.0 copy-done.3
  7.5 0.0 copy-done
  7.5 0.0 copy-done.1
  7.5 0.0 copy-done.2
  7.6 3.8 %first.1 = (f32[4,512]{1,0:T(4,128)S(1)}, f32[2,512]{1,0:T(2,128)S(1)}) custom-call(s32[2,2,1024]{2,1,0:T(2,128)S(1)} %bitcast.12, f32[2,2,1024]{2,1,0:T(2,128)S(1)} %bitcast.14, f32[2,1,1024]{2,1,0:T(1,128)S(1)} %copy-done.2, f32[2,2,256]{2,1,0:T(2,128)S(1)} %bitcast.16, f32[2,2,256]{2,1,0:T(2,128)S(1)} %collective-permute-done.other_ref, ...), custom_call_target="tpu_custom_call" | custom-call | flops 3221225472 | bytes 8388608 | tf_op jit(solution)/shard_map/first/pallas_call | solution.py:497
  11.3 4.5 %collective-permute-start.1 = (f32[4,512]{1,0:T(4,128)S(1)}, f32[4,512]{1,0:T(4,128)S(1)}, u32[]{:S(2)}, u32[]{:S(2)}) collective-permute-start(f32[4,512]{1,0:T(4,128)S(1)} %get-tuple-element.39.own_ref.refs_2_), channel_id=1, source_target_pairs={{0,26},{1,11},{2,8},{3,25},{4,30},{5,15},{6,12},{7,29},{8,2},{9,19... | collective-permute-start | bytes 24584 | tf_op jit(solution)/shard_map/ppermute | solution.py:443
  15.9 0.4 collective-permute-start.2
  16.2 1.6 %collective-permute-done.1.guest_ref = f32[4,512]{1,0:T(4,128)S(1)} collective-permute-done((f32[4,512]{1,0:T(4,128)S(1)}, f32[4,512]{1,0:T(4,128)S(1)}, u32[]{:S(2)}, u32[]{:S(2)}) %collective-permute-start.1) | collective-permute-done | bytes 8224 | tf_op jit(solution)/shard_map/ppermute | solution.py:443
  17.8 0.8 %deposit.3 = (f32[512,512]{1,0:T(8,128)S(1)}, bf16[512,512]{1,0:T(8,128)(2,1)S(1)}, bf16[512,512]{1,0:T(8,128)(2,1)S(1)}, bf16[512,512]{1,0:T(8,128)(2,1)S(1)}) custom-call(f32[4,512]{1,0:T(4,128)S(1)} %collective-permute-done.1.guest_ref, f32[4,512]{1,0:T(4,128)S(1)} %get-tuple-element.39.own_ref.refs_2_), custom_call_target="tpu_custom_call" | custom-call | flops 268435456 | bytes 4194304 | tf_op jit(solution)/shard_map/deposit/pallas_call | solution.py:484
  18.6 2.7 %collective-permute-done.2.refs_1_ = f32[4,512]{1,0:T(4,128)S(1)} collective-permute-done((f32[4,512]{1,0:T(4,128)S(1)}, f32[4,512]{1,0:T(4,128)S(1)}, u32[]{:S(2)}, u32[]{:S(2)}) %collective-permute-start.2) | collective-permute-done | bytes 8224 | tf_op jit(solution)/shard_map/ppermute | solution.py:443
  21.3 3.6 %middle.2 = (f32[4,512]{1,0:T(4,128)S(1)}, f32[2,512]{1,0:T(2,128)S(1)}) custom-call(f32[512,512]{1,0:T(8,128)S(1)} %get-tuple-element.40.refs_0_, f32[4,512]{1,0:T(4,128)S(1)} %collective-permute-done.2.refs_1_, f32[4,512]{1,0:T(4,128)S(1)} %get-tuple-element.39.own_ref.refs_2_, f32[2,512]{1,0:T(2,128)S(1)} %get-tuple-element.41.refs_3_, ...), custom_call_target="tpu_custom_call" | custom-call | flops 3221225472 | bytes 8388608 | tf_op jit(solution)/shard_map/middle/pallas_call | solution.py:497
  24.9 0.1 collective-permute-start.3
  24.9 1.7 %collective-permute-start.4 = (f32[4,512]{1,0:T(4,128)S(1)}, f32[4,512]{1,0:T(4,128)S(1)}, u32[]{:S(2)}, u32[]{:S(2)}) collective-permute-start(f32[4,512]{1,0:T(4,128)S(1)} %get-tuple-element.45.own_ref.refs_2_), channel_id=1, source_target_pairs={{0,17},{1,16},{2,19},{3,18},{4,21},{5,20},{6,23},{7,22},{8,25},{9,... | collective-permute-start | bytes 24584 | tf_op jit(solution)/shard_map/ppermute | solution.py:443
  26.6 3.8 %collective-permute-done.3.guest_ref = f32[4,512]{1,0:T(4,128)S(1)} collective-permute-done((f32[4,512]{1,0:T(4,128)S(1)}, f32[4,512]{1,0:T(4,128)S(1)}, u32[]{:S(2)}, u32[]{:S(2)}) %collective-permute-start.3) | collective-permute-done | bytes 8224 | tf_op jit(solution)/shard_map/ppermute | solution.py:443
  30.4 0.8 %deposit.4 = (f32[512,512]{1,0:T(8,128)S(1)}, bf16[512,512]{1,0:T(8,128)(2,1)S(1)}, bf16[512,512]{1,0:T(8,128)(2,1)S(1)}, bf16[512,512]{1,0:T(8,128)(2,1)S(1)}) custom-call(f32[4,512]{1,0:T(4,128)S(1)} %collective-permute-done.3.guest_ref, f32[4,512]{1,0:T(4,128)S(1)} %get-tuple-element.45.own_ref.refs_2_), custom_call_target="tpu_custom_call" | custom-call | flops 268435456 | bytes 4194304 | tf_op jit(solution)/shard_map/deposit/pallas_call | solution.py:484
  31.2 0.0 collective-permute-done.4.refs_1_
  31.2 3.7 %middle.3 = (f32[4,512]{1,0:T(4,128)S(1)}, f32[2,512]{1,0:T(2,128)S(1)}) custom-call(f32[512,512]{1,0:T(8,128)S(1)} %get-tuple-element.46.refs_0_, f32[4,512]{1,0:T(4,128)S(1)} %collective-permute-done.4.refs_1_, f32[4,512]{1,0:T(4,128)S(1)} %get-tuple-element.45.own_ref.refs_2_, f32[2,512]{1,0:T(2,128)S(1)} %get-tuple-element.47.refs_3_, ...), custom_call_target="tpu_custom_call" | custom-call | flops 3221225472 | bytes 8388608 | tf_op jit(solution)/shard_map/middle/pallas_call | solution.py:497
  34.9 0.8 %collective-permute-start.5 = (f32[4,512]{1,0:T(4,128)S(1)}, f32[4,512]{1,0:T(4,128)S(1)}, u32[]{:S(2)}, u32[]{:S(2)}) collective-permute-start(f32[4,512]{1,0:T(4,128)S(1)} %get-tuple-element.51.own_ref), channel_id=1, source_target_pairs={{0,10},{1,27},{2,24},{3,9},{4,14},{5,31},{6,28},{7,13},{8,18},{9,3... | collective-permute-start | bytes 24584 | tf_op jit(solution)/shard_map/ppermute | solution.py:443
  35.8 1.3 %collective-permute-start.6 = (f32[4,512]{1,0:T(4,128)S(1)}, f32[4,512]{1,0:T(4,128)S(1)}, u32[]{:S(2)}, u32[]{:S(2)}) collective-permute-start(f32[4,512]{1,0:T(4,128)S(1)} %get-tuple-element.51.own_ref), channel_id=1, source_target_pairs={{0,9},{1,24},{2,27},{3,10},{4,13},{5,28},{6,31},{7,14},{8,17},{9,0... | collective-permute-start | bytes 24584 | tf_op jit(solution)/shard_map/ppermute | solution.py:443
  37.1 3.3 %collective-permute-done.5.guest_ref = f32[4,512]{1,0:T(4,128)S(1)} collective-permute-done((f32[4,512]{1,0:T(4,128)S(1)}, f32[4,512]{1,0:T(4,128)S(1)}, u32[]{:S(2)}, u32[]{:S(2)}) %collective-permute-start.5) | collective-permute-done | bytes 8224 | tf_op jit(solution)/shard_map/ppermute | solution.py:443
  40.4 0.8 %deposit.5 = (f32[512,512]{1,0:T(8,128)S(1)}, bf16[512,512]{1,0:T(8,128)(2,1)S(1)}, bf16[512,512]{1,0:T(8,128)(2,1)S(1)}, bf16[512,512]{1,0:T(8,128)(2,1)S(1)}) custom-call(f32[4,512]{1,0:T(4,128)S(1)} %collective-permute-done.5.guest_ref, f32[4,512]{1,0:T(4,128)S(1)} %get-tuple-element.51.own_ref), custom_call_target="tpu_custom_call" | custom-call | flops 268435456 | bytes 4194304 | tf_op jit(solution)/shard_map/deposit/pallas_call | solution.py:484
  41.3 0.0 collective-permute-done.6.refs_1_
  41.3 3.5 %last.1 = (f32[2,256]{1,0:T(2,128)S(1)}, f32[2,256]{1,0:T(2,128)S(1)}) custom-call(f32[512,512]{1,0:T(8,128)S(1)} %get-tuple-element.52.refs_0_, f32[4,512]{1,0:T(4,128)S(1)} %collective-permute-done.6.refs_1_, f32[2,512]{1,0:T(2,128)S(1)} %get-tuple-element.53.refs_2_, bf16[512,512]{1,0:T(8,128)(2,1)S(1)} %get-tuple-element.54.refs_3_, ...), custom_call_target="tpu_custom_call" | custom-call | flops 3221225472 | bytes 8388608 | tf_op jit(solution)/shard_map/last/pallas_call | solution.py:497
  44.8 1.8 %collective-permute-start.7 = (f32[2,256]{1,0:T(2,128)S(1)}, f32[2,256]{1,0:T(2,128)S(1)}, u32[]{:S(2)}, u32[]{:S(2)}) collective-permute-start(f32[2,256]{1,0:T(2,128)S(1)} %get-tuple-element.58), channel_id=1, source_target_pairs={{0,1},{1,0},{2,3},{3,2},{4,5},{5,4},{6,7},{7,6},{8,9},{9,8},{10,11... | collective-permute-start | bytes 6152 | tf_op jit(solution)/shard_map/ppermute | solution.py:443
  46.6 1.9 %collective-permute-done.7 = f32[2,256]{1,0:T(2,128)S(1)} collective-permute-done((f32[2,256]{1,0:T(2,128)S(1)}, f32[2,256]{1,0:T(2,128)S(1)}, u32[]{:S(2)}, u32[]{:S(2)}) %collective-permute-start.7) | collective-permute-done | bytes 2080 | tf_op jit(solution)/shard_map/ppermute | solution.py:443
  48.4 0.6 %maximum_bitcast_fusion = f32[2,1,2,256]{3,2,1,0:T(2,128)} fusion(f32[1,2,256]{2,1,0:T(2,128)S(1)} %get-tuple-element.60, f32[1,2,256]{2,1,0:T(2,128)S(1)} %get-tuple-element.59), kind=kLoop, calls=%fused_computation | loop fusion | flops 1024 | bytes 8192 | tf_op jit(solution)/shard_map/broadcast_in_dim | solution.py:532
  (2 shorter events, 0.0 us)
Async XLA Ops:
  0.0 7.5 %copy-start.3 = (f32[2,1,2,256]{3,2,1,0:T(2,128)S(1)}, f32[2,1,2,256]{3,2,1,0:T(2,128)}, u32[]{:S(2)}) copy-start(f32[2,1,2,256]{3,2,1,0:T(2,128)} %param.9) | copy-start | bytes 12292
  0.0 7.5 %copy-start = (s32[2,1,2,1024]{3,2,1,0:T(2,128)S(1)}, s32[2,1,2,1024]{3,2,1,0:T(2,128)}, u32[]{:S(2)}) copy-start(s32[2,1,2,1024]{3,2,1,0:T(2,128)} %param.6) | copy-start | bytes 49156
  0.0 7.5 %copy-start.1 = (f32[2,1,2,1024]{3,2,1,0:T(2,128)S(1)}, f32[2,1,2,1024]{3,2,1,0:T(2,128)}, u32[]{:S(2)}) copy-start(f32[2,1,2,1024]{3,2,1,0:T(2,128)} %param.7) | copy-start | bytes 49156
  0.0 7.5 %copy-start.2 = (f32[2,1,1024]{2,1,0:T(1,128)S(1)}, f32[2,1,1024]{2,1,0:T(1,128)}, u32[]{:S(2)}) copy-start(f32[2,1,1024]{2,1,0:T(1,128)} %charges_ref.1) | copy-start | bytes 24580
  0.0 7.5 %collective-permute-start = (f32[2,2,256]{2,1,0:T(2,128)}, f32[2,2,256]{2,1,0:T(2,128)S(1)}, u32[]{:S(2)}, u32[]{:S(2)}) collective-permute-start(f32[2,2,256]{2,1,0:T(2,128)} %bitcast.15), channel_id=1, source_target_pairs={{0,1},{1,0},{2,3},{3,2},{4,5},{5,4},{6,7},{7,6},{8,9},{9,8},{10,11... | collective-permute-start | bytes 12296 | tf_op jit(solution)/shard_map/ppermute | solution.py:443
  11.3 6.4 %collective-permute-start.1 = (f32[4,512]{1,0:T(4,128)S(1)}, f32[4,512]{1,0:T(4,128)S(1)}, u32[]{:S(2)}, u32[]{:S(2)}) collective-permute-start(f32[4,512]{1,0:T(4,128)S(1)} %get-tuple-element.39.own_ref.refs_2_), channel_id=1, source_target_pairs={{0,26},{1,11},{2,8},{3,25},{4,30},{5,15},{6,12},{7,29},{8,2},{9,19... | collective-permute-start | bytes 24584 | tf_op jit(solution)/shard_map/ppermute | solution.py:443
  15.9 5.4 %collective-permute-start.2 = (f32[4,512]{1,0:T(4,128)S(1)}, f32[4,512]{1,0:T(4,128)S(1)}, u32[]{:S(2)}, u32[]{:S(2)}) collective-permute-start(f32[4,512]{1,0:T(4,128)S(1)} %get-tuple-element.39.own_ref.refs_2_), channel_id=1, source_target_pairs={{0,25},{1,8},{2,11},{3,26},{4,29},{5,12},{6,15},{7,30},{8,1},{9,16... | collective-permute-start | bytes 24584 | tf_op jit(solution)/shard_map/ppermute | solution.py:443
  24.9 5.5 %collective-permute-start.3 = (f32[4,512]{1,0:T(4,128)S(1)}, f32[4,512]{1,0:T(4,128)S(1)}, u32[]{:S(2)}, u32[]{:S(2)}) collective-permute-start(f32[4,512]{1,0:T(4,128)S(1)} %get-tuple-element.45.own_ref.refs_2_), channel_id=1, source_target_pairs={{0,18},{1,19},{2,16},{3,17},{4,22},{5,23},{6,20},{7,21},{8,26},{9,... | collective-permute-start | bytes 24584 | tf_op jit(solution)/shard_map/ppermute | solution.py:443
  24.9 6.2 %collective-permute-start.4 = (f32[4,512]{1,0:T(4,128)S(1)}, f32[4,512]{1,0:T(4,128)S(1)}, u32[]{:S(2)}, u32[]{:S(2)}) collective-permute-start(f32[4,512]{1,0:T(4,128)S(1)} %get-tuple-element.45.own_ref.refs_2_), channel_id=1, source_target_pairs={{0,17},{1,16},{2,19},{3,18},{4,21},{5,20},{6,23},{7,22},{8,25},{9,... | collective-permute-start | bytes 24584 | tf_op jit(solution)/shard_map/ppermute | solution.py:443
  34.9 5.5 %collective-permute-start.5 = (f32[4,512]{1,0:T(4,128)S(1)}, f32[4,512]{1,0:T(4,128)S(1)}, u32[]{:S(2)}, u32[]{:S(2)}) collective-permute-start(f32[4,512]{1,0:T(4,128)S(1)} %get-tuple-element.51.own_ref), channel_id=1, source_target_pairs={{0,10},{1,27},{2,24},{3,9},{4,14},{5,31},{6,28},{7,13},{8,18},{9,3... | collective-permute-start | bytes 24584 | tf_op jit(solution)/shard_map/ppermute | solution.py:443
  35.8 5.5 %collective-permute-start.6 = (f32[4,512]{1,0:T(4,128)S(1)}, f32[4,512]{1,0:T(4,128)S(1)}, u32[]{:S(2)}, u32[]{:S(2)}) collective-permute-start(f32[4,512]{1,0:T(4,128)S(1)} %get-tuple-element.51.own_ref), channel_id=1, source_target_pairs={{0,9},{1,24},{2,27},{3,10},{4,13},{5,28},{6,31},{7,14},{8,17},{9,0... | collective-permute-start | bytes 24584 | tf_op jit(solution)/shard_map/ppermute | solution.py:443
  44.8 3.7 %collective-permute-start.7 = (f32[2,256]{1,0:T(2,128)S(1)}, f32[2,256]{1,0:T(2,128)S(1)}, u32[]{:S(2)}, u32[]{:S(2)}) collective-permute-start(f32[2,256]{1,0:T(2,128)S(1)} %get-tuple-element.58), channel_id=1, source_target_pairs={{0,1},{1,0},{2,3},{3,2},{4,5},{5,4},{6,7},{7,6},{8,9},{9,8},{10,11... | collective-permute-start | bytes 6152 | tf_op jit(solution)/shard_map/ppermute | solution.py:443
